TPU v7x, 32 devices: a whole 2x2x4 slice. The times are simulated.
32 devices in a mesh: fsdp: 16 (over z, y, x), dp: 2 (over core).
Axes of the slice: x: 2, y: 2, z: 4, core: 2. Of those that a mesh axis runs over, the one named last changes fastest.
Arguments:
- gradients: bfloat16 [2, 64, 256, 256], P('dp', 'fsdp'), may hold values from -6 to 6
- first_moment: float32 [96, 256, 256], P('fsdp'), may hold values from -4 to 4
- second_moment: float32 [96, 256, 256], P('fsdp'), may hold values from 0.05 to 2
- left_basis: float32 [96, 256, 256], P('fsdp'), may hold values from -1 to 1, as said below
- right_basis: float32 [96, 256, 256], P('fsdp'), may hold values from -1 to 1, as said below
- shard_starts: int32 [16], replicated, may hold values from 0 to 48, as said below
- block_owners: int32 [48], replicated, may hold values from 0 to 15, as said below
Outputs:
- direction: float32 [64, 256, 256], P('fsdp')
- first_new: float32 [96, 256, 256], P('fsdp')
- second_new: float32 [96, 256, 256], P('fsdp')
Inputs may be any that keep to these rules, and one draw needn't show every extreme that they name: Starts never fall and shard_starts[0] = 0; a device holds at most 4 blocks, some device exactly 4 and some none. `block_owners`: never falls; a device owns at most 6 blocks, some device exactly 6 and some none; a block's owner differs from its holder by at most 2 fsdp indices, by exactly 2 for some block in each direction. `left_basis`: each matrix is orthogonal up to float32 rounding. `right_basis`: each matrix is orthogonal up to float32 rounding.
All inputs are finite; a program needn't handle non-finite values.
Results may differ from a plain program's by a relative error of at most 0.0014.
Values may be sent and summed in bfloat16 or wider, within the bound.
No kernel may reach another device: no remote copies, remote signals or barrier semaphores. Data moves between devices by JAX's collectives and lax.ppermute only.
A program may use at most 64 MiB of HBM per device.

v0:
```python
import jax
import jax.numpy as jnp
from jax import lax
from jax.sharding import PartitionSpec as P

REACH = 2
STEP = 10


beta_one = 0.9
beta_two = 0.95
epsilon = 1e-08


def from_behind(value, axis, steps):
    count = lax.axis_size(axis)
    initial, last = (max(0, -steps), min(count, count - steps))
    return lax.ppermute(value, axis, [(source, source + steps) for source in range(initial, last)])


def soap_blocks(gradient, moment_one, moment_two, left_basis, right_basis):
    highest = lax.Precision.HIGHEST
    moment_new = beta_one * moment_one + (1.0 - beta_one) * gradient
    turned = jnp.einsum(
        "jad,jde->jae",
        jnp.einsum("jba,jbd->jad", left_basis, gradient, precision=highest),
        right_basis,
        precision=highest,
    )
    turned_moment = jnp.einsum(
        "jad,jde->jae",
        jnp.einsum("jba,jbd->jad", left_basis, moment_new, precision=highest),
        right_basis,
        precision=highest,
    )
    second_next = beta_two * moment_two + (1.0 - beta_two) * turned * turned
    bias_one = 1.0 - beta_one**STEP
    bias_two = 1.0 - beta_two**STEP
    scaled = turned_moment / bias_one / (jnp.sqrt(second_next / bias_two) + epsilon)
    update = jnp.einsum(
        "jad,jed->jae",
        jnp.einsum("jab,jbd->jad", left_basis, scaled, precision=highest),
        right_basis,
        precision=highest,
    )
    return (moment_new, second_next, update)


def layout(shard_starts, block_owners, devices):
    total_blocks = block_owners.shape[0]
    ends = jnp.concatenate([shard_starts[1:], jnp.full((1,), total_blocks, jnp.int32)])
    held_counts = ends - shard_starts
    device_ids = jnp.arange(devices, dtype=jnp.int32)
    own_counts = jnp.sum((block_owners[None, :] == device_ids[:, None]).astype(jnp.int32), axis=1)
    firsts = jnp.cumsum(own_counts) - own_counts
    return (held_counts, own_counts, firsts)


def linking(own_first, own_count, hold_start, hold_count, in_range, slot_count, owned_slots):
    owner_pos = own_first + jnp.arange(owned_slots, dtype=jnp.int32)
    holder_pos = hold_start + jnp.arange(slot_count, dtype=jnp.int32)
    live_pair = (
        (jnp.arange(owned_slots)[:, None] < own_count)
        & (jnp.arange(slot_count)[None, :] < hold_count)
        & in_range
    )
    return (owner_pos[:, None] == holder_pos[None, :]) & live_pair


def body(
    gradients, first_moment, second_moment, left_basis, right_basis, shard_starts, block_owners
):
    devices = lax.axis_size("fsdp")
    myself = lax.axis_index("fsdp")
    slot_count = gradients.shape[1]
    owned_slots = first_moment.shape[0]
    block_width = gradients.shape[3]
    held_counts, own_counts, firsts = layout(shard_starts, block_owners, devices)
    summed = lax.psum_scatter(
        gradients[0].astype(jnp.float32).astype(jnp.bfloat16), "dp", scatter_dimension=1, tiled=True
    )
    assembled = jnp.zeros((owned_slots, summed.shape[1], block_width), jnp.float32)
    for offset in range(-REACH, REACH + 1):
        source = myself - offset
        if offset == 0:
            arriving = summed
        else:
            arriving = from_behind(summed, "fsdp", offset)
        in_range = (source >= 0) & (source < devices)
        picked = jnp.clip(source, 0, devices - 1)
        matching = linking(
            firsts[myself],
            own_counts[myself],
            shard_starts[picked],
            held_counts[picked],
            in_range,
            slot_count,
            owned_slots,
        )
        assembled = assembled + jnp.einsum(
            "js,sab->jab",
            matching.astype(jnp.bfloat16),
            arriving,
            preferred_element_type=jnp.float32,
        )
    gradient = lax.all_gather(assembled.astype(jnp.bfloat16), "dp", axis=1, tiled=True).astype(
        jnp.float32
    )
    own_live = own_counts[myself]
    moment_new, second_next, update = soap_blocks(
        gradient, first_moment, second_moment, left_basis, right_basis
    )
    live_slots = (jnp.arange(owned_slots) < own_live)[:, None, None]
    moment_new = jnp.where(live_slots, moment_new, 0.0)
    second_next = jnp.where(live_slots, second_next, 0.0)
    update = jnp.where(live_slots, update, 0.0)
    half_rows = block_width // lax.axis_size("dp")
    sending = lax.dynamic_slice_in_dim(update, lax.axis_index("dp") * half_rows, half_rows, 1)
    collected = jnp.zeros((slot_count, sending.shape[1], block_width), jnp.float32)
    for offset in range(-REACH, REACH + 1):
        source = myself + offset
        if offset == 0:
            arriving = sending
        else:
            arriving = from_behind(sending, "fsdp", -offset)
        in_range = (source >= 0) & (source < devices)
        picked = jnp.clip(source, 0, devices - 1)
        matching = linking(
            firsts[picked],
            own_counts[picked],
            shard_starts[myself],
            held_counts[myself],
            in_range,
            slot_count,
            owned_slots,
        )
        collected = collected + jnp.einsum(
            "js,jab->sab", matching.astype(jnp.float32), arriving, precision=lax.Precision.HIGHEST
        )
    direction = lax.all_gather(collected, "dp", axis=1, tiled=True)
    return (direction, moment_new, second_next)


def solution(mesh):
    in_specs = (
        P("dp", "fsdp", None, None),
        P("fsdp", None, None),
        P("fsdp", None, None),
        P("fsdp", None, None),
        P("fsdp", None, None),
        P(),
        P(),
    )
    out_specs = (P("fsdp", None, None), P("fsdp", None, None), P("fsdp", None, None))
    return jax.shard_map(body, mesh=mesh, in_specs=in_specs, out_specs=out_specs, check_vma=False)
```

profile of v0, /device:TPU:0, one launch (start us, length us, event | category | flops | bytes accessed | tf_op | source)
XLA Modules:
  0.0 160.9 jit_solution(13953221525241802722)
XLA Ops:
  7.3 2.3 %copy.77 = bf16[1,4,256,256]{3,1,2,0:T(4,128)(2,1)} copy(bf16[1,4,256,256]{3,2,1,0:T(8,128)(2,1)} %param.7) | data formatting | bytes 1048576 | tf_op args[0]
  10.1 0.7 fusion.138
  12.2 0.7 fusion.140
  24.4 7.9 %all-reduce.3.cloned.1.call-done = bf16[4,256,256]{2,0,1:T(4,128)(2,1)} async-done(((bf16[4,256,256]{2,0,1:T(4,128)(2,1)}), bf16[4,256,256]{2,0,1:T(4,128)(2,1)}) %all-reduce.3.cloned.1.call-update) | async-done | bytes 524304
  32.3 1.0 constant_dynamic-slice_fusion
  33.3 1.3 collective-permute-start.1
  35.3 1.3 collective-permute-start
  36.6 6.4 %collective-permute-start.3 = (bf16[4,128,256]{2,0,1:T(4,128)(2,1)S(1)}, bf16[4,128,256]{2,0,1:T(4,128)(2,1)S(1)}, u32[]{:S(2)}, u32[]{:S(2)}) collective-permute-start(bf16[4,128,256]{2,0,1:T(4,128)(2,1)S(1)} %constant_dynamic-slice_fusion), channel_id=1, source_target_pairs={{0,4},{2,6},{4,8},{6,10},{8,12},{10,14},{12,16},{14,18},{16,20},{1... | collective-permute-start | bytes 786440 | tf_op jit(solution)/shard_map/ppermute | solution.py:18
  43.0 2.7 %collective-permute-start.2 = (bf16[4,128,256]{2,0,1:T(4,128)(2,1)S(1)}, bf16[4,128,256]{2,0,1:T(4,128)(2,1)S(1)}, u32[]{:S(2)}, u32[]{:S(2)}) collective-permute-start(bf16[4,128,256]{2,0,1:T(4,128)(2,1)S(1)} %constant_dynamic-slice_fusion), channel_id=1, source_target_pairs={{0,2},{2,4},{4,6},{6,8},{8,10},{10,12},{12,14},{14,16},{16,18},{18... | collective-permute-start | bytes 786440 | tf_op jit(solution)/shard_map/ppermute | solution.py:18
  46.6 0.9 collective-permute-done
  47.9 12.0 %collective-permute-done.3 = bf16[4,128,256]{2,0,1:T(4,128)(2,1)S(1)} collective-permute-done((bf16[4,128,256]{2,0,1:T(4,128)(2,1)S(1)}, bf16[4,128,256]{2,0,1:T(4,128)(2,1)S(1)}, u32[]{:S(2)}, u32[]{:S(2)}) %collective-permute-start.3) | collective-permute-done | bytes 262176 | tf_op jit(solution)/shard_map/ppermute | solution.py:18
  60.9 2.7 %all_gather.6 = bf16[6,256,256]{2,1,0:T(8,128)(2,1)S(1)} all-gather(bf16[6,128,256]{2,1,0:T(8,128)(2,1)S(1)} %copy.47), channel_id=1, replica_groups=mesh['fsdp'=16,'dp'=2] {'dp'}, dimensions={1}, use_global_device_ids=true | all-gather | bytes 1179648 | tf_op jit(solution)/shard_map/all_gather | solution.py:106
  63.6 1.4 fusion.143
  65.0 2.8 %fusion.21 = f32[6,256,256]{1,2,0:T(8,128)S(1)} fusion(f32[6,256,256]{2,1,0:T(8,128)S(1)} %copy-done.1, bf16[6,256,256]{2,1,0:T(8,128)(2,1)S(1)} %all_gather.6, f32[6,256,256]{2,1,0:T(8,128)S(1)} %copy-done.2), kind=kOutput, calls=%fused_computation.27 | convolution fusion | flops 1209532416 | bytes 5505024 | tf_op jit(solution)/shard_map/jba,jbd->jad/dot_general | solution.py:32
  67.8 1.6 %fusion.142 = f32[6,256,256]{2,1,0:T(8,128)S(1)} fusion(f32[6,256,256]{1,2,0:T(8,128)S(1)} %fusion.21, f32[6,256,256]{2,1,0:T(8,128)S(1)} %copy-done), kind=kOutput, calls=%fused_computation.178 | convolution fusion | flops 1207959552 | bytes 4718592 | tf_op jit(solution)/shard_map/jad,jde->jae/dot_general | solution.py:30
  69.5 3.5 %broadcast_select_fusion = (f32[6,256,256]{2,1,0:T(8,128)}, f32[6,256,256]{2,1,0:T(8,128)}, f32[6,256,256]{2,1,0:T(8,128)S(1)}) fusion(pred[6]{0:T(512)(128)(4,1)S(1)} %iota_compare_fusion.10, f32[6,256,256]{2,1,0:T(8,128)S(1)} %copy-done.3, bf16[6,256,256]{2,1,0:T(8,128)(2,1)S(1)} %all_gather.6, f32[6,256,256]{2,1,0:T(8,128)S(1)} %copy-done.2, ...), kind=kOutput, calls=%fused_computation.29 | convolution fusion | flops 1211891712 | bytes 11796486 | tf_op jit(solution)/shard_map/jad,jde->jae/dot_general | solution.py:24
  73.0 2.7 %fusion.1 = f32[6,256,256]{1,2,0:T(8,128)S(1)} fusion(f32[6,256,256]{2,1,0:T(8,128)S(1)} %copy-done.1, f32[6,256,256]{2,1,0:T(8,128)S(1)} %fusion.142, f32[6,256,256]{2,1,0:T(8,128)S(1)} %get-tuple-element.41, f32[6,256,256]{2,1,0:T(8,128)S(1)} %copy-done.3), kind=kOutput, calls=%fused_computation.2 | convolution fusion | flops 1211105280 | bytes 7864320 | tf_op jit(solution)/shard_map/jab,jbd->jad/dot_general | solution.py:42
  75.7 1.9 %fusion.144 = f32[6,256,256]{2,1,0:T(8,128)S(1)} fusion(f32[6,256,256]{1,2,0:T(8,128)S(1)} %fusion.1, f32[6,256,256]{2,1,0:T(8,128)S(1)} %copy-done), kind=kOutput, calls=%fused_computation.180 | convolution fusion | flops 1207959552 | bytes 4718592 | tf_op jit(solution)/shard_map/jad,jed->jae/dot_general | solution.py:40
  77.8 1.3 collective-permute-start.5
  80.2 1.3 collective-permute-start.7
  83.5 5.6 %collective-permute-start.4 = (f32[6,128,256]{2,1,0:T(8,128)S(1)}, f32[6,128,256]{2,1,0:T(8,128)S(1)}, u32[]{:S(2)}, u32[]{:S(2)}) collective-permute-start(f32[6,128,256]{2,1,0:T(8,128)S(1)} %dynamic-slice_select_fusion), channel_id=1, source_target_pairs={{0,4},{2,6},{4,8},{6,10},{8,12},{10,14},{12,16},{14,18},{16,20},{1... | collective-permute-start | bytes 2359304 | tf_op jit(solution)/shard_map/ppermute | solution.py:18
  89.1 1.3 collective-permute-start.6
  90.4 1.0 fusion.15
  91.5 4.9 %collective-permute-done.5 = f32[6,128,256]{2,1,0:T(8,128)S(1)} collective-permute-done((f32[6,128,256]{2,1,0:T(8,128)S(1)}, f32[6,128,256]{2,1,0:T(8,128)S(1)}, u32[]{:S(2)}, u32[]{:S(2)}) %collective-permute-start.5) | collective-permute-done | bytes 786464 | tf_op jit(solution)/shard_map/ppermute | solution.py:18
  96.4 1.0 fusion.17
  97.5 5.6 %collective-permute-done.7 = f32[6,128,256]{2,1,0:T(8,128)S(1)} collective-permute-done((f32[6,128,256]{2,1,0:T(8,128)S(1)}, f32[6,128,256]{2,1,0:T(8,128)S(1)}, u32[]{:S(2)}, u32[]{:S(2)}) %collective-permute-start.7) | collective-permute-done | bytes 786464 | tf_op jit(solution)/shard_map/ppermute | solution.py:18
  103.0 1.0 fusion.12
  104.1 29.8 %collective-permute-done.4 = f32[6,128,256]{2,1,0:T(8,128)S(1)} collective-permute-done((f32[6,128,256]{2,1,0:T(8,128)S(1)}, f32[6,128,256]{2,1,0:T(8,128)S(1)}, u32[]{:S(2)}, u32[]{:S(2)}) %collective-permute-start.4) | collective-permute-done | bytes 786464 | tf_op jit(solution)/shard_map/ppermute | solution.py:18
  133.9 1.1 fusion.10
  135.0 1.9 %fusion.11 = f32[4,128,256]{2,0,1:T(4,128)} fusion(f32[4,128,256]{2,0,1:T(4,128)S(1)} %fusion.12, f32[4,128,256]{2,0,1:T(4,128)S(1)} %fusion.10, f32[6,128,256]{2,1,0:T(8,128)S(1)} %collective-permute-done.6, s32[6]{0:T(128)S(1)} %iota_add_fusion.1, pred[6]{0:T(512)(128)(4,1)S(1)} %iota_compare_fusion.2, pred[]{:T(512)S(6)} %and.232, ...), kind=kOutput, calls=%fused_computation.17 | convolution fusion | flops 9699424 | bytes 2359347 | tf_op jit(solution)/shard_map/js,jab->sab/dot_general | solution.py:137
  136.9 14.8 %all-gather.2.cloned.1.call-done = f32[4,256,256]{2,0,1:T(4,128)} async-done(((f32[4,128,256]{2,0,1:T(4,128)}), f32[4,256,256]{2,0,1:T(4,128)}) %all-gather.2.cloned.1.call-update) | async-done | bytes 1048592 | tf_op jit(solution)/shard_map/all_gather | solution.py:140
  151.7 2.4 %copy.59 = f32[4,256,256]{2,1,0:T(8,128)} copy(f32[4,256,256]{2,0,1:T(4,128)} %all-gather.2.cloned.1.call-done) | data formatting | bytes 2097152
  (60 shorter events, 18.6 us)
Async XLA Ops:
  7.2 60.6 %copy-start = (f32[6,256,256]{2,1,0:T(8,128)S(1)}, f32[6,256,256]{2,1,0:T(8,128)}, u32[]{:S(2)}) copy-start(f32[6,256,256]{2,1,0:T(8,128)} %param.11) | copy-start | bytes 4718596
  7.2 12.8 %copy-start.6 = (u32[32]{0:T(128)S(1)}, u32[32]{0:T(128)}, u32[]{:S(2)}) copy-start(u32[32]{0:T(128)} %constant.69) | copy-start | bytes 388
  7.2 2.5 %copy-start.5 = (s32[48]{0:T(128)S(1)}, s32[48]{0:T(128)}, u32[]{:S(2)}) copy-start(s32[48]{0:T(128)} %param.13) | copy-start | bytes 580
  7.2 4.8 %copy-start.4 = (s32[16]{0:T(128)S(1)}, s32[16]{0:T(128)}, u32[]{:S(2)}) copy-start(s32[16]{0:T(128)} %param.12) | copy-start | bytes 196
  7.2 25.1 %all-reduce.3.cloned.1.call-start = ((), (), s32[]{:S(2)}) async-start(), calls=%async_computation.1 | async-start | bytes 1048576
  9.6 142.1 %all-gather.2.cloned.1.call-start = ((), (), s32[]{:S(2)}) async-start(), calls=%async_computation | async-start | bytes 1572864 | tf_op jit(solution)/shard_map/all_gather | solution.py:140
  33.3 12.8 %collective-permute-start.1 = (bf16[4,128,256]{2,0,1:T(4,128)(2,1)S(1)}, bf16[4,128,256]{2,0,1:T(4,128)(2,1)S(1)}, u32[]{:S(2)}, u32[]{:S(2)}) collective-permute-start(bf16[4,128,256]{2,0,1:T(4,128)(2,1)S(1)} %constant_dynamic-slice_fusion), channel_id=1, source_target_pairs={{2,0},{4,2},{6,4},{8,6},{10,8},{12,10},{14,12},{16,14},{18,16},{20... | collective-permute-start | bytes 786440 | tf_op jit(solution)/shard_map/ppermute | solution.py:18
  35.3 12.2 %collective-permute-start = (bf16[4,128,256]{2,0,1:T(4,128)(2,1)S(1)}, bf16[4,128,256]{2,0,1:T(4,128)(2,1)S(1)}, u32[]{:S(2)}, u32[]{:S(2)}) collective-permute-start(bf16[4,128,256]{2,0,1:T(4,128)(2,1)S(1)} %constant_dynamic-slice_fusion), channel_id=1, source_target_pairs={{4,0},{6,2},{8,4},{10,6},{12,8},{14,10},{16,12},{18,14},{20,16},{2... | collective-permute-start | bytes 786440 | tf_op jit(solution)/shard_map/ppermute | solution.py:18
  36.6 23.3 %collective-permute-start.3 = (bf16[4,128,256]{2,0,1:T(4,128)(2,1)S(1)}, bf16[4,128,256]{2,0,1:T(4,128)(2,1)S(1)}, u32[]{:S(2)}, u32[]{:S(2)}) collective-permute-start(bf16[4,128,256]{2,0,1:T(4,128)(2,1)S(1)} %constant_dynamic-slice_fusion), channel_id=1, source_target_pairs={{0,4},{2,6},{4,8},{6,10},{8,12},{10,14},{12,16},{14,18},{16,20},{1... | collective-permute-start | bytes 786440 | tf_op jit(solution)/shard_map/ppermute | solution.py:18
  43.0 17.3 %collective-permute-start.2 = (bf16[4,128,256]{2,0,1:T(4,128)(2,1)S(1)}, bf16[4,128,256]{2,0,1:T(4,128)(2,1)S(1)}, u32[]{:S(2)}, u32[]{:S(2)}) collective-permute-start(bf16[4,128,256]{2,0,1:T(4,128)(2,1)S(1)} %constant_dynamic-slice_fusion), channel_id=1, source_target_pairs={{0,2},{2,4},{4,6},{6,8},{8,10},{10,12},{12,14},{14,16},{16,18},{18... | collective-permute-start | bytes 786440 | tf_op jit(solution)/shard_map/ppermute | solution.py:18
  60.8 2.8 %copy-start.1 = (f32[6,256,256]{2,1,0:T(8,128)S(1)}, f32[6,256,256]{2,1,0:T(8,128)}, u32[]{:S(2)}) copy-start(f32[6,256,256]{2,1,0:T(8,128)} %param.10) | copy-start | bytes 4718596
  63.6 1.5 copy-start.2
  67.8 1.7 %copy-start.3 = (f32[6,256,256]{2,1,0:T(8,128)S(1)}, f32[6,256,256]{2,1,0:T(8,128)}, u32[]{:S(2)}) copy-start(f32[6,256,256]{2,1,0:T(8,128)} %param.9) | copy-start | bytes 4718596
  77.8 18.7 %collective-permute-start.5 = (f32[6,128,256]{2,1,0:T(8,128)S(1)}, f32[6,128,256]{2,1,0:T(8,128)S(1)}, u32[]{:S(2)}, u32[]{:S(2)}) collective-permute-start(f32[6,128,256]{2,1,0:T(8,128)S(1)} %dynamic-slice_select_fusion), channel_id=1, source_target_pairs={{0,2},{2,4},{4,6},{6,8},{8,10},{10,12},{12,14},{14,16},{16,18},{18... | collective-permute-start | bytes 2359304 | tf_op jit(solution)/shard_map/ppermute | solution.py:18
  80.2 22.8 %collective-permute-start.7 = (f32[6,128,256]{2,1,0:T(8,128)S(1)}, f32[6,128,256]{2,1,0:T(8,128)S(1)}, u32[]{:S(2)}, u32[]{:S(2)}) collective-permute-start(f32[6,128,256]{2,1,0:T(8,128)S(1)} %dynamic-slice_select_fusion), channel_id=1, source_target_pairs={{4,0},{6,2},{8,4},{10,6},{12,8},{14,10},{16,12},{18,14},{20,16},{2... | collective-permute-start | bytes 2359304 | tf_op jit(solution)/shard_map/ppermute | solution.py:18
  83.5 50.4 %collective-permute-start.4 = (f32[6,128,256]{2,1,0:T(8,128)S(1)}, f32[6,128,256]{2,1,0:T(8,128)S(1)}, u32[]{:S(2)}, u32[]{:S(2)}) collective-permute-start(f32[6,128,256]{2,1,0:T(8,128)S(1)} %dynamic-slice_select_fusion), channel_id=1, source_target_pairs={{0,4},{2,6},{4,8},{6,10},{8,12},{10,14},{12,16},{14,18},{16,20},{1... | collective-permute-start | bytes 2359304 | tf_op jit(solution)/shard_map/ppermute | solution.py:18
  89.1 45.8 %collective-permute-start.6 = (f32[6,128,256]{2,1,0:T(8,128)S(1)}, f32[6,128,256]{2,1,0:T(8,128)S(1)}, u32[]{:S(2)}, u32[]{:S(2)}) collective-permute-start(f32[6,128,256]{2,1,0:T(8,128)S(1)} %dynamic-slice_select_fusion), channel_id=1, source_target_pairs={{2,0},{4,2},{6,4},{8,6},{10,8},{12,10},{14,12},{16,14},{18,16},{20... | collective-permute-start | bytes 2359304 | tf_op jit(solution)/shard_map/ppermute | solution.py:18
Sparse Core Ops, SparseCore 0:
  10.9 21.3 all-reduce.2
  137.0 14.6 all-gather.1
where the time goes:
time: 162 us; the launch traced here: 161 us
  waiting for transfers between devices  75.9 us (47%)
  matrix products  22.2 us (14%)
  starting transfers between devices  21.4 us (13%)
  other arithmetic  15.5 us (10%)
  between operations  15.2 us (9%)
  local copies, waits for them, and re-layouts  8.05 us (5%)
  blocking collectives  2.68 us (2%)
    ppermute x8, waiting for transfers between devices, from_behind(): lax.ppermute(value, axis, [(source, source + steps) for source in range(i...  53.2 us
    ppermute x8, starting transfers between devices, from_behind(): lax.ppermute(value, axis, [(source, source + steps) for source in range(i...  21.3 us
    all_gather x1, waiting for transfers between devices, body(): direction = lax.all_gather(collected, 'dp', axis=1, tiled=True)  14.8 us
    unnamed x3, waiting for transfers between devices  7.93 us
    unnamed x18, local copies, waits for them, and re-layouts  6.41 us
    dot_general x5, matrix products, body(): jnp.einsum('js,jab->sab', matching.astype(jnp.float32), arriving, precisi...  6.13 us
    add x6, other arithmetic, linking(): holder_pos = hold_start + jnp.arange(slot_count, dtype=jnp.int32)  3.84 us
    lt x6, other arithmetic, linking(): jnp.arange(slot_count)[None, :] < hold_count  3.77 us
  transfers between devices with their start and end apart: 10, of which 7 were waited for; matrix products, arithmetic and copies ran while one was open for 15% of the time, Pallas kernels for 0%

commit v1 on v0

v1 whole, which is shorter than its diff:
```python
import functools

import jax
import jax.numpy as jnp
from jax import lax
from jax.experimental import pallas as pl
from jax.experimental.pallas import tpu as pltpu
from jax.sharding import PartitionSpec as P

STEP = 10
CODE_ROWS = 16
CODE_STEPS = 128.0

beta_one = 0.9
beta_two = 0.95
epsilon = 1e-08

HERE, SIDE, CROSS, FLIP, FAR = range(5)


def exchange(value, pairs):
    return lax.ppermute(value, "fsdp", pairs + [(b, a) for a, b in pairs])


def partner_pairs(devices):
    side = [(i, i + 1) for i in range(0, devices - 1, 2)]
    cross = [(i, i + 1) for i in range(1, devices - 1, 2)]
    flip = [(i, i + 2) for i in range(devices - 2) if not i & 2]
    far = [(i, i + 2) for i in range(devices - 2) if i & 2]
    return (side, cross, flip, far)


def swap_cores(value):
    return lax.ppermute(value, "dp", [(0, 1), (1, 0)])


def partner_kind(me, other):
    step = other - me
    near = jnp.where(other == me ^ 1, SIDE, CROSS)
    distant = jnp.where(other == me ^ 2, FLIP, FAR)
    return jnp.where(step == 0, HERE, jnp.where(jnp.abs(step) == 1, near, distant))


def tables(shard_starts, block_owners, me, slot_count, owned_slots):
    devices = shard_starts.shape[0]
    total = block_owners.shape[0]
    ids = jnp.arange(devices, dtype=jnp.int32)
    first = jnp.sum((block_owners < me).astype(jnp.int32))
    count = jnp.sum((block_owners == me).astype(jnp.int32))
    owned = first + jnp.arange(owned_slots, dtype=jnp.int32)
    begun = shard_starts[None, :] <= owned[:, None]
    holder = jnp.sum(begun.astype(jnp.int32), axis=1) - 1
    slot = owned - jnp.max(jnp.where(begun, shard_starts[None, :], 0), axis=1)
    owned_kind = jnp.where(jnp.arange(owned_slots) < count, partner_kind(me, holder), -1)
    start = jnp.sum(jnp.where(ids == me, shard_starts, 0))
    end = jnp.sum(jnp.where(ids == me + 1, shard_starts, 0)) + jnp.where(me == devices - 1, total, 0)
    held = start + jnp.arange(slot_count, dtype=jnp.int32)
    blocks = jnp.arange(total, dtype=jnp.int32)
    owner = jnp.sum(jnp.where(blocks[None, :] == held[:, None], block_owners[None, :], 0), axis=1)
    held_kind = jnp.where(held < end, partner_kind(me, owner), -1)
    return (
        owned_kind.astype(jnp.int32),
        jnp.clip(slot, 0, slot_count - 1).astype(jnp.int32),
        held_kind.astype(jnp.int32),
    )


def split(value):
    high = value.astype(jnp.bfloat16)
    return high, (value - high.astype(jnp.float32)).astype(jnp.bfloat16)


def product(a, b, dims):
    return lax.dot_general(a, b, (dims, ((), ())), preferred_element_type=jnp.float32)


def product3(a, b, dims):
    return product(a[0], b[0], dims) + (product(a[0], b[1], dims) + product(a[1], b[0], dims))


TN = ((0,), (0,))
NN = ((1,), (0,))
NT = ((1,), (1,))


def moment_kernel(moment_ref, left_ref, right_ref, out_ref):
    left, right = split(left_ref[0]), split(right_ref[0])
    half = product3(left, split(moment_ref[0]), TN)
    out_ref[0] = product3(split(half), right, NN)


def turn_moment(first_moment, left_basis, right_basis):
    count, width, _ = first_moment.shape
    spec = pl.BlockSpec((1, width, width), lambda j: (j, 0, 0))
    return pl.pallas_call(
        moment_kernel,
        grid=(count,),
        in_specs=[spec] * 3,
        out_specs=spec,
        out_shape=jax.ShapeDtypeStruct(first_moment.shape, jnp.float32),
        cost_estimate=pl.CostEstimate(
            flops=12 * count * width**3, bytes_accessed=16 * count * width**2, transcendentals=0
        ),
        name="turn_moment",
    )(first_moment, left_basis, right_basis)


def collect_kernel(kind_ref, slot_ref, *refs, rows, extra):
    sources, out_ref, sem = refs[:5], refs[5], refs[6]
    count = kind_ref.shape[0]

    def each(j, act):
        for kind in range(5):

            @pl.when(kind_ref[j] == kind)
            def _():
                act(
                    pltpu.make_async_copy(
                        sources[kind].at[pl.ds(pl.multiple_of(slot_ref[j] * rows, rows), rows)],
                        out_ref.at[pl.ds(j * rows, rows)],
                        sem.at[j],
                    )
                )

    for j in range(count):
        each(j, lambda copy: copy.start())
    for j in range(count):
        each(j, lambda copy: copy.wait())


def collect(kind, slot, sources):
    count = kind.shape[0]
    rows, width = sources[0].shape[1:]
    flat = [source.reshape(-1, width) for source in sources]
    out = pl.pallas_call(
        functools.partial(collect_kernel, rows=rows, extra=0),
        in_specs=[pl.BlockSpec(memory_space=pltpu.SMEM)] * 2 + [pl.BlockSpec(memory_space=pl.ANY)] * 5,
        out_specs=pl.BlockSpec(memory_space=pltpu.VMEM),
        out_shape=jax.ShapeDtypeStruct((count * rows, width), sources[0].dtype),
        scratch_shapes=[pltpu.SemaphoreType.DMA((count,))],
        name="collect",
    )(kind, slot, *flat)
    return out.reshape(count, rows, width)


def step_kernel(
    kind_ref,
    slot_ref,
    place_ref,
    mine_ref,
    other_ref,
    moment_ref,
    second_ref,
    left_ref,
    right_ref,
    turned_ref,
    first_out,
    second_out,
    *refs,
):
    sends, codes = refs[:5], refs[5]
    j = pl.program_id(0)
    live = kind_ref[j] >= 0
    half = mine_ref.shape[1]
    here = pl.multiple_of(place_ref[0] * half, half)
    there = pl.multiple_of((1 - place_ref[0]) * half, half)
    parts = ((here, mine_ref), (there, other_ref))

    @pl.when(j == 0)
    def _():
        codes[...] = jnp.zeros_like(codes)

    @pl.when(jnp.logical_not(live))
    def _():
        first_out[...] = jnp.zeros_like(first_out)
        second_out[...] = jnp.zeros_like(second_out)

    @pl.when(live)
    def _():
        right = split(right_ref[0])
        half_turned = None
        for at, part in parts:
            gradient = part[0]
            first_out[0, pl.ds(at, half)] = beta_one * moment_ref[0, pl.ds(at, half)] + (
                1.0 - beta_one
            ) * gradient.astype(jnp.float32)
            high, low = split(left_ref[0, pl.ds(at, half)])
            term = product(high, gradient, TN) + product(low, gradient, TN)
            half_turned = term if half_turned is None else half_turned + term
        turned = product3(split(half_turned), right, NN)
        second = beta_two * second_ref[0] + (1.0 - beta_two) * turned * turned
        second_out[0] = second
        turned_moment = beta_one * turned_ref[0] + (1.0 - beta_one) * turned
        bias_one = 1.0 - beta_one**STEP
        bias_two = 1.0 - beta_two**STEP
        scaled = turned_moment / bias_one / (jnp.sqrt(second / bias_two) + epsilon)
        back = product3(split(left_ref[0, pl.ds(here, half)]), split(scaled), NN)
        update = product3(split(back), right, NT)
        peak = jnp.max(jnp.abs(update), axis=0, keepdims=True)
        code = jnp.ceil(jnp.log2(jnp.maximum(peak, 1e-30) * (1.0 / 32000.0)) * CODE_STEPS)
        coded = jnp.round(update * jnp.exp2(code * (-1.0 / CODE_STEPS)))
        coded = jnp.clip(coded, -32767.0, 32767.0).astype(jnp.int32).astype(jnp.int16)
        slot = slot_ref[j]
        rows = pl.ds(pl.multiple_of(slot * half, half), half)
        spots = lax.broadcasted_iota(jnp.int32, codes.shape[1:], 0)
        for kind in range(5):

            @pl.when(kind_ref[j] == kind)
            def _():
                sends[kind][rows] = coded
                codes[kind] = jnp.where(spots == slot, code.astype(jnp.int32), codes[kind])

    @pl.when(j == pl.num_programs(0) - 1)
    def _():
        for kind in range(5):
            top = sends[kind].shape[0] - CODE_ROWS
            sends[kind][pl.ds(top, CODE_ROWS)] = codes[kind].astype(jnp.int16)


def soap_step(kind, slot, place, mine, other, moment, second, left, right, turned, slot_count):
    count, width, _ = moment.shape
    half = mine.shape[1]
    full = pl.BlockSpec((1, width, width), lambda j, *_: (j, 0, 0))
    part = pl.BlockSpec((1, half, width), lambda j, *_: (j, 0, 0))
    send_rows = slot_count * half + CODE_ROWS
    send = pl.BlockSpec((send_rows, width), lambda j, *_: (0, 0))
    return pl.pallas_call(
        step_kernel,
        grid_spec=pltpu.PrefetchScalarGridSpec(
            num_scalar_prefetch=3,
            grid=(count,),
            in_specs=[part, part, full, full, full, full, full],
            out_specs=[full, full] + [send] * 5,
            scratch_shapes=[pltpu.VMEM((5, CODE_ROWS, width), jnp.int32)],
        ),
        out_shape=[jax.ShapeDtypeStruct(moment.shape, jnp.float32)] * 2
        + [jax.ShapeDtypeStruct((send_rows, width), jnp.int16)] * 5,
        name="soap_step",
    )(kind, slot, place, mine, other, moment, second, left, right, turned)


def gather_kernel(kind_ref, *refs, half):
    sources, out_ref, codes, sem, code_sem = refs[:5], refs[5], refs[6], refs[7], refs[8]
    count = kind_ref.shape[0]
    top = count * half

    def code_copy(kind):
        return pltpu.make_async_copy(
            sources[kind].at[pl.ds(top, CODE_ROWS)], codes.at[kind], code_sem.at[kind]
        )

    def each(s, act):
        for kind in range(5):

            @pl.when(kind_ref[s] == kind)
            def _():
                rows = pl.ds(s * half, half)
                act(pltpu.make_async_copy(sources[kind].at[rows], out_ref.at[rows], sem.at[s]))

    for kind in range(5):
        code_copy(kind).start()
    for s in range(count):
        each(s, lambda copy: copy.start())
    for kind in range(5):
        code_copy(kind).wait()
    spots = lax.broadcasted_iota(jnp.int32, codes.shape[1:], 0)
    chosen = jnp.zeros(codes.shape[1:], jnp.int32)
    for s in range(count):
        for kind in range(5):
            use = jnp.logical_and(spots == s, kind_ref[s] == kind)
            chosen = jnp.where(use, codes[kind].astype(jnp.int32), chosen)
    out_ref[pl.ds(top, CODE_ROWS)] = chosen.astype(jnp.int16)
    for s in range(count):
        each(s, lambda copy: copy.wait())


def gather_held(kind, sources):
    count = kind.shape[0]
    rows, width = sources[0].shape
    half = (rows - CODE_ROWS) // count
    return pl.pallas_call(
        functools.partial(gather_kernel, half=half),
        in_specs=[pl.BlockSpec(memory_space=pltpu.SMEM)] + [pl.BlockSpec(memory_space=pl.ANY)] * 5,
        out_specs=pl.BlockSpec(memory_space=pltpu.VMEM),
        out_shape=jax.ShapeDtypeStruct((rows, width), sources[0].dtype),
        scratch_shapes=[
            pltpu.VMEM((5, CODE_ROWS, width), jnp.int16),
            pltpu.SemaphoreType.DMA((count,)),
            pltpu.SemaphoreType.DMA((5,)),
        ],
        name="gather_held",
    )(kind, *sources)


def decode_kernel(kind_ref, place_ref, mine_ref, other_ref, mine_code, other_code, out_ref):
    s = pl.program_id(0)
    half = mine_ref.shape[0]
    live = kind_ref[s] >= 0
    spots = lax.broadcasted_iota(jnp.int32, mine_code.shape, 0)
    for place, coded, codes in ((place_ref[0], mine_ref, mine_code), (1 - place_ref[0], other_ref, other_code)):
        picked = jnp.where(spots == s, codes[...].astype(jnp.int32).astype(jnp.float32), 0.0)
        scale = jnp.exp2(jnp.sum(picked, axis=0, keepdims=True) * (1.0 / CODE_STEPS))
        value = coded[...].astype(jnp.int32).astype(jnp.float32) * scale
        out_ref[0, pl.ds(pl.multiple_of(place * half, half), half)] = jnp.where(live, value, 0.0)


def decode(kind, place, mine, other, width):
    count = kind.shape[0]
    half = (mine.shape[0] - CODE_ROWS) // count
    body_spec = pl.BlockSpec((half, width), lambda s, *_: (s, 0))
    code_spec = pl.BlockSpec((CODE_ROWS, width), lambda s, *_: (count * half // CODE_ROWS, 0))
    return pl.pallas_call(
        decode_kernel,
        grid_spec=pltpu.PrefetchScalarGridSpec(
            num_scalar_prefetch=2,
            grid=(count,),
            in_specs=[body_spec, body_spec, code_spec, code_spec],
            out_specs=pl.BlockSpec((1, 2 * half, width), lambda s, *_: (s, 0, 0)),
        ),
        out_shape=jax.ShapeDtypeStruct((count, 2 * half, width), jnp.float32),
        name="decode",
    )(kind, place, mine, other, mine, other)


def body(
    gradients, first_moment, second_moment, left_basis, right_basis, shard_starts, block_owners
):
    me = lax.axis_index("fsdp").astype(jnp.int32)
    core = lax.axis_index("dp").astype(jnp.int32)
    devices = lax.axis_size("fsdp")
    slot_count, width = gradients.shape[1], gradients.shape[3]
    owned_slots = first_moment.shape[0]
    half = width // lax.axis_size("dp")
    side, cross, flip, far = partner_pairs(devices)
    own_kind, own_slot, held_kind = tables(shard_starts, block_owners, me, slot_count, owned_slots)
    place = core.reshape(1)

    replica = gradients[0]
    twin = swap_cores(replica)

    def rows_of(value):
        return lax.dynamic_slice_in_dim(value, core * half, half, 1).astype(jnp.float32)

    summed = (rows_of(replica) + rows_of(twin)).astype(jnp.bfloat16)
    by_side = exchange(summed, side)
    by_flip = exchange(summed, flip)
    by_cross = exchange(summed, cross)
    by_far = exchange(summed, far)
    turned = turn_moment(first_moment, left_basis, right_basis)
    mine = collect(own_kind, own_slot, (summed, by_side, by_cross, by_flip, by_far))
    other = swap_cores(mine)
    first_new, second_new, keep, to_side, to_cross, to_flip, to_far = soap_step(
        own_kind,
        own_slot,
        place,
        mine,
        other,
        first_moment,
        second_moment,
        left_basis,
        right_basis,
        turned,
        slot_count,
    )
    sent = (
        keep,
        exchange(to_side, side),
        exchange(to_cross, cross),
        exchange(to_flip, flip),
        exchange(to_far, far),
    )
    coded = gather_held(held_kind, sent)
    direction = decode(held_kind, place, coded, swap_cores(coded), width)
    return (direction, first_new, second_new)


def solution(mesh):
    in_specs = (
        P("dp", "fsdp", None, None),
        P("fsdp", None, None),
        P("fsdp", None, None),
        P("fsdp", None, None),
        P("fsdp", None, None),
        P(),
        P(),
    )
    out_specs = (P("fsdp", None, None), P("fsdp", None, None), P("fsdp", None, None))
    return jax.shard_map(body, mesh=mesh, in_specs=in_specs, out_specs=out_specs, check_vma=False)
```

time: 162 us -> 85.8 us (0.53)
  waiting for transfers between devices: 75.9 us -> 28.7 us
  Pallas kernels: 0 us -> 25.4 us
  matrix products: 22.2 us -> 0 us
  between operations: 15.2 us -> 1.36 us
  other arithmetic: 15.5 us -> 8.19 us
  local copies, waits for them, and re-layouts: 8.05 us -> 2.95 us
  starting transfers between devices: 21.4 us -> 18.4 us
  blocking collectives: 2.68 us -> 0 us
    pallas_call x0 -> x5, Pallas kernels: none -> 25.4 us  [the longest x1 9.77 us: soap_step(): pl.pallas_call(step_kernel, grid_spec=pltpu.PrefetchScalarGridSpec(num_sc...]
    ppermute x8 -> x11, waiting for transfers between devices: 53.2 us -> 28.7 us  [the longest x8 26.9 us: exchange(): return lax.ppermute(value, 'fsdp', pairs + [(b, a) for a, b in pairs])]
    dot_general x16 -> x0, matrix products: 22.2 us -> none  [the longest x5 6.13 us: body(): jnp.einsum('js,jab->sab', matching.astype(jnp.float32), arriving, precisi...]
    all_gather x1 -> x0, waiting for transfers between devices: 14.8 us -> none  [body(): direction = lax.all_gather(collected, 'dp', axis=1, tiled=True)]
    unnamed x3 -> x0, waiting for transfers between devices: 7.93 us -> none
    lt x12 -> x0, other arithmetic: 7.56 us -> none  [the longest x6 3.77 us: linking(): jnp.arange(slot_count)[None, :] < hold_count]
    add x12 -> x2, other arithmetic: 7.47 us -> 1.22 us  [the longest x1 0.65 us: tables(): owned = first + jnp.arange(owned_slots, dtype=jnp.int32)]
    unnamed x18 -> x26, local copies, waits for them, and re-layouts: 6.41 us -> 2.95 us
  transfers between devices with their start and end apart: 10 -> 11, of which waited for: 7 -> 4; matrix products, arithmetic and copies ran while one was open for 15% -> 8% of each run, Pallas kernels for 0% -> 8%
where the time goes in v1:
time: 85.8 us; the launch traced here: 84.9 us
  waiting for transfers between devices  28.7 us (33%)
  Pallas kernels  25.4 us (30%)
  starting transfers between devices  18.4 us (21%)
  other arithmetic  8.19 us (10%)
  local copies, waits for them, and re-layouts  2.95 us (3%)
  between operations  1.36 us (2%)
    ppermute x8, waiting for transfers between devices, exchange(): return lax.ppermute(value, 'fsdp', pairs + [(b, a) for a, b in pairs])  26.9 us
    ppermute x8, starting transfers between devices, exchange(): return lax.ppermute(value, 'fsdp', pairs + [(b, a) for a, b in pairs])  17.7 us
    pallas_call x1, Pallas kernels, soap_step(): pl.pallas_call(step_kernel, grid_spec=pltpu.PrefetchScalarGridSpec(num_sc...  9.77 us
    pallas_call x1, Pallas kernels, turn_moment(): pl.pallas_call(moment_kernel, grid=(count,), in_specs=[spec] * 3, out_spe...  6.94 us
    pallas_call x1, Pallas kernels, decode(): pl.pallas_call(decode_kernel, grid_spec=pltpu.PrefetchScalarGridSpec(num_...  3.94 us
    unnamed x26, local copies, waits for them, and re-layouts  2.95 us
    pallas_call x1, Pallas kernels, gather_held(): pl.pallas_call(functools.partial(gather_kernel, half=half), in_specs=[pl....  2.42 us
    pallas_call x1, Pallas kernels, collect(): pl.pallas_call(functools.partial(collect_kernel, rows=rows, extra=0), in_...  2.35 us
  transfers between devices with their start and end apart: 11, of which 4 were waited for; matrix products, arithmetic and copies ran while one was open for 8% of the time, Pallas kernels for 8%

profile of v1, /device:TPU:0, one launch (start us, length us, event | category | flops | bytes accessed | tf_op | source)
XLA Modules:
  0.0 84.9 jit_solution(9320902489320832501)
XLA Ops:
  0.6 0.6 collective-permute-start
  1.2 1.3 %fusion.5 = (s32[]{:T(128)}, s32[]{:T(128)}) fusion(s32[48]{0:T(128)} %param.13, s32[]{:T(128)S(6)} %axis_index.23), kind=kLoop, calls=%fused_computation.24 | loop fusion | flops 286 | bytes 204 | tf_op jit(solution)/shard_map/reduce_sum | solution.py:49
  2.5 0.6 iota_add_fusion
  3.2 1.0 %fusion = bf16[4,128,256]{2,1,0:T(8,128)(2,1)S(1)} fusion(bf16[4,256,256]{2,1,0:T(8,128)(2,1)S(1)} %collective-permute-done, s32[]{:T(128)S(6)} %select_n.76, bf16[1,4,256,256]{3,2,1,0:T(8,128)(2,1)} %param.7), kind=kLoop, calls=%fused_computation.1 | loop fusion | flops 524288 | bytes 786436 | tf_op jit(solution)/shard_map/convert_element_type | solution.py:344
  4.2 0.7 collective-permute-start.4
  4.9 5.5 %collective-permute-start.3 = (bf16[4,128,256]{2,1,0:T(8,128)(2,1)S(1)}, bf16[4,128,256]{2,1,0:T(8,128)(2,1)S(1)}, u32[]{:S(2)}, u32[]{:S(2)}) collective-permute-start(bf16[4,128,256]{2,1,0:T(8,128)(2,1)S(1)} %fusion), channel_id=1, source_target_pairs={{0,4},{2,6},{8,12},{10,14},{16,20},{18,22},{24,28},{26,30},{4,0},{... | collective-permute-start | bytes 786440 | tf_op jit(solution)/shard_map/ppermute | solution.py:22
  10.4 0.7 collective-permute-start.2
  11.0 2.8 %collective-permute-start.1 = (bf16[4,128,256]{2,1,0:T(8,128)(2,1)S(1)}, bf16[4,128,256]{2,1,0:T(8,128)(2,1)S(1)}, u32[]{:S(2)}, u32[]{:S(2)}) collective-permute-start(bf16[4,128,256]{2,1,0:T(8,128)(2,1)S(1)} %fusion), channel_id=1, source_target_pairs={{0,2},{4,6},{8,10},{12,14},{16,18},{20,22},{24,26},{28,30},{2,0},{... | collective-permute-start | bytes 786440 | tf_op jit(solution)/shard_map/ppermute | solution.py:22
  13.8 0.9 %fusion.2 = (s32[6]{0:T(128)S(1)}, s32[6]{0:T(128)S(1)}) fusion(s32[16]{0:T(128)} %param.12, s32[6]{0:T(128)S(1)} %iota_add_fusion), kind=kLoop, calls=%fused_computation.5 | loop fusion | flops 468 | bytes 136 | tf_op jit(solution)/shard_map/reduce_max | solution.py:53
  14.7 1.8 %compare_select_fusion.5 = (s32[6]{0:T(128)}, s32[6]{0:T(128)}) fusion(s32[6]{0:T(128)S(1)} %get-tuple-element.18, s32[]{:T(128)S(6)} %xor.9, s32[]{:T(128)S(6)} %xor.8, s32[]{:T(128)S(6)} %axis_index.23, s32[]{:T(128)} %get-tuple-element.19, s32[6]{0:T(128)S(1)} %get-tuple-element.17, s32[]{:T(128)} %get-tuple-element.20), kind=kLoop, calls=%fused_computation.13 | loop fusion | flops 96 | bytes 116 | tf_op jit(solution)/shard_map/jit(_where)/select_n | solution.py:54
  16.5 10.4 %collective-permute-done.3 = bf16[4,128,256]{2,1,0:T(8,128)(2,1)S(1)} collective-permute-done((bf16[4,128,256]{2,1,0:T(8,128)(2,1)S(1)}, bf16[4,128,256]{2,1,0:T(8,128)(2,1)S(1)}, u32[]{:S(2)}, u32[]{:S(2)}) %collective-permute-start.3) | collective-permute-done | bytes 262176 | tf_op jit(solution)/shard_map/ppermute | solution.py:22
  27.0 1.1 %collective-permute-done.1 = bf16[4,128,256]{2,1,0:T(8,128)(2,1)S(1)} collective-permute-done((bf16[4,128,256]{2,1,0:T(8,128)(2,1)S(1)}, bf16[4,128,256]{2,1,0:T(8,128)(2,1)S(1)}, u32[]{:S(2)}, u32[]{:S(2)}) %collective-permute-start.1) | collective-permute-done | bytes 262176 | tf_op jit(solution)/shard_map/ppermute | solution.py:22
  28.1 0.7 copy-done.10
  28.7 2.3 %collect.1 = bf16[768,256]{1,0:T(8,128)(2,1)} custom-call(s32[6]{0:T(128)} %get-tuple-element.23.kind_ref, s32[6]{0:T(128)} %get-tuple-element.24.slot_ref, bf16[512,256]{1,0:T(8,128)(2,1)} %bitcast.13, bf16[512,256]{1,0:T(8,128)(2,1)} %bitcast.17, bf16[512,256]{1,0:T(8,128)(2,1)} %bitcast.16, bf16[512,256]{1,0:T(8,128)(2,1)} %bitcast.15, ...), custom_call_target="tpu_custom_call" | custom-call | tf_op jit(solution)/shard_map/collect/pallas_call | solution.py:135
  31.2 0.6 fusion.4
  31.8 0.6 iota_add_fusion.1
  32.4 6.9 %turn_moment.1.turned_ref = f32[6,256,256]{2,1,0:T(8,128)} custom-call(f32[6,256,256]{2,1,0:T(8,128)} %moment_ref.3, f32[6,256,256]{2,1,0:T(8,128)} %left_ref.3, f32[6,256,256]{2,1,0:T(8,128)} %right_ref.3), custom_call_target="tpu_custom_call" | custom-call | flops 1207959552 | bytes 6291456 | tf_op jit(solution)/shard_map/turn_moment/pallas_call | solution.py:95
  39.3 0.8 copy-done.2
  40.1 9.8 %soap_step.1 = (f32[6,256,256]{2,1,0:T(8,128)}, f32[6,256,256]{2,1,0:T(8,128)}, s16[528,256]{1,0:T(8,128)(2,1)}, s16[528,256]{1,0:T(8,128)(2,1)}, s16[528,256]{1...) custom-call(s32[6]{0:T(128)} %get-tuple-element.23.kind_ref, s32[6]{0:T(128)} %get-tuple-element.24.slot_ref, ...), custom_call_target="tpu_custom_call" | custom-call | tf_op jit(solution)/shard_map/soap_step/pallas_call | solution.py:227
  49.8 1.8 %collective-permute-start.6 = (s16[528,256]{1,0:T(8,128)(2,1)}, s16[528,256]{1,0:T(8,128)(2,1)S(1)}, u32[]{:S(2)}, u32[]{:S(2)}) collective-permute-start(s16[528,256]{1,0:T(8,128)(2,1)} %get-tuple-element.11), channel_id=1, source_target_pairs={{0,2},{4,6},{8,10},{12,14},{16,18},{20,22},{24,26},{28,30},{2,0},{... | collective-permute-start | bytes 811016 | tf_op jit(solution)/shard_map/ppermute | solution.py:22
  51.6 0.7 collective-permute-start.7
  52.3 5.0 %collective-permute-start.8 = (s16[528,256]{1,0:T(8,128)(2,1)}, s16[528,256]{1,0:T(8,128)(2,1)S(1)}, u32[]{:S(2)}, u32[]{:S(2)}) collective-permute-start(s16[528,256]{1,0:T(8,128)(2,1)} %get-tuple-element.13), channel_id=1, source_target_pairs={{0,4},{2,6},{8,12},{10,14},{16,20},{18,22},{24,28},{26,30},{4,0},{... | collective-permute-start | bytes 811016 | tf_op jit(solution)/shard_map/ppermute | solution.py:22
  57.2 0.7 collective-permute-start.9
  57.9 0.2 select_reduce_fusion
  58.7 1.2 %compare_select_fusion.10.kind_ref = s32[4]{0:T(128)} fusion(s32[4]{0:T(128)S(1)} %select_reduce_fusion, s32[]{:T(128)S(6)} %xor.9, s32[]{:T(128)S(6)} %xor.8, s32[]{:T(128)S(6)} %axis_index.23, s32[]{:T(128)S(6)} %add.37, s32[]{:T(128)} %get-tuple-element.22), kind=kLoop, calls=%fused_computation.19 | loop fusion | flops 52 | bytes 52 | tf_op jit(solution)/shard_map/jit(_where)/select_n | solution.py:60
  59.8 15.4 %collective-permute-done.8.refs_3_ = s16[528,256]{1,0:T(8,128)(2,1)S(1)} collective-permute-done((s16[528,256]{1,0:T(8,128)(2,1)}, s16[528,256]{1,0:T(8,128)(2,1)S(1)}, u32[]{:S(2)}, u32[]{:S(2)}) %collective-permute-start.8) | collective-permute-done | bytes 270368 | tf_op jit(solution)/shard_map/ppermute | solution.py:22
  75.3 0.7 copy-done.5
  76.0 0.1 copy-done.6
  76.1 2.4 %gather_held.1.mine_ref.mine_code = s16[528,256]{1,0:T(8,128)(2,1)} custom-call(s32[4]{0:T(128)} %compare_select_fusion.10.kind_ref, s16[528,256]{1,0:T(8,128)(2,1)} %get-tuple-element.10.refs_0_, s16[528,256]{1,0:T(8,128)(2,1)} %copy-done.3, s16[528,256]{1,0:T(8,128)(2,1)} %copy-done.4, s16[528,256]{1,0:T(8,128)(2,1)} %copy-done.5, s16[528,256]{1,0:T(8,128)(2,1)} %copy-done.6), custom_call_target="tpu_custom_call" | custom-call | tf_op jit(solution)/shard_map/gather_held/pallas_call | solution.py:281
  78.6 1.7 %collective-permute-done.10.other_ref.other_code = s16[528,256]{1,0:T(8,128)(2,1)S(1)} collective-permute-done((s16[528,256]{1,0:T(8,128)(2,1)}, s16[528,256]{1,0:T(8,128)(2,1)S(1)}, u32[]{:S(2)}, u32[]{:S(2)}) %collective-permute-start.10) | collective-permute-done | bytes 270368 | tf_op jit(solution)/shard_map/ppermute | solution.py:34
  80.3 0.7 copy-done
  81.0 3.9 %decode.1 = f32[4,256,256]{2,1,0:T(8,128)} custom-call(s32[4]{0:T(128)} %compare_select_fusion.10.kind_ref, s32[1]{0:T(128)} %bitcast.place_ref, s16[528,256]{1,0:T(8,128)(2,1)} %gather_held.1.mine_ref.mine_code, s16[528,256]{1,0:T(8,128)(2,1)} %copy-done, s16[528,256]{1,0:T(8,128)(2,1)} %gather_held.1.mine_ref.mine_code, s16[528,256]{1,0:T(8,128)(2,1)} %copy-done), custom_call_target="tpu_custom_call" | custom-call | tf_op jit(solution)/shard_map/decode/pallas_call | solution.py:312
  (30 shorter events, 0.2 us)
Async XLA Ops:
  0.6 30.5 %copy-start.11 = (s32[16]{0:T(128)S(1)}, s32[16]{0:T(128)}, u32[]{:S(2)}) copy-start(s32[16]{0:T(128)} %param.12) | copy-start | bytes 196
  0.6 2.5 %collective-permute-start = (bf16[4,256,256]{2,1,0:T(8,128)(2,1)}, bf16[4,256,256]{2,1,0:T(8,128)(2,1)S(1)}, u32[]{:S(2)}, u32[]{:S(2)}) collective-permute-start(bf16[4,256,256]{2,1,0:T(8,128)(2,1)} %bitcast.18), channel_id=1, source_target_pairs={{0,1},{1,0},{2,3},{3,2},{4,5},{5,4},{6,7},{7,6},{8,9},{9,8},{10,11... | collective-permute-start | bytes 1572872 | tf_op jit(solution)/shard_map/ppermute | solution.py:34
  4.2 23.8 %copy-start.1 = (bf16[4,128,256]{2,1,0:T(8,128)(2,1)}, bf16[4,128,256]{2,1,0:T(8,128)(2,1)S(1)}, u32[]{:S(2)}) copy-start(bf16[4,128,256]{2,1,0:T(8,128)(2,1)S(1)} %fusion) | copy-start | bytes 786436
  4.2 12.3 %collective-permute-start.4 = (bf16[4,128,256]{2,1,0:T(8,128)(2,1)S(1)}, bf16[4,128,256]{2,1,0:T(8,128)(2,1)S(1)}, u32[]{:S(2)}, u32[]{:S(2)}) collective-permute-start(bf16[4,128,256]{2,1,0:T(8,128)(2,1)S(1)} %fusion), channel_id=1, source_target_pairs={{4,8},{6,10},{12,16},{14,18},{20,24},{22,26},{8,4},{10,6},{16,12},... | collective-permute-start | bytes 786440 | tf_op jit(solution)/shard_map/ppermute | solution.py:22
  4.9 22.1 %collective-permute-start.3 = (bf16[4,128,256]{2,1,0:T(8,128)(2,1)S(1)}, bf16[4,128,256]{2,1,0:T(8,128)(2,1)S(1)}, u32[]{:S(2)}, u32[]{:S(2)}) collective-permute-start(bf16[4,128,256]{2,1,0:T(8,128)(2,1)S(1)} %fusion), channel_id=1, source_target_pairs={{0,4},{2,6},{8,12},{10,14},{16,20},{18,22},{24,28},{26,30},{4,0},{... | collective-permute-start | bytes 786440 | tf_op jit(solution)/shard_map/ppermute | solution.py:22
  10.4 16.6 %collective-permute-start.2 = (bf16[4,128,256]{2,1,0:T(8,128)(2,1)S(1)}, bf16[4,128,256]{2,1,0:T(8,128)(2,1)S(1)}, u32[]{:S(2)}, u32[]{:S(2)}) collective-permute-start(bf16[4,128,256]{2,1,0:T(8,128)(2,1)S(1)} %fusion), channel_id=1, source_target_pairs={{2,4},{6,8},{10,12},{14,16},{18,20},{22,24},{26,28},{4,2},{8,6},{1... | collective-permute-start | bytes 786440 | tf_op jit(solution)/shard_map/ppermute | solution.py:22
  11.0 17.0 %collective-permute-start.1 = (bf16[4,128,256]{2,1,0:T(8,128)(2,1)S(1)}, bf16[4,128,256]{2,1,0:T(8,128)(2,1)S(1)}, u32[]{:S(2)}, u32[]{:S(2)}) collective-permute-start(bf16[4,128,256]{2,1,0:T(8,128)(2,1)S(1)} %fusion), channel_id=1, source_target_pairs={{0,2},{4,6},{8,10},{12,14},{16,18},{20,22},{24,26},{28,30},{2,0},{... | collective-permute-start | bytes 786440 | tf_op jit(solution)/shard_map/ppermute | solution.py:22
  16.5 11.5 %copy-start.7 = (bf16[4,128,256]{2,1,0:T(8,128)(2,1)}, bf16[4,128,256]{2,1,0:T(8,128)(2,1)S(1)}, u32[]{:S(2)}) copy-start(bf16[4,128,256]{2,1,0:T(8,128)(2,1)S(1)} %collective-permute-done.4) | copy-start | bytes 786436
  27.0 1.1 %copy-start.8 = (bf16[4,128,256]{2,1,0:T(8,128)(2,1)}, bf16[4,128,256]{2,1,0:T(8,128)(2,1)S(1)}, u32[]{:S(2)}) copy-start(bf16[4,128,256]{2,1,0:T(8,128)(2,1)S(1)} %collective-permute-done.3) | copy-start | bytes 786436
  27.0 1.1 %copy-start.9 = (bf16[4,128,256]{2,1,0:T(8,128)(2,1)}, bf16[4,128,256]{2,1,0:T(8,128)(2,1)S(1)}, u32[]{:S(2)}) copy-start(bf16[4,128,256]{2,1,0:T(8,128)(2,1)S(1)} %collective-permute-done.2) | copy-start | bytes 786436
  28.0 0.7 copy-start.10
  31.1 8.2 %collective-permute-start.5 = (bf16[6,128,256]{2,1,0:T(8,128)(2,1)}, bf16[6,128,256]{2,1,0:T(8,128)(2,1)S(1)}, u32[]{:S(2)}, u32[]{:S(2)}) collective-permute-start(bf16[6,128,256]{2,1,0:T(8,128)(2,1)} %bitcast.11), channel_id=1, source_target_pairs={{0,1},{1,0},{2,3},{3,2},{4,5},{5,4},{6,7},{7,6},{8,9},{9,8},{10,11... | collective-permute-start | bytes 1179656 | tf_op jit(solution)/shard_map/ppermute | solution.py:34
  39.3 0.8 copy-start.2
  40.1 17.9 %copy-start.12 = (s32[48]{0:T(128)S(1)}, s32[48]{0:T(128)}, u32[]{:S(2)}) copy-start(s32[48]{0:T(128)} %param.13) | copy-start | bytes 580
  49.8 10.0 %collective-permute-start.6 = (s16[528,256]{1,0:T(8,128)(2,1)}, s16[528,256]{1,0:T(8,128)(2,1)S(1)}, u32[]{:S(2)}, u32[]{:S(2)}) collective-permute-start(s16[528,256]{1,0:T(8,128)(2,1)} %get-tuple-element.11), channel_id=1, source_target_pairs={{0,2},{4,6},{8,10},{12,14},{16,18},{20,22},{24,26},{28,30},{2,0},{... | collective-permute-start | bytes 811016 | tf_op jit(solution)/shard_map/ppermute | solution.py:22
  51.6 8.2 %collective-permute-start.7 = (s16[528,256]{1,0:T(8,128)(2,1)}, s16[528,256]{1,0:T(8,128)(2,1)S(1)}, u32[]{:S(2)}, u32[]{:S(2)}) collective-permute-start(s16[528,256]{1,0:T(8,128)(2,1)} %get-tuple-element.12), channel_id=1, source_target_pairs={{2,4},{6,8},{10,12},{14,16},{18,20},{22,24},{26,28},{4,2},{8,6},{1... | collective-permute-start | bytes 811016 | tf_op jit(solution)/shard_map/ppermute | solution.py:22
  52.3 23.0 %collective-permute-start.8 = (s16[528,256]{1,0:T(8,128)(2,1)}, s16[528,256]{1,0:T(8,128)(2,1)S(1)}, u32[]{:S(2)}, u32[]{:S(2)}) collective-permute-start(s16[528,256]{1,0:T(8,128)(2,1)} %get-tuple-element.13), channel_id=1, source_target_pairs={{0,4},{2,6},{8,12},{10,14},{16,20},{18,22},{24,28},{26,30},{4,0},{... | collective-permute-start | bytes 811016 | tf_op jit(solution)/shard_map/ppermute | solution.py:22
  57.2 18.0 %collective-permute-start.9 = (s16[528,256]{1,0:T(8,128)(2,1)}, s16[528,256]{1,0:T(8,128)(2,1)S(1)}, u32[]{:S(2)}, u32[]{:S(2)}) collective-permute-start(s16[528,256]{1,0:T(8,128)(2,1)} %get-tuple-element.14), channel_id=1, source_target_pairs={{4,8},{6,10},{12,16},{14,18},{20,24},{22,26},{8,4},{10,6},{16,12},... | collective-permute-start | bytes 811016 | tf_op jit(solution)/shard_map/ppermute | solution.py:22
  59.8 15.4 %copy-start.3 = (s16[528,256]{1,0:T(8,128)(2,1)}, s16[528,256]{1,0:T(8,128)(2,1)S(1)}, u32[]{:S(2)}) copy-start(s16[528,256]{1,0:T(8,128)(2,1)S(1)} %collective-permute-done.6.refs_1_) | copy-start | bytes 811012
  59.8 15.4 %copy-start.4 = (s16[528,256]{1,0:T(8,128)(2,1)}, s16[528,256]{1,0:T(8,128)(2,1)S(1)}, u32[]{:S(2)}) copy-start(s16[528,256]{1,0:T(8,128)(2,1)S(1)} %collective-permute-done.7.refs_2_) | copy-start | bytes 811012
  75.3 0.7 copy-start.5
  75.3 0.8 copy-start.6
  78.5 1.8 %collective-permute-start.10 = (s16[528,256]{1,0:T(8,128)(2,1)}, s16[528,256]{1,0:T(8,128)(2,1)S(1)}, u32[]{:S(2)}, u32[]{:S(2)}) collective-permute-start(s16[528,256]{1,0:T(8,128)(2,1)} %gather_held.1.mine_ref.mine_code), channel_id=1, source_target_pairs={{0,1},{1,0},{2,3},{3,2},{4,5},{5,4},{6,7},{7,6},{8,9},{9,8},{10,11... | collective-permute-start | bytes 811016 | tf_op jit(solution)/shard_map/ppermute | solution.py:34
  80.3 0.7 copy-start

commit v2 on v1

v2 whole, which is shorter than its diff:
```python
import jax
import jax.numpy as jnp
from jax import lax
from jax.experimental import pallas as pl
from jax.experimental.pallas import tpu as pltpu
from jax.sharding import PartitionSpec as P


STEP = 10
CODE_ROWS = 16
CODE_STEPS = 128.0
GROUP = 3
SMALL_VMEM = 12 * 2**20
STEP_VMEM = 28 * 2**20

beta_one = 0.9
beta_two = 0.95
epsilon = 1e-08

HERE, SIDE, CROSS, FLIP, FAR = range(5)


def exchange(value, pairs):
    return lax.ppermute(value, "fsdp", pairs + [(b, a) for a, b in pairs])


def partner_pairs(devices):
    side = [(i, i + 1) for i in range(0, devices - 1, 2)]
    cross = [(i, i + 1) for i in range(1, devices - 1, 2)]
    flip = [(i, i + 2) for i in range(devices - 2) if not i & 2]
    far = [(i, i + 2) for i in range(devices - 2) if i & 2]
    return (side, cross, flip, far)


def swap_cores(value):
    return lax.ppermute(value, "dp", [(0, 1), (1, 0)])


def partner_kind(me, other):
    step = other - me
    near = jnp.where(other == me ^ 1, SIDE, CROSS)
    distant = jnp.where(other == me ^ 2, FLIP, FAR)
    return jnp.where(step == 0, HERE, jnp.where(jnp.abs(step) == 1, near, distant))


def tables(shard_starts, block_owners, me, slot_count, owned_slots):
    devices = shard_starts.shape[0]
    total = block_owners.shape[0]
    ids = jnp.arange(devices, dtype=jnp.int32)
    first = jnp.sum((block_owners < me).astype(jnp.int32))
    count = jnp.sum((block_owners == me).astype(jnp.int32))
    owned = first + jnp.arange(owned_slots, dtype=jnp.int32)
    begun = shard_starts[None, :] <= owned[:, None]
    holder = jnp.sum(begun.astype(jnp.int32), axis=1) - 1
    slot = owned - jnp.max(jnp.where(begun, shard_starts[None, :], 0), axis=1)
    owned_kind = jnp.where(jnp.arange(owned_slots) < count, partner_kind(me, holder), -1)
    start = jnp.sum(jnp.where(ids == me, shard_starts, 0))
    end = jnp.sum(jnp.where(ids == me + 1, shard_starts, 0)) + jnp.where(me == devices - 1, total, 0)
    held = start + jnp.arange(slot_count, dtype=jnp.int32)
    blocks = jnp.arange(total, dtype=jnp.int32)
    owner = jnp.sum(jnp.where(blocks[None, :] == held[:, None], block_owners[None, :], 0), axis=1)
    held_kind = jnp.where(held < end, partner_kind(me, owner), -1)
    return (
        owned_kind.astype(jnp.int32),
        jnp.clip(slot, 0, slot_count - 1).astype(jnp.int32),
        held_kind.astype(jnp.int32),
    )


def split(value):
    high = value.astype(jnp.bfloat16)
    return high, (value - high.astype(jnp.float32)).astype(jnp.bfloat16)


def product(a, b, dims):
    return lax.dot_general(a, b, (dims, ((), ())), preferred_element_type=jnp.float32)


def product3(a, b, dims):
    left = jnp.concatenate((a[0], a[0], a[1]), axis=dims[0][0])
    right = jnp.concatenate((b[0], b[1], b[0]), axis=dims[1][0])
    return product(left, right, dims)


NN = ((1,), (0,))
NT = ((1,), (1,))


def moment_kernel(moment_ref, left_ref, right_ref, out_ref, *refs):
    left_high, left_low, right_high, right_low = refs
    flipped, right = split(left_ref[0].T), split(right_ref[0])
    half = product3(split(moment_ref[0]), right, NN)
    out_ref[0] = product3(flipped, split(half), NN)
    left_high[0], left_low[0] = flipped
    right_high[0], right_low[0] = right


def in_hbm(*values):
    return tuple(pltpu.with_memory_space_constraint(value, pltpu.HBM) for value in values)


def turn_moment(first_moment, left_basis, right_basis):
    count, width, _ = first_moment.shape
    spec = pl.BlockSpec((1, width, width), lambda j: (j, 0, 0))
    short = pltpu.HBM(first_moment.shape, jnp.bfloat16)
    return pl.pallas_call(
        moment_kernel,
        grid=(count,),
        in_specs=[spec] * 3,
        out_specs=[spec] * 5,
        out_shape=[pltpu.HBM(first_moment.shape, jnp.float32)] + [short] * 4,
        compiler_params=pltpu.CompilerParams(vmem_limit_bytes=SMALL_VMEM),
        cost_estimate=pl.CostEstimate(
            flops=12 * count * width**3, bytes_accessed=24 * count * width**2, transcendentals=0
        ),
        name="turn_moment",
    )(*in_hbm(first_moment, left_basis, right_basis))


def collect_kernel(kind_ref, slot_ref, *refs):
    sources, out_ref = refs[:5], refs[5]
    for j in range(out_ref.shape[0]):
        for kind in range(5):

            @pl.when(kind_ref[j] == kind)
            def _():
                out_ref[j] = sources[kind][slot_ref[j]]


def collect(kind, slot, sources):
    count = kind.shape[0]
    return pl.pallas_call(
        collect_kernel,
        in_specs=[pl.BlockSpec(memory_space=pltpu.SMEM)] * 2
        + [pl.BlockSpec(memory_space=pltpu.VMEM)] * 5,
        out_specs=pl.BlockSpec(memory_space=pltpu.VMEM),
        out_shape=jax.ShapeDtypeStruct((count,) + sources[0].shape[1:], sources[0].dtype),
        compiler_params=pltpu.CompilerParams(vmem_limit_bytes=SMALL_VMEM),
        name="collect",
    )(kind, slot, *sources)


def step_kernel(
    kind_ref,
    slot_ref,
    place_ref,
    mine_ref,
    other_ref,
    moment_ref,
    second_ref,
    rows_ref,
    turned_ref,
    left_high,
    left_low,
    right_high,
    right_low,
    first_out,
    second_out,
    *refs,
):
    sends, codes, grads = refs[:5], refs[5], refs[6]
    step = pl.program_id(0)
    group, half = mine_ref.shape[:2]
    here = pl.multiple_of(place_ref[0] * half, half)
    there = pl.multiple_of((1 - place_ref[0]) * half, half)
    every = range(group)
    live = [kind_ref[step * group + g] >= 0 for g in every]

    @pl.when(step == 0)
    def _():
        codes[...] = jnp.zeros_like(codes)

    for g in every:
        grads[g, pl.ds(here, half)] = mine_ref[g]
        grads[g, pl.ds(there, half)] = other_ref[g]
    right = [(right_high[g], right_low[g]) for g in every]
    first = [
        product(jnp.concatenate((grads[g],) * 2, axis=1), jnp.concatenate(right[g], axis=0), NN)
        for g in every
    ]
    for g in every:
        moment = beta_one * moment_ref[g] + (1.0 - beta_one) * grads[g].astype(jnp.float32)
        first_out[g] = jnp.where(live[g], moment, 0.0)
    turned = [product3((left_high[g], left_low[g]), split(first[g]), NN) for g in every]
    bias_one = 1.0 - beta_one**STEP
    bias_two = 1.0 - beta_two**STEP
    scaled = []
    for g in every:
        second = beta_two * second_ref[g] + (1.0 - beta_two) * turned[g] * turned[g]
        second_out[g] = jnp.where(live[g], second, 0.0)
        turned_moment = beta_one * turned_ref[g] + (1.0 - beta_one) * turned[g]
        scaled.append(
            split(
                turned_moment * (1.0 / bias_one) / (jnp.sqrt(second * (1.0 / bias_two)) + epsilon)
            )
        )
    back = [product3(split(rows_ref[g]), scaled[g], NN) for g in every]
    update = [product3(split(back[g]), right[g], NT) for g in every]
    spots = lax.broadcasted_iota(jnp.int32, codes.shape[1:], 0)
    for g in every:
        peak = jnp.max(jnp.abs(update[g]), axis=0, keepdims=True)
        code = jnp.ceil(jnp.log2(jnp.maximum(peak, 1e-30) * (1.0 / 32000.0)) * CODE_STEPS)
        coded = jnp.round(update[g] * jnp.exp2(code * (-1.0 / CODE_STEPS)))
        coded = jnp.clip(coded, -32767.0, 32767.0).astype(jnp.int32).astype(jnp.int16)
        slot = slot_ref[step * group + g]
        rows = pl.ds(pl.multiple_of(slot * half, half), half)
        for kind in range(5):

            @pl.when(kind_ref[step * group + g] == kind)
            def _():
                sends[kind][rows] = coded
                codes[kind] = jnp.where(spots == slot, code.astype(jnp.int32), codes[kind])

    @pl.when(step == pl.num_programs(0) - 1)
    def _():
        for kind in range(5):
            top = sends[kind].shape[0] - CODE_ROWS
            sends[kind][pl.ds(top, CODE_ROWS)] = codes[kind].astype(jnp.int16)


def soap_step(kind, slot, place, mine, other, moment, second, left, turned, slot_count):
    count, width, _ = moment.shape
    half = mine.shape[1]
    group = GROUP if count % GROUP == 0 else 1
    full = pl.BlockSpec((group, width, width), lambda j, *_: (j, 0, 0))
    part = pl.BlockSpec((group, half, width), lambda j, *_: (j, 0, 0))
    rows = pl.BlockSpec((group, half, width), lambda j, kinds, slots, place: (j, place[0], 0))
    send_rows = slot_count * half + CODE_ROWS
    send = pl.BlockSpec((send_rows, width), lambda j, *_: (0, 0))
    return pl.pallas_call(
        step_kernel,
        grid_spec=pltpu.PrefetchScalarGridSpec(
            num_scalar_prefetch=3,
            grid=(count // group,),
            in_specs=[part, part, full, full, rows] + [full] * 5,
            out_specs=[full, full] + [send] * 5,
            scratch_shapes=[
                pltpu.VMEM((5, CODE_ROWS, width), jnp.int32),
                pltpu.VMEM((group, width, width), jnp.bfloat16),
            ],
        ),
        out_shape=[jax.ShapeDtypeStruct(moment.shape, jnp.float32)] * 2
        + [jax.ShapeDtypeStruct((send_rows, width), jnp.int16)] * 5,
        compiler_params=pltpu.CompilerParams(vmem_limit_bytes=STEP_VMEM),
        name="soap_step",
    )(kind, slot, place, mine, other, *in_hbm(moment, second, left, *turned))


def gather_kernel(kind_ref, *refs):
    sources, out_ref = refs[:5], refs[5]
    count = kind_ref.shape[0]
    top = out_ref.shape[0] - CODE_ROWS
    half = top // count
    spots = lax.broadcasted_iota(jnp.int32, (CODE_ROWS, out_ref.shape[1]), 0)
    chosen = jnp.zeros(spots.shape, jnp.int32)
    for s in range(count):
        for kind in range(5):

            @pl.when(kind_ref[s] == kind)
            def _():
                rows = pl.ds(s * half, half)
                out_ref[rows] = sources[kind][rows]

    for kind in range(5):
        code = sources[kind][pl.ds(top, CODE_ROWS)].astype(jnp.int32)
        for s in range(count):
            chosen = jnp.where((spots == s) & (kind_ref[s] == kind), code, chosen)
    out_ref[pl.ds(top, CODE_ROWS)] = chosen.astype(jnp.int16)


def gather_held(kind, sources):
    return pl.pallas_call(
        gather_kernel,
        in_specs=[pl.BlockSpec(memory_space=pltpu.SMEM)]
        + [pl.BlockSpec(memory_space=pltpu.VMEM)] * 5,
        out_specs=pl.BlockSpec(memory_space=pltpu.VMEM),
        out_shape=jax.ShapeDtypeStruct(sources[0].shape, sources[0].dtype),
        compiler_params=pltpu.CompilerParams(vmem_limit_bytes=SMALL_VMEM),
        name="gather_held",
    )(kind, *sources)


def decode_kernel(kind_ref, place_ref, mine_ref, other_ref, out_ref, scales):
    s = pl.program_id(0)
    count = kind_ref.shape[0]
    top = mine_ref.shape[0] - CODE_ROWS
    half = top // count
    live = kind_ref[s] >= 0
    both = ((place_ref[0], mine_ref), (1 - place_ref[0], other_ref))

    @pl.when(s == 0)
    def _():
        for i, (_, coded) in enumerate(both):
            code = coded[pl.ds(top, CODE_ROWS)].astype(jnp.int32).astype(jnp.float32)
            scales[i] = jnp.exp2(code * (1.0 / CODE_STEPS))

    for i, (place, coded) in enumerate(both):
        rows = pl.ds(pl.multiple_of(s * half, half), half)
        value = coded[rows].astype(jnp.int32).astype(jnp.float32) * scales[i, pl.ds(s, 1)]
        to = pl.ds(pl.multiple_of(place * half, half), half)
        out_ref[0, to] = jnp.where(live, value, 0.0)


def decode(kind, place, mine, other, width):
    count = kind.shape[0]
    half = (mine.shape[0] - CODE_ROWS) // count
    whole = pl.BlockSpec(memory_space=pltpu.VMEM)
    return pl.pallas_call(
        decode_kernel,
        grid=(count,),
        in_specs=[pl.BlockSpec(memory_space=pltpu.SMEM)] * 2 + [whole, whole],
        out_specs=pl.BlockSpec((1, 2 * half, width), lambda s: (s, 0, 0)),
        out_shape=jax.ShapeDtypeStruct((count, 2 * half, width), jnp.float32),
        scratch_shapes=[pltpu.VMEM((2, CODE_ROWS, width), jnp.float32)],
        compiler_params=pltpu.CompilerParams(vmem_limit_bytes=SMALL_VMEM),
        name="decode",
    )(kind, place, mine, other)


def body(
    gradients, first_moment, second_moment, left_basis, right_basis, shard_starts, block_owners
):
    me = lax.axis_index("fsdp").astype(jnp.int32)
    core = lax.axis_index("dp").astype(jnp.int32)
    devices = lax.axis_size("fsdp")
    slot_count, width = gradients.shape[1], gradients.shape[3]
    owned_slots = first_moment.shape[0]
    half = width // lax.axis_size("dp")
    side, cross, flip, far = partner_pairs(devices)
    place = core.reshape(1)

    replica = gradients[0]
    twin = swap_cores(replica)

    def rows_of(value):
        return lax.dynamic_slice_in_dim(value, core * half, half, 1).astype(jnp.float32)

    summed = (rows_of(replica) + rows_of(twin)).astype(jnp.bfloat16)
    summed, shard_starts, block_owners = lax.optimization_barrier(
        (summed, shard_starts, block_owners)
    )
    own_kind, own_slot, held_kind = tables(shard_starts, block_owners, me, slot_count, owned_slots)
    by_flip = exchange(summed, flip)
    by_cross = exchange(summed, cross)
    by_far = exchange(summed, far)
    by_side = exchange(summed, side)
    turned = turn_moment(first_moment, left_basis, right_basis)
    mine = collect(own_kind, own_slot, (summed, by_side, by_cross, by_flip, by_far))
    other = swap_cores(mine)
    first_new, second_new, keep, to_side, to_cross, to_flip, to_far = soap_step(
        own_kind,
        own_slot,
        place,
        mine,
        other,
        first_moment,
        second_moment,
        left_basis,
        turned,
        slot_count,
    )
    sent = (
        keep,
        exchange(to_side, side),
        exchange(to_cross, cross),
        exchange(to_flip, flip),
        exchange(to_far, far),
    )
    coded = gather_held(held_kind, sent)
    direction = decode(held_kind, place, coded, swap_cores(coded), width)
    return (direction, first_new, second_new)


def solution(mesh):
    in_specs = (
        P("dp", "fsdp", None, None),
        P("fsdp", None, None),
        P("fsdp", None, None),
        P("fsdp", None, None),
        P("fsdp", None, None),
        P(),
        P(),
    )
    out_specs = (P("fsdp", None, None), P("fsdp", None, None), P("fsdp", None, None))
    return jax.shard_map(body, mesh=mesh, in_specs=in_specs, out_specs=out_specs, check_vma=False)
```

time: 85.8 us -> 74.1 us (0.86)
  Pallas kernels: 25.4 us -> 19.3 us
  local copies, waits for them, and re-layouts: 2.95 us -> 0.01 us
  starting transfers between devices: 18.4 us -> 16.6 us
  other arithmetic: 8.19 us -> 7.25 us
    pallas_call x3, Pallas kernels: 8.7 us -> 3.67 us  [the longest x1 2.14 us: decode(): pl.pallas_call(decode_kernel, grid=(count,), in_specs=[pl.BlockSpec(memor...]
    unnamed x26 -> x4, local copies, waits for them, and re-layouts: 2.95 us -> 0.01 us
    ppermute x8, waiting for transfers between devices: 26.9 us -> 25.1 us  [exchange(): return lax.ppermute(value, 'fsdp', pairs + [(b, a) for a, b in pairs])]
    ppermute x8, starting transfers between devices: 17.7 us -> 15.9 us  [exchange(): return lax.ppermute(value, 'fsdp', pairs + [(b, a) for a, b in pairs])]
    pallas_call x1, Pallas kernels: 9.77 us -> 8.18 us  [soap_step(): pl.pallas_call(step_kernel, grid_spec=pltpu.PrefetchScalarGridSpec(num_sc...]
    ppermute x3, waiting for transfers between devices: 1.75 us -> 3.28 us  [swap_cores(): return lax.ppermute(value, 'dp', [(0, 1), (1, 0)])]
  transfers between devices with their start and end apart: 11 -> 11, of which waited for: 4 -> 6; matrix products, arithmetic and copies ran while one was open for 8% -> 9% of each run, Pallas kernels for 8% -> 10%
where the time goes in v2:
time: 74.1 us; the launch traced here: 73 us
  waiting for transfers between devices  28.4 us (38%)
  Pallas kernels  19.3 us (26%)
  starting transfers between devices  16.6 us (22%)
  other arithmetic  7.25 us (10%)
  between operations  1.41 us (2%)
    ppermute x8, waiting for transfers between devices, exchange(): return lax.ppermute(value, 'fsdp', pairs + [(b, a) for a, b in pairs])  25.1 us
    ppermute x8, starting transfers between devices, exchange(): return lax.ppermute(value, 'fsdp', pairs + [(b, a) for a, b in pairs])  15.9 us
    pallas_call x1, Pallas kernels, soap_step(): pl.pallas_call(step_kernel, grid_spec=pltpu.PrefetchScalarGridSpec(num_sc...  8.18 us
    pallas_call x1, Pallas kernels, turn_moment(): pl.pallas_call(moment_kernel, grid=(count,), in_specs=[spec] * 3, out_spe...  7.41 us
    ppermute x3, waiting for transfers between devices, swap_cores(): return lax.ppermute(value, 'dp', [(0, 1), (1, 0)])  3.28 us
    pallas_call x1, Pallas kernels, decode(): pl.pallas_call(decode_kernel, grid=(count,), in_specs=[pl.BlockSpec(memor...  2.14 us
  transfers between devices with their start and end apart: 11, of which 6 were waited for; matrix products, arithmetic and copies ran while one was open for 9% of the time, Pallas kernels for 10%

profile of v2, /device:TPU:0, one launch (start us, length us, event | category | flops | bytes accessed | tf_op | source)
XLA Modules:
  0.0 73.0 jit_solution(1576635587398449482)
XLA Ops:
  0.6 0.6 collective-permute-start
  1.2 1.7 %collective-permute-done = bf16[4,256,256]{2,1,0:T(8,128)(2,1)S(1)} collective-permute-done((bf16[4,256,256]{2,1,0:T(8,128)(2,1)}, bf16[4,256,256]{2,1,0:T(8,128)(2,1)S(1)}, u32[]{:S(2)}, u32[]{:S(2)}) %collective-permute-start) | collective-permute-done | bytes 524320 | tf_op jit(solution)/shard_map/ppermute | solution.py:36
  2.9 1.0 %fusion.refs_0_ = bf16[4,128,256]{2,1,0:T(8,128)(2,1)S(1)} fusion(bf16[4,256,256]{2,1,0:T(8,128)(2,1)S(1)} %collective-permute-done, s32[]{:T(128)S(6)} %select_n.61, bf16[1,4,256,256]{3,2,1,0:T(8,128)(2,1)} %param.7), kind=kLoop, calls=%fused_computation.1 | loop fusion | flops 524288 | bytes 786436 | tf_op jit(solution)/shard_map/convert_element_type | solution.py:338
  4.0 0.7 collective-permute-start.4
  4.6 5.7 %collective-permute-start.3 = (bf16[4,128,256]{2,1,0:T(8,128)(2,1)S(1)}, bf16[4,128,256]{2,1,0:T(8,128)(2,1)S(1)}, u32[]{:S(2)}, u32[]{:S(2)}) collective-permute-start(bf16[4,128,256]{2,1,0:T(8,128)(2,1)S(1)} %fusion.refs_0_), channel_id=1, source_target_pairs={{0,4},{2,6},{8,12},{10,14},{16,20},{18,22},{24,28},{26,30},{4,0},{... | collective-permute-start | bytes 786440 | tf_op jit(solution)/shard_map/ppermute | solution.py:24
  10.3 0.7 collective-permute-start.2
  11.0 2.8 %collective-permute-start.1 = (bf16[4,128,256]{2,1,0:T(8,128)(2,1)S(1)}, bf16[4,128,256]{2,1,0:T(8,128)(2,1)S(1)}, u32[]{:S(2)}, u32[]{:S(2)}) collective-permute-start(bf16[4,128,256]{2,1,0:T(8,128)(2,1)S(1)} %fusion.refs_0_), channel_id=1, source_target_pairs={{0,2},{4,6},{8,10},{12,14},{16,18},{20,22},{24,26},{28,30},{2,0},{... | collective-permute-start | bytes 786440 | tf_op jit(solution)/shard_map/ppermute | solution.py:24
  13.8 1.3 %fusion.5 = (s32[]{:T(128)}, s32[]{:T(128)}) fusion(s32[48]{0:T(128)} %param.13, s32[]{:T(128)S(6)} %axis_index.23), kind=kLoop, calls=%fused_computation.24 | loop fusion | flops 286 | bytes 204 | tf_op jit(solution)/shard_map/reduce_sum | solution.py:51
  15.1 0.6 iota_add_fusion
  15.8 0.9 %fusion.2 = (s32[6]{0:T(128)S(1)}, s32[6]{0:T(128)S(1)}) fusion(s32[16]{0:T(128)} %param.12, s32[6]{0:T(128)S(1)} %iota_add_fusion), kind=kLoop, calls=%fused_computation.5 | loop fusion | flops 468 | bytes 136 | tf_op jit(solution)/shard_map/reduce_max | solution.py:55
  16.6 1.3 %compare_select_fusion.5 = (s32[6]{0:T(128)S(1)}, s32[6]{0:T(128)S(1)}) fusion(s32[6]{0:T(128)S(1)} %get-tuple-element.34, s32[]{:T(128)S(6)} %xor.9, s32[]{:T(128)S(6)} %xor.8, s32[]{:T(128)S(6)} %axis_index.23, s32[]{:T(128)} %get-tuple-element.35, s32[6]{0:T(128)S(1)} %get-tuple-element.33, s32[]{:T(128)} %get-tuple-element.36), kind=kLoop, calls=%fused_computation.13 | loop fusion | flops 96 | bytes 116 | tf_op jit(solution)/shard_map/jit(_where)/select_n | solution.py:56
  17.9 8.8 %collective-permute-done.3.refs_3_ = bf16[4,128,256]{2,1,0:T(8,128)(2,1)S(1)} collective-permute-done((bf16[4,128,256]{2,1,0:T(8,128)(2,1)S(1)}, bf16[4,128,256]{2,1,0:T(8,128)(2,1)S(1)}, u32[]{:S(2)}, u32[]{:S(2)}) %collective-permute-start.3) | collective-permute-done | bytes 262176 | tf_op jit(solution)/shard_map/ppermute | solution.py:24
  26.7 1.1 %collective-permute-done.1.refs_1_ = bf16[4,128,256]{2,1,0:T(8,128)(2,1)S(1)} collective-permute-done((bf16[4,128,256]{2,1,0:T(8,128)(2,1)S(1)}, bf16[4,128,256]{2,1,0:T(8,128)(2,1)S(1)}, u32[]{:S(2)}, u32[]{:S(2)}) %collective-permute-start.1) | collective-permute-done | bytes 262176 | tf_op jit(solution)/shard_map/ppermute | solution.py:24
  27.8 0.8 %collect.1.mine_ref = bf16[6,128,256]{2,1,0:T(8,128)(2,1)S(1)} custom-call(s32[6]{0:T(128)S(1)} %get-tuple-element.39.kind_ref, s32[6]{0:T(128)S(1)} %get-tuple-element.40.slot_ref, bf16[4,128,256]{2,1,0:T(8,128)(2,1)S(1)} %fusion.refs_0_, bf16[4,128,256]{2,1,0:T(8,128)(2,1)S(1)} %collective-permute-done.1.refs_1_, ...), custom_call_target="tpu_custom_call" | custom-call | tf_op jit(solution)/shard_map/collect/pallas_call | solution.py:132
  28.6 0.1 collective-permute-start.5
  28.7 0.0 copy-start
  28.7 7.4 %turn_moment.1 = (f32[6,256,256]{2,1,0:T(8,128)}, bf16[6,256,256]{2,1,0:T(8,128)(2,1)}, bf16[6,256,256]{2,1,0:T(8,128)(2,1)}, bf16[6,256,256]{2,1,0:T(8,128)(2,1)}, bf16[6,256,256]{2,1,0:T(8,128)(2,1)}) custom-call(f32[6,256,256]{2,1,0:T(8,128)} %moment_ref.3, f32[6,256,256]{2,1,0:T(8,128)} %rows_ref.1, f32[6,256,256]{2,1,0:T(8,128)} %right_ref.1), custom_call_target="tpu_custom_call" | custom-call | flops 1207959552 | bytes 9437184 | tf_op jit(solution)/shard_map/turn_moment/pallas_call | solution.py:106
  36.1 0.7 fusion.4
  36.8 0.6 iota_add_fusion.1
  37.5 8.2 %soap_step.1 = (f32[6,256,256]{2,1,0:T(8,128)}, f32[6,256,256]{2,1,0:T(8,128)}, s16[528,256]{1,0:T(8,128)(2,1)S(1)}, s16[528,256]{1,0:T(8,128)(2,1)S(1)}, s16[52...) custom-call(s32[6]{0:T(128)S(1)} %get-tuple-element.39.kind_ref, ...), custom_call_target="tpu_custom_call" | custom-call | tf_op jit(solution)/shard_map/soap_step/pallas_call | solution.py:230
  45.6 0.4 collective-permute-start.6
  46.1 0.7 collective-permute-start.7
  46.7 4.3 %collective-permute-start.8 = (s16[528,256]{1,0:T(8,128)(2,1)S(1)}, s16[528,256]{1,0:T(8,128)(2,1)S(1)}, u32[]{:S(2)}, u32[]{:S(2)}) collective-permute-start(s16[528,256]{1,0:T(8,128)(2,1)S(1)} %get-tuple-element.29), channel_id=1, source_target_pairs={{0,4},{2,6},{8,12},{10,14},{16,20},{18,22},{24,28},{26,30},{4,0},{... | collective-permute-start | bytes 811016 | tf_op jit(solution)/shard_map/ppermute | solution.py:24
  51.1 0.7 collective-permute-start.9
  51.8 0.2 select_reduce_fusion
  52.6 0.6 compare_select_fusion.10.kind_ref
  53.2 4.1 %collective-permute-done.6.refs_1_ = s16[528,256]{1,0:T(8,128)(2,1)S(1)} collective-permute-done((s16[528,256]{1,0:T(8,128)(2,1)S(1)}, s16[528,256]{1,0:T(8,128)(2,1)S(1)}, u32[]{:S(2)}, u32[]{:S(2)}) %collective-permute-start.6) | collective-permute-done | bytes 270368 | tf_op jit(solution)/shard_map/ppermute | solution.py:24
  57.3 11.2 %collective-permute-done.8.refs_3_ = s16[528,256]{1,0:T(8,128)(2,1)S(1)} collective-permute-done((s16[528,256]{1,0:T(8,128)(2,1)S(1)}, s16[528,256]{1,0:T(8,128)(2,1)S(1)}, u32[]{:S(2)}, u32[]{:S(2)}) %collective-permute-start.8) | collective-permute-done | bytes 270368 | tf_op jit(solution)/shard_map/ppermute | solution.py:24
  68.5 0.7 gather_held.1.mine_ref
  69.2 0.1 collective-permute-start.10
  69.3 1.5 %collective-permute-done.10.other_ref = s16[528,256]{1,0:T(8,128)(2,1)S(1)} collective-permute-done((s16[528,256]{1,0:T(8,128)(2,1)S(1)}, s16[528,256]{1,0:T(8,128)(2,1)S(1)}, u32[]{:S(2)}, u32[]{:S(2)}) %collective-permute-start.10) | collective-permute-done | bytes 270368 | tf_op jit(solution)/shard_map/ppermute | solution.py:36
  70.8 2.1 %decode.1 = f32[4,256,256]{2,1,0:T(8,128)} custom-call(s32[4]{0:T(128)S(1)} %compare_select_fusion.10.kind_ref, s32[1]{0:T(128)} %bitcast.2.place_ref, s16[528,256]{1,0:T(8,128)(2,1)S(1)} %gather_held.1.mine_ref, s16[528,256]{1,0:T(8,128)(2,1)S(1)} %collective-permute-done.10.other_ref), custom_call_target="tpu_custom_call" | custom-call | tf_op jit(solution)/shard_map/decode/pallas_call | solution.py:308
  (8 shorter events, 0.0 us)
Async XLA Ops:
  0.6 2.3 %collective-permute-start = (bf16[4,256,256]{2,1,0:T(8,128)(2,1)}, bf16[4,256,256]{2,1,0:T(8,128)(2,1)S(1)}, u32[]{:S(2)}, u32[]{:S(2)}) collective-permute-start(bf16[4,256,256]{2,1,0:T(8,128)(2,1)} %bitcast.5), channel_id=1, source_target_pairs={{0,1},{1,0},{2,3},{3,2},{4,5},{5,4},{6,7},{7,6},{8,9},{9,8},{10,11... | collective-permute-start | bytes 1572872 | tf_op jit(solution)/shard_map/ppermute | solution.py:36
  4.0 14.0 %collective-permute-start.4 = (bf16[4,128,256]{2,1,0:T(8,128)(2,1)S(1)}, bf16[4,128,256]{2,1,0:T(8,128)(2,1)S(1)}, u32[]{:S(2)}, u32[]{:S(2)}) collective-permute-start(bf16[4,128,256]{2,1,0:T(8,128)(2,1)S(1)} %fusion.refs_0_), channel_id=1, source_target_pairs={{4,8},{6,10},{12,16},{14,18},{20,24},{22,26},{8,4},{10,6},{16,12},... | collective-permute-start | bytes 786440 | tf_op jit(solution)/shard_map/ppermute | solution.py:24
  4.6 22.1 %collective-permute-start.3 = (bf16[4,128,256]{2,1,0:T(8,128)(2,1)S(1)}, bf16[4,128,256]{2,1,0:T(8,128)(2,1)S(1)}, u32[]{:S(2)}, u32[]{:S(2)}) collective-permute-start(bf16[4,128,256]{2,1,0:T(8,128)(2,1)S(1)} %fusion.refs_0_), channel_id=1, source_target_pairs={{0,4},{2,6},{8,12},{10,14},{16,20},{18,22},{24,28},{26,30},{4,0},{... | collective-permute-start | bytes 786440 | tf_op jit(solution)/shard_map/ppermute | solution.py:24
  10.3 16.4 %collective-permute-start.2 = (bf16[4,128,256]{2,1,0:T(8,128)(2,1)S(1)}, bf16[4,128,256]{2,1,0:T(8,128)(2,1)S(1)}, u32[]{:S(2)}, u32[]{:S(2)}) collective-permute-start(bf16[4,128,256]{2,1,0:T(8,128)(2,1)S(1)} %fusion.refs_0_), channel_id=1, source_target_pairs={{2,4},{6,8},{10,12},{14,16},{18,20},{22,24},{26,28},{4,2},{8,6},{1... | collective-permute-start | bytes 786440 | tf_op jit(solution)/shard_map/ppermute | solution.py:24
  11.0 16.8 %collective-permute-start.1 = (bf16[4,128,256]{2,1,0:T(8,128)(2,1)S(1)}, bf16[4,128,256]{2,1,0:T(8,128)(2,1)S(1)}, u32[]{:S(2)}, u32[]{:S(2)}) collective-permute-start(bf16[4,128,256]{2,1,0:T(8,128)(2,1)S(1)} %fusion.refs_0_), channel_id=1, source_target_pairs={{0,2},{4,6},{8,10},{12,14},{16,18},{20,22},{24,26},{28,30},{2,0},{... | collective-permute-start | bytes 786440 | tf_op jit(solution)/shard_map/ppermute | solution.py:24
  28.6 8.8 %collective-permute-start.5 = (bf16[6,128,256]{2,1,0:T(8,128)(2,1)S(1)}, bf16[6,128,256]{2,1,0:T(8,128)(2,1)S(1)}, u32[]{:S(2)}, u32[]{:S(2)}) collective-permute-start(bf16[6,128,256]{2,1,0:T(8,128)(2,1)S(1)} %collect.1.mine_ref), channel_id=1, source_target_pairs={{0,1},{1,0},{2,3},{3,2},{4,5},{5,4},{6,7},{7,6},{8,9},{9,8},{10,11... | collective-permute-start | bytes 1179656 | tf_op jit(solution)/shard_map/ppermute | solution.py:36
  28.7 7.4 %copy-start = (s32[16]{0:T(128)S(1)}, s32[16]{0:T(128)}, u32[]{:S(2)}) copy-start(s32[16]{0:T(128)} %param.12) | copy-start | bytes 196
  37.4 14.3 %copy-start.1 = (s32[48]{0:T(128)S(1)}, s32[48]{0:T(128)}, u32[]{:S(2)}) copy-start(s32[48]{0:T(128)} %param.13) | copy-start | bytes 580
  45.6 11.6 %collective-permute-start.6 = (s16[528,256]{1,0:T(8,128)(2,1)S(1)}, s16[528,256]{1,0:T(8,128)(2,1)S(1)}, u32[]{:S(2)}, u32[]{:S(2)}) collective-permute-start(s16[528,256]{1,0:T(8,128)(2,1)S(1)} %get-tuple-element.27), channel_id=1, source_target_pairs={{0,2},{4,6},{8,10},{12,14},{16,18},{20,22},{24,26},{28,30},{2,0},{... | collective-permute-start | bytes 811016 | tf_op jit(solution)/shard_map/ppermute | solution.py:24
  46.1 11.2 %collective-permute-start.7 = (s16[528,256]{1,0:T(8,128)(2,1)S(1)}, s16[528,256]{1,0:T(8,128)(2,1)S(1)}, u32[]{:S(2)}, u32[]{:S(2)}) collective-permute-start(s16[528,256]{1,0:T(8,128)(2,1)S(1)} %get-tuple-element.28), channel_id=1, source_target_pairs={{2,4},{6,8},{10,12},{14,16},{18,20},{22,24},{26,28},{4,2},{8,6},{1... | collective-permute-start | bytes 811016 | tf_op jit(solution)/shard_map/ppermute | solution.py:24
  46.7 21.7 %collective-permute-start.8 = (s16[528,256]{1,0:T(8,128)(2,1)S(1)}, s16[528,256]{1,0:T(8,128)(2,1)S(1)}, u32[]{:S(2)}, u32[]{:S(2)}) collective-permute-start(s16[528,256]{1,0:T(8,128)(2,1)S(1)} %get-tuple-element.29), channel_id=1, source_target_pairs={{0,4},{2,6},{8,12},{10,14},{16,20},{18,22},{24,28},{26,30},{4,0},{... | collective-permute-start | bytes 811016 | tf_op jit(solution)/shard_map/ppermute | solution.py:24
  51.1 17.4 %collective-permute-start.9 = (s16[528,256]{1,0:T(8,128)(2,1)S(1)}, s16[528,256]{1,0:T(8,128)(2,1)S(1)}, u32[]{:S(2)}, u32[]{:S(2)}) collective-permute-start(s16[528,256]{1,0:T(8,128)(2,1)S(1)} %get-tuple-element.30), channel_id=1, source_target_pairs={{4,8},{6,10},{12,16},{14,18},{20,24},{22,26},{8,4},{10,6},{16,12},... | collective-permute-start | bytes 811016 | tf_op jit(solution)/shard_map/ppermute | solution.py:24
  69.2 1.6 %collective-permute-start.10 = (s16[528,256]{1,0:T(8,128)(2,1)S(1)}, s16[528,256]{1,0:T(8,128)(2,1)S(1)}, u32[]{:S(2)}, u32[]{:S(2)}) collective-permute-start(s16[528,256]{1,0:T(8,128)(2,1)S(1)} %gather_held.1.mine_ref), channel_id=1, source_target_pairs={{0,1},{1,0},{2,3},{3,2},{4,5},{5,4},{6,7},{7,6},{8,9},{9,8},{10,11... | collective-permute-start | bytes 811016 | tf_op jit(solution)/shard_map/ppermute | solution.py:36

commit v3 on v2

v3 whole, which is shorter than its diff:
```python
import jax
import jax.numpy as jnp
from jax import lax
from jax.experimental import pallas as pl
from jax.experimental.pallas import tpu as pltpu
from jax.sharding import PartitionSpec as P


REACH = 2
STEP = 10
CODE_ROWS = 16
CODE_STEPS = 128.0
PREPARE_GROUP = 3
GROUP = 3
SMALL_VMEM = 12 * 2**20
STEP_VMEM = 28 * 2**20

beta_one = 0.9
beta_two = 0.95
epsilon = 1e-08
bias_one = 1.0 - beta_one**STEP
bias_two = 1.0 - beta_two**STEP

HERE, SIDE, CROSS, FLIP, FAR = range(5)


def exchange(value, pairs):
    return lax.ppermute(value, "fsdp", pairs + [(b, a) for a, b in pairs])


def partner_pairs(devices):
    side = [(i, i + 1) for i in range(0, devices - 1, 2)]
    cross = [(i, i + 1) for i in range(1, devices - 1, 2)]
    flip = [(i, i + 2) for i in range(devices - 2) if not i & 2]
    far = [(i, i + 2) for i in range(devices - 2) if i & 2]
    return (side, cross, flip, far)


def swap_cores(value):
    return lax.ppermute(value, "dp", [(0, 1), (1, 0)])


def partner_kind(me, other):
    step = jnp.abs(other - me)
    near = jnp.where(other == me ^ 1, SIDE, CROSS)
    distant = jnp.where(other == me ^ 2, FLIP, FAR)
    return jnp.where(step == 0, HERE, jnp.where(step == 1, near, distant))


def in_hbm(*values):
    return tuple(pltpu.with_memory_space_constraint(value, pltpu.HBM) for value in values)


def in_vmem(*values):
    return tuple(pltpu.with_memory_space_constraint(value, pltpu.VMEM) for value in values)


def tables_kernel(me_ref, starts_ref, owners_ref, owned_kind, owned_slot, held_kind):
    me = me_ref[0]
    devices, total = starts_ref.shape[0], owners_ref.shape[0]

    def tally(b, sums):
        owner = owners_ref[b]
        return sums[0] + (owner < me).astype(jnp.int32), sums[1] + (owner == me).astype(jnp.int32)

    zero = jnp.int32(0)
    first, count = lax.fori_loop(0, total, tally, (zero, zero))
    near = [me + step for step in range(-REACH, REACH + 1)]
    begins = [starts_ref[jnp.clip(device, 0, devices - 1)] for device in near]
    for j in range(owned_kind.shape[0]):
        holder, start = near[0], begins[0]
        for device, begin in zip(near, begins):
            reached = (device >= 0) & (device < devices) & (begin <= first + j)
            holder = jnp.where(reached, device, holder)
            start = jnp.where(reached, begin, start)
        owned_kind[j] = jnp.where(j < count, partner_kind(me, holder), -1)
        owned_slot[j] = jnp.clip(first + j - start, 0, held_kind.shape[0] - 1)
    start = starts_ref[me]
    end = jnp.where(me + 1 < devices, starts_ref[jnp.minimum(me + 1, devices - 1)], total)
    for s in range(held_kind.shape[0]):
        owner = owners_ref[jnp.minimum(start + s, total - 1)]
        held_kind[s] = jnp.where(start + s < end, partner_kind(me, owner), -1)


def tables(shard_starts, block_owners, me, slot_count, owned_slots):
    owned = jax.ShapeDtypeStruct((owned_slots,), jnp.int32)
    return pl.pallas_call(
        tables_kernel,
        in_specs=[pl.BlockSpec(memory_space=pltpu.SMEM)] * 3,
        out_specs=[pl.BlockSpec(memory_space=pltpu.SMEM)] * 3,
        out_shape=[owned, owned, jax.ShapeDtypeStruct((slot_count,), jnp.int32)],
        compiler_params=pltpu.CompilerParams(vmem_limit_bytes=SMALL_VMEM),
        name="tables",
    )(me.reshape(1), *in_hbm(shard_starts, block_owners))


def split(value):
    high = value.astype(jnp.bfloat16)
    return high, (value - high.astype(jnp.float32)).astype(jnp.bfloat16)


def product(a, b, dims):
    return lax.dot_general(a, b, (dims, ((), ())), preferred_element_type=jnp.float32)


def product3(a, b, dims):
    left = jnp.concatenate((a[0], a[0], a[1]), axis=dims[0][0])
    right = jnp.concatenate((b[0], b[1], b[0]), axis=dims[1][0])
    return product(left, right, dims)


NN = ((1,), (0,))
NT = ((1,), (1,))


def prepare_kernel(place_ref, moment_ref, second_ref, left_ref, right_ref, *outs):
    turned_out, second_out, flip_high, flip_low, right_high, right_low, row_high, row_low = outs
    every = range(moment_ref.shape[0])
    half = row_high.shape[1]
    here = pl.multiple_of(place_ref[0] * half, half)
    right = [split(right_ref[g]) for g in every]
    first = [product3(split(moment_ref[g]), right[g], NN) for g in every]
    flipped = [split(left_ref[g].T) for g in every]
    turned = [product3(flipped[g], split(first[g]), NN) for g in every]
    for g in every:
        turned_out[g] = turned[g] * (beta_one / bias_one)
        second_out[g] = second_ref[g] * beta_two
        flip_high[g], flip_low[g] = flipped[g]
        right_high[g], right_low[g] = right[g]
        row_high[g], row_low[g] = split(left_ref[g, pl.ds(here, half)])


def prepare(place, first_moment, second_moment, left_basis, right_basis, half):
    count, width, _ = first_moment.shape
    group = PREPARE_GROUP if count % PREPARE_GROUP == 0 else 1
    spec = pl.BlockSpec((group, width, width), lambda j: (j, 0, 0))
    part = pl.BlockSpec((group, half, width), lambda j: (j, 0, 0))
    full = pltpu.VMEM(first_moment.shape, jnp.float32)
    short = pltpu.VMEM(first_moment.shape, jnp.bfloat16)
    rows = pltpu.VMEM((count, half, width), jnp.bfloat16)
    return pl.pallas_call(
        prepare_kernel,
        grid=(count // group,),
        in_specs=[pl.BlockSpec(memory_space=pltpu.SMEM)] + [spec] * 4,
        out_specs=[spec] * 6 + [part] * 2,
        out_shape=[full] * 2 + [short] * 4 + [rows] * 2,
        compiler_params=pltpu.CompilerParams(vmem_limit_bytes=STEP_VMEM),
        cost_estimate=pl.CostEstimate(
            flops=12 * count * width**3, bytes_accessed=16 * count * width**2, transcendentals=0
        ),
        name="prepare",
    )(place, *in_hbm(first_moment, second_moment, left_basis, right_basis))


def load_kernel(place_ref, source_ref, out_ref):
    out_ref[...] = source_ref[...]


def load_rows(place, source, half):
    count, _, width = source.shape
    return pl.pallas_call(
        load_kernel,
        grid_spec=pltpu.PrefetchScalarGridSpec(
            num_scalar_prefetch=1,
            grid=(1,),
            in_specs=[pl.BlockSpec((count, half, width), lambda _, place: (0, place[0], 0))],
            out_specs=pl.BlockSpec((count, half, width), lambda _, place: (0, 0, 0)),
        ),
        out_shape=pltpu.VMEM((count, half, width), source.dtype),
        compiler_params=pltpu.CompilerParams(vmem_limit_bytes=SMALL_VMEM),
        name="load_rows",
    )(place, *in_hbm(source))


def add_kernel(place_ref, mine_ref, other_ref, out_ref):
    half = out_ref.shape[1]
    rows = pl.ds(pl.multiple_of(place_ref[0] * half, half), half)
    for s in range(out_ref.shape[0]):
        total = mine_ref[s].astype(jnp.float32) + other_ref[s, rows].astype(jnp.float32)
        out_ref[s] = total.astype(out_ref.dtype)


def add_replicas(place, mine, other):
    return pl.pallas_call(
        add_kernel,
        in_specs=[pl.BlockSpec(memory_space=pltpu.SMEM)]
        + [pl.BlockSpec(memory_space=pltpu.VMEM)] * 2,
        out_specs=pl.BlockSpec(memory_space=pltpu.VMEM),
        out_shape=pltpu.VMEM(mine.shape, mine.dtype),
        compiler_params=pltpu.CompilerParams(vmem_limit_bytes=SMALL_VMEM),
        name="add_replicas",
    )(place, *in_vmem(mine, other))


def collect_kernel(kind_ref, slot_ref, *refs):
    sources, out_ref = refs[:5], refs[5]
    for j in range(out_ref.shape[0]):
        for kind in range(5):

            @pl.when(kind_ref[j] == kind)
            def _():
                out_ref[j] = sources[kind][slot_ref[j]]


def collect(kind, slot, sources):
    count = kind.shape[0]
    return pl.pallas_call(
        collect_kernel,
        in_specs=[pl.BlockSpec(memory_space=pltpu.SMEM)] * 2
        + [pl.BlockSpec(memory_space=pltpu.VMEM)] * 5,
        out_specs=pl.BlockSpec(memory_space=pltpu.VMEM),
        out_shape=jax.ShapeDtypeStruct((count,) + sources[0].shape[1:], sources[0].dtype),
        compiler_params=pltpu.CompilerParams(vmem_limit_bytes=SMALL_VMEM),
        name="collect",
    )(kind, slot, *sources)


def step_kernel(kind_ref, slot_ref, place_ref, mine_ref, other_ref, *refs):
    turned_ref, second_ref, flip_high, flip_low, right_high, right_low, row_high, row_low = refs[:8]
    second_out, sends, codes, grads = refs[8], refs[9:14], refs[14], refs[15]
    step = pl.program_id(0)
    group, half = mine_ref.shape[:2]
    here = pl.multiple_of(place_ref[0] * half, half)
    there = pl.multiple_of((1 - place_ref[0]) * half, half)
    every = range(group)

    @pl.when(step == 0)
    def _():
        codes[...] = jnp.zeros_like(codes)

    for g in every:
        grads[g, pl.ds(here, half)] = mine_ref[g]
        grads[g, pl.ds(there, half)] = other_ref[g]
    right = [(right_high[g], right_low[g]) for g in every]
    first = [
        product(jnp.concatenate((grads[g],) * 2, axis=1), jnp.concatenate(right[g], axis=0), NN)
        for g in every
    ]
    turned = [product3((flip_high[g], flip_low[g]), split(first[g]), NN) for g in every]
    scaled = []
    for g in every:
        second = second_ref[g] + (1.0 - beta_two) * turned[g] * turned[g]
        second_out[g] = second
        unbiased = second * (1.0 / bias_two)
        root = unbiased * lax.rsqrt(unbiased)
        moment = turned_ref[g] + ((1.0 - beta_one) / bias_one) * turned[g]
        scaled.append(split(moment / (root + epsilon)))
    back = [product3((row_high[g], row_low[g]), scaled[g], NN) for g in every]
    update = [product3(split(back[g]), right[g], NT) for g in every]
    spots = lax.broadcasted_iota(jnp.int32, codes.shape[1:], 0)
    for g in every:
        peak = jnp.max(jnp.abs(update[g]), axis=0, keepdims=True)
        code = jnp.ceil(jnp.log2(jnp.maximum(peak, 1e-30) * (1.0 / 32000.0)) * CODE_STEPS)
        coded = jnp.round(update[g] * jnp.exp2(code * (-1.0 / CODE_STEPS)))
        coded = jnp.clip(coded, -32767.0, 32767.0).astype(jnp.int32).astype(jnp.int16)
        slot = slot_ref[step * group + g]
        rows = pl.ds(pl.multiple_of(slot * half, half), half)
        for kind in range(5):

            @pl.when(kind_ref[step * group + g] == kind)
            def _():
                sends[kind][rows] = coded
                codes[kind] = jnp.where(spots == slot, code.astype(jnp.int32), codes[kind])

    @pl.when(step == pl.num_programs(0) - 1)
    def _():
        for kind in range(5):
            top = sends[kind].shape[0] - CODE_ROWS
            sends[kind][pl.ds(top, CODE_ROWS)] = codes[kind].astype(jnp.int16)


def soap_step(kind, slot, place, mine, other, prepared, slot_count):
    count, half, width = mine.shape
    group = GROUP if count % GROUP == 0 else 1
    full = pl.BlockSpec((group, width, width), lambda j, *_: (j, 0, 0))
    part = pl.BlockSpec((group, half, width), lambda j, *_: (j, 0, 0))
    send_rows = slot_count * half + CODE_ROWS
    send = pl.BlockSpec((send_rows, width), lambda j, *_: (0, 0))
    return pl.pallas_call(
        step_kernel,
        grid_spec=pltpu.PrefetchScalarGridSpec(
            num_scalar_prefetch=3,
            grid=(count // group,),
            in_specs=[part, part] + [full] * 6 + [part] * 2,
            out_specs=[full] + [send] * 5,
            scratch_shapes=[
                pltpu.VMEM((5, CODE_ROWS, width), jnp.int32),
                pltpu.VMEM((group, width, width), jnp.bfloat16),
            ],
        ),
        out_shape=[pltpu.VMEM((count, width, width), jnp.float32)]
        + [pltpu.VMEM((send_rows, width), jnp.int16)] * 5,
        compiler_params=pltpu.CompilerParams(vmem_limit_bytes=STEP_VMEM),
        name="soap_step",
    )(kind, slot, place, *in_vmem(mine, other, *prepared))


def finish_kernel(kind_ref, place_ref, mine_ref, other_ref, moment_ref, second_ref, *outs):
    first_out, second_out = outs
    j = pl.program_id(0)
    half = mine_ref.shape[1]
    live = kind_ref[j] >= 0
    for place, part in ((place_ref[0], mine_ref), (1 - place_ref[0], other_ref)):
        rows = pl.ds(pl.multiple_of(place * half, half), half)
        gradient = part[0].astype(jnp.float32)
        moment = beta_one * moment_ref[0, rows] + (1.0 - beta_one) * gradient
        first_out[0, rows] = jnp.where(live, moment, 0.0)
    second_out[0] = jnp.where(live, second_ref[0], 0.0)


def finish(kind, place, mine, other, first_moment, second):
    count, width, _ = first_moment.shape
    half = mine.shape[1]
    full = pl.BlockSpec((1, width, width), lambda j: (j, 0, 0))
    part = pl.BlockSpec((1, half, width), lambda j: (j, 0, 0))
    return pl.pallas_call(
        finish_kernel,
        grid=(count,),
        in_specs=[pl.BlockSpec(memory_space=pltpu.SMEM)] * 2 + [part, part, full, full],
        out_specs=[full] * 2,
        out_shape=[pltpu.HBM(first_moment.shape, jnp.float32)] * 2,
        compiler_params=pltpu.CompilerParams(vmem_limit_bytes=SMALL_VMEM),
        cost_estimate=pl.CostEstimate(
            flops=12 * count * width**2, bytes_accessed=12 * count * width**2, transcendentals=0
        ),
        name="finish",
    )(kind, place, *in_vmem(mine, other), *in_hbm(first_moment), *in_vmem(second))


def gather_kernel(kind_ref, *refs):
    sources, out_ref = refs[:5], refs[5]
    count = kind_ref.shape[0]
    top = out_ref.shape[0] - CODE_ROWS
    half = top // count
    spots = lax.broadcasted_iota(jnp.int32, (CODE_ROWS, out_ref.shape[1]), 0)
    chosen = jnp.zeros(spots.shape, jnp.int32)
    for s in range(count):
        for kind in range(5):

            @pl.when(kind_ref[s] == kind)
            def _():
                rows = pl.ds(s * half, half)
                out_ref[rows] = sources[kind][rows]

    for kind in range(5):
        code = sources[kind][pl.ds(top, CODE_ROWS)].astype(jnp.int32)
        for s in range(count):
            chosen = jnp.where((spots == s) & (kind_ref[s] == kind), code, chosen)
    out_ref[pl.ds(top, CODE_ROWS)] = chosen.astype(jnp.int16)


def gather_held(kind, sources):
    return pl.pallas_call(
        gather_kernel,
        in_specs=[pl.BlockSpec(memory_space=pltpu.SMEM)]
        + [pl.BlockSpec(memory_space=pltpu.VMEM)] * 5,
        out_specs=pl.BlockSpec(memory_space=pltpu.VMEM),
        out_shape=jax.ShapeDtypeStruct(sources[0].shape, sources[0].dtype),
        compiler_params=pltpu.CompilerParams(vmem_limit_bytes=SMALL_VMEM),
        name="gather_held",
    )(kind, *sources)


def decode_kernel(kind_ref, place_ref, mine_ref, other_ref, out_ref, values, sems):
    count = values.shape[0]
    top = mine_ref.shape[0] - CODE_ROWS
    half = top // count
    both = ((place_ref[0], mine_ref), (1 - place_ref[0], other_ref))
    scales = []
    for _, coded in both:
        code = coded[pl.ds(top, CODE_ROWS)].astype(jnp.int32).astype(jnp.float32)
        scales.append(jnp.exp2(code * (1.0 / CODE_STEPS)))
    copies = []
    for s in range(count):
        for (place, coded), scale in zip(both, scales):
            value = coded[pl.ds(s * half, half)].astype(jnp.int32).astype(jnp.float32)
            to = pl.ds(pl.multiple_of(place * half, half), half)
            values[s, to] = jnp.where(kind_ref[s] >= 0, value * scale[s : s + 1], 0.0)
        copies.append(pltpu.make_async_copy(values.at[s], out_ref.at[s], sems.at[s]))
        copies[-1].start()
    for copy in copies:
        copy.wait()


def decode(kind, place, mine, other, width):
    count = kind.shape[0]
    return pl.pallas_call(
        decode_kernel,
        in_specs=[pl.BlockSpec(memory_space=pltpu.SMEM)] * 2
        + [pl.BlockSpec(memory_space=pltpu.VMEM)] * 2,
        out_specs=pl.BlockSpec(memory_space=pltpu.HBM),
        out_shape=pltpu.HBM((count, width, width), jnp.float32),
        scratch_shapes=[
            pltpu.VMEM((count, width, width), jnp.float32),
            pltpu.SemaphoreType.DMA((count,)),
        ],
        compiler_params=pltpu.CompilerParams(vmem_limit_bytes=SMALL_VMEM),
        name="decode",
    )(kind, place, mine, other)


def body(
    gradients, first_moment, second_moment, left_basis, right_basis, shard_starts, block_owners
):
    me = lax.axis_index("fsdp").astype(jnp.int32)
    core = lax.axis_index("dp").astype(jnp.int32)
    devices = lax.axis_size("fsdp")
    slot_count, width = gradients.shape[1], gradients.shape[3]
    owned_slots = first_moment.shape[0]
    half = width // lax.axis_size("dp")
    side, cross, flip, far = partner_pairs(devices)
    place = core.reshape(1)

    own_kind, own_slot, held_kind = tables(
        shard_starts, block_owners, me, slot_count, owned_slots
    )
    replica = gradients[0]
    twin = swap_cores(replica)

    summed = add_replicas(place, load_rows(place, replica, half), twin)
    by_flip = exchange(summed, flip)
    by_cross = exchange(summed, cross)
    by_far = exchange(summed, far)
    by_side = exchange(summed, side)
    prepared = prepare(place, first_moment, second_moment, left_basis, right_basis, half)
    mine = collect(own_kind, own_slot, (summed, by_side, by_cross, by_flip, by_far))
    other = swap_cores(mine)
    second, keep, to_side, to_cross, to_flip, to_far = soap_step(
        own_kind, own_slot, place, mine, other, prepared, slot_count
    )
    first_new, second_new = finish(own_kind, place, mine, other, first_moment, second)
    sent = (
        keep,
        exchange(to_side, side),
        exchange(to_cross, cross),
        exchange(to_flip, flip),
        exchange(to_far, far),
    )
    coded = gather_held(held_kind, sent)
    direction = decode(held_kind, place, coded, swap_cores(coded), width)
    return (direction, first_new, second_new)


def solution(mesh):
    in_specs = (
        P("dp", "fsdp", None, None),
        P("fsdp", None, None),
        P("fsdp", None, None),
        P("fsdp", None, None),
        P("fsdp", None, None),
        P(),
        P(),
    )
    out_specs = (P("fsdp", None, None), P("fsdp", None, None), P("fsdp", None, None))
    return jax.shard_map(body, mesh=mesh, in_specs=in_specs, out_specs=out_specs, check_vma=False)
```

time: 74.1 us -> 67.5 us (0.911)
  the two profiles are of different devices: /device:TPU:0 before, /device:TPU:11 now
where the time goes in v3:
time: 67.5 us; the launch traced here: 67.1 us
  waiting for transfers between devices  29.5 us (44%)
  Pallas kernels  18.9 us (28%)
  starting transfers between devices  18.1 us (27%)
  between operations  0.72 us (1%)
    ppermute x8, waiting for transfers between devices, exchange(): return lax.ppermute(value, 'fsdp', pairs + [(b, a) for a, b in pairs])  28.7 us
    ppermute x8, starting transfers between devices, exchange(): return lax.ppermute(value, 'fsdp', pairs + [(b, a) for a, b in pairs])  15.3 us
    pallas_call x1, Pallas kernels, finish(): pl.pallas_call(finish_kernel, grid=(count,), in_specs=[pl.BlockSpec(memor...  4.91 us
    pallas_call x1, Pallas kernels, soap_step(): pl.pallas_call(step_kernel, grid_spec=pltpu.PrefetchScalarGridSpec(num_sc...  4.05 us
    pallas_call x1, Pallas kernels, prepare(): pl.pallas_call(prepare_kernel, grid=(count // group,), in_specs=[pl.Block...  3.94 us
    ppermute x3, starting transfers between devices, swap_cores(): return lax.ppermute(value, 'dp', [(0, 1), (1, 0)])  2.82 us
    pallas_call x1, Pallas kernels, tables(): pl.pallas_call(tables_kernel, in_specs=[pl.BlockSpec(memory_space=pltpu.S...  1.77 us
    pallas_call x1, Pallas kernels, decode(): pl.pallas_call(decode_kernel, in_specs=[pl.BlockSpec(memory_space=pltpu.S...  1.64 us
  transfers between devices with their start and end apart: 11, of which 6 were waited for; matrix products, arithmetic and copies ran while one was open for 0% of the time, Pallas kernels for 17%

profile of v3, /device:TPU:11, one launch (start us, length us, event | category | flops | bytes accessed | tf_op | source)
XLA Modules:
  0.0 67.1 jit_solution(17482185887479164911)
XLA Ops:
  0.6 0.7 %collective-permute-start = (bf16[4,256,256]{2,1,0:T(8,128)(2,1)}, bf16[4,256,256]{2,1,0:T(8,128)(2,1)S(1)}, u32[]{:S(2)}, u32[]{:S(2)}) collective-permute-start(bf16[4,256,256]{2,1,0:T(8,128)(2,1)} %bitcast.3), channel_id=1, source_target_pairs={{0,1},{1,0},{2,3},{3,2},{4,5},{5,4},{6,7},{7,6},{8,9},{9,8},{10,11... | collective-permute-start | bytes 1572872 | tf_op jit(solution)/shard_map/ppermute | solution.py:40
  1.4 1.0 %load_rows.1.mine_ref = bf16[4,128,256]{2,1,0:T(8,128)(2,1)S(1)} custom-call(s32[1]{0:T(128)} %bitcast.1.place_ref, bf16[4,256,256]{2,1,0:T(8,128)(2,1)} %bitcast.4), custom_call_target="tpu_custom_call" | custom-call | tf_op jit(solution)/shard_map/load_rows/pallas_call | solution.py:161
  2.3 0.8 %collective-permute-done.other_ref = bf16[4,256,256]{2,1,0:T(8,128)(2,1)S(1)} collective-permute-done((bf16[4,256,256]{2,1,0:T(8,128)(2,1)}, bf16[4,256,256]{2,1,0:T(8,128)(2,1)S(1)}, u32[]{:S(2)}, u32[]{:S(2)}) %collective-permute-start) | collective-permute-done | bytes 524320 | tf_op jit(solution)/shard_map/ppermute | solution.py:40
  3.1 0.1 add_replicas.1.refs_0_
  3.2 3.0 %collective-permute-start.4 = (bf16[4,128,256]{2,1,0:T(8,128)(2,1)S(1)}, bf16[4,128,256]{2,1,0:T(8,128)(2,1)S(1)}, u32[]{:S(2)}, u32[]{:S(2)}) collective-permute-start(bf16[4,128,256]{2,1,0:T(8,128)(2,1)S(1)} %add_replicas.1.refs_0_), channel_id=1, source_target_pairs={{4,8},{6,10},{12,16},{14,18},{20,24},{22,26},{8,4},{10,6},{16,12},... | collective-permute-start | bytes 786440 | tf_op jit(solution)/shard_map/ppermute | solution.py:28
  6.2 1.4 %collective-permute-start.3 = (bf16[4,128,256]{2,1,0:T(8,128)(2,1)S(1)}, bf16[4,128,256]{2,1,0:T(8,128)(2,1)S(1)}, u32[]{:S(2)}, u32[]{:S(2)}) collective-permute-start(bf16[4,128,256]{2,1,0:T(8,128)(2,1)S(1)} %add_replicas.1.refs_0_), channel_id=1, source_target_pairs={{0,4},{2,6},{8,12},{10,14},{16,20},{18,22},{24,28},{26,30},{4,0},{... | collective-permute-start | bytes 786440 | tf_op jit(solution)/shard_map/ppermute | solution.py:28
  7.6 2.0 %collective-permute-start.2 = (bf16[4,128,256]{2,1,0:T(8,128)(2,1)S(1)}, bf16[4,128,256]{2,1,0:T(8,128)(2,1)S(1)}, u32[]{:S(2)}, u32[]{:S(2)}) collective-permute-start(bf16[4,128,256]{2,1,0:T(8,128)(2,1)S(1)} %add_replicas.1.refs_0_), channel_id=1, source_target_pairs={{2,4},{6,8},{10,12},{14,16},{18,20},{22,24},{26,28},{4,2},{8,6},{1... | collective-permute-start | bytes 786440 | tf_op jit(solution)/shard_map/ppermute | solution.py:28
  9.6 1.1 %collective-permute-start.1 = (bf16[4,128,256]{2,1,0:T(8,128)(2,1)S(1)}, bf16[4,128,256]{2,1,0:T(8,128)(2,1)S(1)}, u32[]{:S(2)}, u32[]{:S(2)}) collective-permute-start(bf16[4,128,256]{2,1,0:T(8,128)(2,1)S(1)} %add_replicas.1.refs_0_), channel_id=1, source_target_pairs={{0,2},{4,6},{8,10},{12,14},{16,18},{20,22},{24,26},{28,30},{2,0},{... | collective-permute-start | bytes 786440 | tf_op jit(solution)/shard_map/ppermute | solution.py:28
  10.7 1.8 %tables.1 = (s32[6]{0:T(128)S(1)}, s32[6]{0:T(128)S(1)}, s32[4]{0:T(128)S(1)}) custom-call(s32[1]{0:T(128)} %bitcast.me_ref, s32[16]{0:T(128)} %starts_ref.1, s32[48]{0:T(128)} %owners_ref.1), custom_call_target="tpu_custom_call" | custom-call | tf_op jit(solution)/shard_map/tables/pallas_call | solution.py:87
  12.5 1.2 %collective-permute-done.4.refs_4_ = bf16[4,128,256]{2,1,0:T(8,128)(2,1)S(1)} collective-permute-done((bf16[4,128,256]{2,1,0:T(8,128)(2,1)S(1)}, bf16[4,128,256]{2,1,0:T(8,128)(2,1)S(1)}, u32[]{:S(2)}, u32[]{:S(2)}) %collective-permute-start.4) | collective-permute-done | bytes 262176 | tf_op jit(solution)/shard_map/ppermute | solution.py:28
  13.6 11.8 %collective-permute-done.3.refs_3_ = bf16[4,128,256]{2,1,0:T(8,128)(2,1)S(1)} collective-permute-done((bf16[4,128,256]{2,1,0:T(8,128)(2,1)S(1)}, bf16[4,128,256]{2,1,0:T(8,128)(2,1)S(1)}, u32[]{:S(2)}, u32[]{:S(2)}) %collective-permute-start.3) | collective-permute-done | bytes 262176 | tf_op jit(solution)/shard_map/ppermute | solution.py:28
  25.4 0.0 collective-permute-done.2.refs_2_
  25.4 0.0 collective-permute-done.1.refs_1_
  25.4 0.8 %collect.1.mine_ref = bf16[6,128,256]{2,1,0:T(8,128)(2,1)S(1)} custom-call(s32[6]{0:T(128)S(1)} %get-tuple-element.23.kind_ref, s32[6]{0:T(128)S(1)} %get-tuple-element.24.slot_ref, bf16[4,128,256]{2,1,0:T(8,128)(2,1)S(1)} %add_replicas.1.refs_0_, bf16[4,128,256]{2,1,0:T(8,128)(2,1)S(1)} %collective-permute-done.1.refs_1_, ...), custom_call_target="tpu_custom_call" | custom-call | tf_op jit(solution)/shard_map/collect/pallas_call | solution.py:207
  26.3 0.6 collective-permute-start.5
  26.8 3.9 %prepare.1 = (f32[6,256,256]{2,1,0:T(8,128)S(1)}, f32[6,256,256]{2,1,0:T(8,128)S(1)}, bf16[6,256,256]{2,1,0:T(8,128)(2,1)S(1)}, bf16[6,256,256]{2,1,0:T(8,128)(2...) custom-call(s32[1]{0:T(128)} %bitcast.1.place_ref, ...), custom_call_target="tpu_custom_call" | custom-call | flops 1207959552 | bytes 6291456 | tf_op jit(solution)/shard_map/prepare/pallas_call | solution.py:141
  30.8 0.0 collective-permute-done.5.other_ref
  30.8 4.1 %soap_step.1 = (f32[6,256,256]{2,1,0:T(8,128)S(1)}, s16[528,256]{1,0:T(8,128)(2,1)S(1)}, s16[528,256]{1,0:T(8,128)(2,1)S(1)}, s16[528,256]{1,0:T(8,128)(2,1)S(1)...) custom-call(s32[6]{0:T(128)S(1)} %get-tuple-element.23.kind_ref, s32[6]{0:T(128)S(1)} %get-tuple-element.24.slot_ref, ...), custom_call_target="tpu_custom_call" | custom-call | tf_op jit(solution)/shard_map/soap_step/pallas_call | solution.py:279
  34.8 0.4 collective-permute-start.6
  35.2 4.0 %collective-permute-start.7 = (s16[528,256]{1,0:T(8,128)(2,1)S(1)}, s16[528,256]{1,0:T(8,128)(2,1)S(1)}, u32[]{:S(2)}, u32[]{:S(2)}) collective-permute-start(s16[528,256]{1,0:T(8,128)(2,1)S(1)} %get-tuple-element.35), channel_id=1, source_target_pairs={{2,4},{6,8},{10,12},{14,16},{18,20},{22,24},{26,28},{4,2},{8,6},{1... | collective-permute-start | bytes 811016 | tf_op jit(solution)/shard_map/ppermute | solution.py:28
  39.2 1.3 %collective-permute-start.8 = (s16[528,256]{1,0:T(8,128)(2,1)S(1)}, s16[528,256]{1,0:T(8,128)(2,1)S(1)}, u32[]{:S(2)}, u32[]{:S(2)}) collective-permute-start(s16[528,256]{1,0:T(8,128)(2,1)S(1)} %get-tuple-element.36), channel_id=1, source_target_pairs={{0,4},{2,6},{8,12},{10,14},{16,20},{18,22},{24,28},{26,30},{4,0},{... | collective-permute-start | bytes 811016 | tf_op jit(solution)/shard_map/ppermute | solution.py:28
  40.6 2.0 %collective-permute-start.9 = (s16[528,256]{1,0:T(8,128)(2,1)S(1)}, s16[528,256]{1,0:T(8,128)(2,1)S(1)}, u32[]{:S(2)}, u32[]{:S(2)}) collective-permute-start(s16[528,256]{1,0:T(8,128)(2,1)S(1)} %get-tuple-element.37), channel_id=1, source_target_pairs={{4,8},{6,10},{12,16},{14,18},{20,24},{22,26},{8,4},{10,6},{16,12},... | collective-permute-start | bytes 811016 | tf_op jit(solution)/shard_map/ppermute | solution.py:28
  42.6 5.9 %collective-permute-done.6.refs_1_ = s16[528,256]{1,0:T(8,128)(2,1)S(1)} collective-permute-done((s16[528,256]{1,0:T(8,128)(2,1)S(1)}, s16[528,256]{1,0:T(8,128)(2,1)S(1)}, u32[]{:S(2)}, u32[]{:S(2)}) %collective-permute-start.6) | collective-permute-done | bytes 270368 | tf_op jit(solution)/shard_map/ppermute | solution.py:28
  48.5 3.1 %collective-permute-done.7.refs_2_ = s16[528,256]{1,0:T(8,128)(2,1)S(1)} collective-permute-done((s16[528,256]{1,0:T(8,128)(2,1)S(1)}, s16[528,256]{1,0:T(8,128)(2,1)S(1)}, u32[]{:S(2)}, u32[]{:S(2)}) %collective-permute-start.7) | collective-permute-done | bytes 270368 | tf_op jit(solution)/shard_map/ppermute | solution.py:28
  51.6 6.8 %collective-permute-done.8.refs_3_ = s16[528,256]{1,0:T(8,128)(2,1)S(1)} collective-permute-done((s16[528,256]{1,0:T(8,128)(2,1)S(1)}, s16[528,256]{1,0:T(8,128)(2,1)S(1)}, u32[]{:S(2)}, u32[]{:S(2)}) %collective-permute-start.8) | collective-permute-done | bytes 270368 | tf_op jit(solution)/shard_map/ppermute | solution.py:28
  58.3 0.0 collective-permute-done.9.refs_4_
  58.3 0.7 %gather_held.1.mine_ref = s16[528,256]{1,0:T(8,128)(2,1)S(1)} custom-call(s32[4]{0:T(128)S(1)} %get-tuple-element.22.kind_ref, s16[528,256]{1,0:T(8,128)(2,1)S(1)} %get-tuple-element.33.refs_0_, s16[528,256]{1,0:T(8,128)(2,1)S(1)} %collective-permute-done.6.refs_1_, s16[528,256]{1,0:T(8,128)(2,1)S(1)} %collective-permute-done.7.refs_2_, ...), custom_call_target="tpu_custom_call" | custom-call | tf_op jit(solution)/shard_map/gather_held/pallas_call | solution.py:353
  59.1 1.5 %collective-permute-start.10 = (s16[528,256]{1,0:T(8,128)(2,1)S(1)}, s16[528,256]{1,0:T(8,128)(2,1)S(1)}, u32[]{:S(2)}, u32[]{:S(2)}) collective-permute-start(s16[528,256]{1,0:T(8,128)(2,1)S(1)} %gather_held.1.mine_ref), channel_id=1, source_target_pairs={{0,1},{1,0},{2,3},{3,2},{4,5},{5,4},{6,7},{7,6},{8,9},{9,8},{10,11... | collective-permute-start | bytes 811016 | tf_op jit(solution)/shard_map/ppermute | solution.py:40
  60.6 4.9 %finish.1 = (f32[6,256,256]{2,1,0:T(8,128)}, f32[6,256,256]{2,1,0:T(8,128)}) custom-call(s32[6]{0:T(128)S(1)} %get-tuple-element.23.kind_ref, s32[1]{0:T(128)} %bitcast.1.place_ref, bf16[6,128,256]{2,1,0:T(8,128)(2,1)S(1)} %collect.1.mine_ref, bf16[6,128,256]{2,1,0:T(8,128)(2,1)S(1)} %collective-permute-done.5.other_ref, f32[6,256,256]{2,1,0:T(8,128)} %moment_ref.3, ...), custom_call_target="tpu_custom_call" | custom-call | flops 4718592 | bytes 4718592 | tf_op jit(solution)/shard_map/finish/pallas_call | solution.py:316
  65.5 0.0 collective-permute-done.10.other_ref
  65.5 1.6 %decode.1 = f32[4,256,256]{2,1,0:T(8,128)} custom-call(s32[4]{0:T(128)S(1)} %get-tuple-element.22.kind_ref, s32[1]{0:T(128)} %bitcast.1.place_ref, s16[528,256]{1,0:T(8,128)(2,1)S(1)} %gather_held.1.mine_ref, s16[528,256]{1,0:T(8,128)(2,1)S(1)} %collective-permute-done.10.other_ref), custom_call_target="tpu_custom_call" | custom-call | tf_op jit(solution)/shard_map/decode/pallas_call | solution.py:387
Async XLA Ops:
  0.6 2.5 %collective-permute-start = (bf16[4,256,256]{2,1,0:T(8,128)(2,1)}, bf16[4,256,256]{2,1,0:T(8,128)(2,1)S(1)}, u32[]{:S(2)}, u32[]{:S(2)}) collective-permute-start(bf16[4,256,256]{2,1,0:T(8,128)(2,1)} %bitcast.3), channel_id=1, source_target_pairs={{0,1},{1,0},{2,3},{3,2},{4,5},{5,4},{6,7},{7,6},{8,9},{9,8},{10,11... | collective-permute-start | bytes 1572872 | tf_op jit(solution)/shard_map/ppermute | solution.py:40
  3.2 10.5 %collective-permute-start.4 = (bf16[4,128,256]{2,1,0:T(8,128)(2,1)S(1)}, bf16[4,128,256]{2,1,0:T(8,128)(2,1)S(1)}, u32[]{:S(2)}, u32[]{:S(2)}) collective-permute-start(bf16[4,128,256]{2,1,0:T(8,128)(2,1)S(1)} %add_replicas.1.refs_0_), channel_id=1, source_target_pairs={{4,8},{6,10},{12,16},{14,18},{20,24},{22,26},{8,4},{10,6},{16,12},... | collective-permute-start | bytes 786440 | tf_op jit(solution)/shard_map/ppermute | solution.py:28
  6.2 19.2 %collective-permute-start.3 = (bf16[4,128,256]{2,1,0:T(8,128)(2,1)S(1)}, bf16[4,128,256]{2,1,0:T(8,128)(2,1)S(1)}, u32[]{:S(2)}, u32[]{:S(2)}) collective-permute-start(bf16[4,128,256]{2,1,0:T(8,128)(2,1)S(1)} %add_replicas.1.refs_0_), channel_id=1, source_target_pairs={{0,4},{2,6},{8,12},{10,14},{16,20},{18,22},{24,28},{26,30},{4,0},{... | collective-permute-start | bytes 786440 | tf_op jit(solution)/shard_map/ppermute | solution.py:28
  7.6 17.8 %collective-permute-start.2 = (bf16[4,128,256]{2,1,0:T(8,128)(2,1)S(1)}, bf16[4,128,256]{2,1,0:T(8,128)(2,1)S(1)}, u32[]{:S(2)}, u32[]{:S(2)}) collective-permute-start(bf16[4,128,256]{2,1,0:T(8,128)(2,1)S(1)} %add_replicas.1.refs_0_), channel_id=1, source_target_pairs={{2,4},{6,8},{10,12},{14,16},{18,20},{22,24},{26,28},{4,2},{8,6},{1... | collective-permute-start | bytes 786440 | tf_op jit(solution)/shard_map/ppermute | solution.py:28
  9.6 15.8 %collective-permute-start.1 = (bf16[4,128,256]{2,1,0:T(8,128)(2,1)S(1)}, bf16[4,128,256]{2,1,0:T(8,128)(2,1)S(1)}, u32[]{:S(2)}, u32[]{:S(2)}) collective-permute-start(bf16[4,128,256]{2,1,0:T(8,128)(2,1)S(1)} %add_replicas.1.refs_0_), channel_id=1, source_target_pairs={{0,2},{4,6},{8,10},{12,14},{16,18},{20,22},{24,26},{28,30},{2,0},{... | collective-permute-start | bytes 786440 | tf_op jit(solution)/shard_map/ppermute | solution.py:28
  26.3 4.5 %collective-permute-start.5 = (bf16[6,128,256]{2,1,0:T(8,128)(2,1)S(1)}, bf16[6,128,256]{2,1,0:T(8,128)(2,1)S(1)}, u32[]{:S(2)}, u32[]{:S(2)}) collective-permute-start(bf16[6,128,256]{2,1,0:T(8,128)(2,1)S(1)} %collect.1.mine_ref), channel_id=1, source_target_pairs={{0,1},{1,0},{2,3},{3,2},{4,5},{5,4},{6,7},{7,6},{8,9},{9,8},{10,11... | collective-permute-start | bytes 1179656 | tf_op jit(solution)/shard_map/ppermute | solution.py:40
  34.8 13.6 %collective-permute-start.6 = (s16[528,256]{1,0:T(8,128)(2,1)S(1)}, s16[528,256]{1,0:T(8,128)(2,1)S(1)}, u32[]{:S(2)}, u32[]{:S(2)}) collective-permute-start(s16[528,256]{1,0:T(8,128)(2,1)S(1)} %get-tuple-element.34), channel_id=1, source_target_pairs={{0,2},{4,6},{8,10},{12,14},{16,18},{20,22},{24,26},{28,30},{2,0},{... | collective-permute-start | bytes 811016 | tf_op jit(solution)/shard_map/ppermute | solution.py:28
  35.2 16.3 %collective-permute-start.7 = (s16[528,256]{1,0:T(8,128)(2,1)S(1)}, s16[528,256]{1,0:T(8,128)(2,1)S(1)}, u32[]{:S(2)}, u32[]{:S(2)}) collective-permute-start(s16[528,256]{1,0:T(8,128)(2,1)S(1)} %get-tuple-element.35), channel_id=1, source_target_pairs={{2,4},{6,8},{10,12},{14,16},{18,20},{22,24},{26,28},{4,2},{8,6},{1... | collective-permute-start | bytes 811016 | tf_op jit(solution)/shard_map/ppermute | solution.py:28
  39.2 19.1 %collective-permute-start.8 = (s16[528,256]{1,0:T(8,128)(2,1)S(1)}, s16[528,256]{1,0:T(8,128)(2,1)S(1)}, u32[]{:S(2)}, u32[]{:S(2)}) collective-permute-start(s16[528,256]{1,0:T(8,128)(2,1)S(1)} %get-tuple-element.36), channel_id=1, source_target_pairs={{0,4},{2,6},{8,12},{10,14},{16,20},{18,22},{24,28},{26,30},{4,0},{... | collective-permute-start | bytes 811016 | tf_op jit(solution)/shard_map/ppermute | solution.py:28
  40.6 17.8 %collective-permute-start.9 = (s16[528,256]{1,0:T(8,128)(2,1)S(1)}, s16[528,256]{1,0:T(8,128)(2,1)S(1)}, u32[]{:S(2)}, u32[]{:S(2)}) collective-permute-start(s16[528,256]{1,0:T(8,128)(2,1)S(1)} %get-tuple-element.37), channel_id=1, source_target_pairs={{4,8},{6,10},{12,16},{14,18},{20,24},{22,26},{8,4},{10,6},{16,12},... | collective-permute-start | bytes 811016 | tf_op jit(solution)/shard_map/ppermute | solution.py:28
  59.1 6.4 %collective-permute-start.10 = (s16[528,256]{1,0:T(8,128)(2,1)S(1)}, s16[528,256]{1,0:T(8,128)(2,1)S(1)}, u32[]{:S(2)}, u32[]{:S(2)}) collective-permute-start(s16[528,256]{1,0:T(8,128)(2,1)S(1)} %gather_held.1.mine_ref), channel_id=1, source_target_pairs={{0,1},{1,0},{2,3},{3,2},{4,5},{5,4},{6,7},{7,6},{8,9},{9,8},{10,11... | collective-permute-start | bytes 811016 | tf_op jit(solution)/shard_map/ppermute | solution.py:40

commit v4 on v3

--- a/solution.py
+++ b/solution.py
@@ -1,3 +1,5 @@
+import functools
+
 import jax
 import jax.numpy as jnp
 from jax import lax
@@ -8,10 +10,10 @@
 
 REACH = 2
 STEP = 10
-CODE_ROWS = 16
+CODE_ROWS = 8
 CODE_STEPS = 128.0
 PREPARE_GROUP = 3
-GROUP = 3
+GROUP = 6
 SMALL_VMEM = 12 * 2**20
 STEP_VMEM = 28 * 2**20
 
@@ -55,8 +57,13 @@
     return tuple(pltpu.with_memory_space_constraint(value, pltpu.VMEM) for value in values)
 
 
-def tables_kernel(me_ref, starts_ref, owners_ref, owned_kind, owned_slot, held_kind):
-    me = me_ref[0]
+def in_smem(*values):
+    return tuple(pltpu.with_memory_space_constraint(value, pltpu.SMEM) for value in values)
+
+
+def tables_kernel(at_ref, starts_ref, owners_ref, owned_kind, owned_slot, held_kind, core):
+    me = at_ref[0]
+    core[0] = at_ref[1]
     devices, total = starts_ref.shape[0], owners_ref.shape[0]
 
     def tally(b, sums):
@@ -82,16 +89,17 @@
         held_kind[s] = jnp.where(start + s < end, partner_kind(me, owner), -1)
 
 
-def tables(shard_starts, block_owners, me, slot_count, owned_slots):
-    owned = jax.ShapeDtypeStruct((owned_slots,), jnp.int32)
+def tables(shard_starts, block_owners, at, slot_count, owned_slots):
+    owned = pltpu.SMEM((owned_slots,), jnp.int32)
     return pl.pallas_call(
         tables_kernel,
         in_specs=[pl.BlockSpec(memory_space=pltpu.SMEM)] * 3,
-        out_specs=[pl.BlockSpec(memory_space=pltpu.SMEM)] * 3,
-        out_shape=[owned, owned, jax.ShapeDtypeStruct((slot_count,), jnp.int32)],
+        out_specs=[pl.BlockSpec(memory_space=pltpu.SMEM)] * 4,
+        out_shape=[owned, owned]
+        + [pltpu.SMEM((size,), jnp.int32) for size in (slot_count, 1)],
         compiler_params=pltpu.CompilerParams(vmem_limit_bytes=SMALL_VMEM),
         name="tables",
-    )(me.reshape(1), *in_hbm(shard_starts, block_owners))
+    )(at, *in_hbm(shard_starts, block_owners))
 
 
 def split(value):
@@ -104,9 +112,9 @@
 
 
 def product3(a, b, dims):
-    left = jnp.concatenate((a[0], a[0], a[1]), axis=dims[0][0])
-    right = jnp.concatenate((b[0], b[1], b[0]), axis=dims[1][0])
-    return product(left, right, dims)
+    count = a[0].shape[0]
+    tall = product(jnp.concatenate(a, axis=0), b[0], dims)
+    return tall[:count] + (tall[count:] + product(a[0], b[1], dims))
 
 
 NN = ((1,), (0,))
@@ -212,7 +220,7 @@
         out_shape=jax.ShapeDtypeStruct((count,) + sources[0].shape[1:], sources[0].dtype),
         compiler_params=pltpu.CompilerParams(vmem_limit_bytes=SMALL_VMEM),
         name="collect",
-    )(kind, slot, *sources)
+    )(*in_smem(kind, slot), *sources)
 
 
 def step_kernel(kind_ref, slot_ref, place_ref, mine_ref, other_ref, *refs):
@@ -228,30 +236,38 @@
     def _():
         codes[...] = jnp.zeros_like(codes)
 
-    for g in every:
+    spots = lax.broadcasted_iota(jnp.int32, codes.shape[1:], 0)
+    at = [dict() for _ in every]
+
+    def rotate_right(g):
         grads[g, pl.ds(here, half)] = mine_ref[g]
         grads[g, pl.ds(there, half)] = other_ref[g]
-    right = [(right_high[g], right_low[g]) for g in every]
-    first = [
-        product(jnp.concatenate((grads[g],) * 2, axis=1), jnp.concatenate(right[g], axis=0), NN)
-        for g in every
-    ]
-    turned = [product3((flip_high[g], flip_low[g]), split(first[g]), NN) for g in every]
-    scaled = []
-    for g in every:
-        second = second_ref[g] + (1.0 - beta_two) * turned[g] * turned[g]
+        wide = jnp.concatenate((grads[g],) * 2, axis=1)
+        at[g]["first"] = product(wide, jnp.concatenate((right_high[g], right_low[g]), axis=0), NN)
+
+    def rotate_left(g):
+        at[g]["turned"] = product3((flip_high[g], flip_low[g]), split(at[g].pop("first")), NN)
+
+    def scale(g):
+        turned = at[g].pop("turned")
+        second = second_ref[g] + (1.0 - beta_two) * turned * turned
         second_out[g] = second
         unbiased = second * (1.0 / bias_two)
         root = unbiased * lax.rsqrt(unbiased)
-        moment = turned_ref[g] + ((1.0 - beta_one) / bias_one) * turned[g]
-        scaled.append(split(moment / (root + epsilon)))
-    back = [product3((row_high[g], row_low[g]), scaled[g], NN) for g in every]
-    update = [product3(split(back[g]), right[g], NT) for g in every]
-    spots = lax.broadcasted_iota(jnp.int32, codes.shape[1:], 0)
-    for g in every:
-        peak = jnp.max(jnp.abs(update[g]), axis=0, keepdims=True)
+        moment = turned_ref[g] + ((1.0 - beta_one) / bias_one) * turned
+        at[g]["scaled"] = split(moment / (root + epsilon))
+
+    def return_left(g):
+        at[g]["back"] = product3((row_high[g], row_low[g]), at[g].pop("scaled"), NN)
+
+    def return_right(g):
+        at[g]["update"] = product3(split(at[g].pop("back")), (right_high[g], right_low[g]), NT)
+
+    def code_update(g):
+        update = at[g].pop("update")
+        peak = jnp.max(jnp.abs(update), axis=0, keepdims=True)
         code = jnp.ceil(jnp.log2(jnp.maximum(peak, 1e-30) * (1.0 / 32000.0)) * CODE_STEPS)
-        coded = jnp.round(update[g] * jnp.exp2(code * (-1.0 / CODE_STEPS)))
+        coded = jnp.round(update * jnp.exp2(code * (-1.0 / CODE_STEPS)))
         coded = jnp.clip(coded, -32767.0, 32767.0).astype(jnp.int32).astype(jnp.int16)
         slot = slot_ref[step * group + g]
         rows = pl.ds(pl.multiple_of(slot * half, half), half)
@@ -261,6 +277,14 @@
             def _():
                 sends[kind][rows] = coded
                 codes[kind] = jnp.where(spots == slot, code.astype(jnp.int32), codes[kind])
+
+    stages = (rotate_right, rotate_left, scale, return_left, return_right)
+    for wave in range(group + len(stages) - 1):
+        for depth in reversed(range(len(stages))):
+            if 0 <= wave - depth < group:
+                stages[depth](wave - depth)
+    for g in every:
+        code_update(g)
 
     @pl.when(step == pl.num_programs(0) - 1)
     def _():
@@ -272,27 +296,27 @@
 def soap_step(kind, slot, place, mine, other, prepared, slot_count):
     count, half, width = mine.shape
     group = GROUP if count % GROUP == 0 else 1
-    full = pl.BlockSpec((group, width, width), lambda j, *_: (j, 0, 0))
-    part = pl.BlockSpec((group, half, width), lambda j, *_: (j, 0, 0))
+    full = pl.BlockSpec((group, width, width), lambda j: (j, 0, 0))
+    part = pl.BlockSpec((group, half, width), lambda j: (j, 0, 0))
     send_rows = slot_count * half + CODE_ROWS
-    send = pl.BlockSpec((send_rows, width), lambda j, *_: (0, 0))
+    send = pl.BlockSpec((send_rows, width), lambda j: (0, 0))
     return pl.pallas_call(
         step_kernel,
-        grid_spec=pltpu.PrefetchScalarGridSpec(
-            num_scalar_prefetch=3,
-            grid=(count // group,),
-            in_specs=[part, part] + [full] * 6 + [part] * 2,
-            out_specs=[full] + [send] * 5,
-            scratch_shapes=[
-                pltpu.VMEM((5, CODE_ROWS, width), jnp.int32),
-                pltpu.VMEM((group, width, width), jnp.bfloat16),
-            ],
-        ),
+        grid=(count // group,),
+        in_specs=[pl.BlockSpec(memory_space=pltpu.SMEM)] * 3
+        + [part, part]
+        + [full] * 6
+        + [part] * 2,
+        out_specs=[full] + [send] * 5,
+        scratch_shapes=[
+            pltpu.VMEM((5, CODE_ROWS, width), jnp.int32),
+            pltpu.VMEM((group, width, width), jnp.bfloat16),
+        ],
         out_shape=[pltpu.VMEM((count, width, width), jnp.float32)]
         + [pltpu.VMEM((send_rows, width), jnp.int16)] * 5,
         compiler_params=pltpu.CompilerParams(vmem_limit_bytes=STEP_VMEM),
         name="soap_step",
-    )(kind, slot, place, *in_vmem(mine, other, *prepared))
+    )(*in_smem(kind, slot, place), *in_vmem(mine, other, *prepared))
 
 
 def finish_kernel(kind_ref, place_ref, mine_ref, other_ref, moment_ref, second_ref, *outs):
@@ -324,7 +348,7 @@
             flops=12 * count * width**2, bytes_accessed=12 * count * width**2, transcendentals=0
         ),
         name="finish",
-    )(kind, place, *in_vmem(mine, other), *in_hbm(first_moment), *in_vmem(second))
+    )(*in_smem(kind, place), *in_vmem(mine, other), *in_hbm(first_moment), *in_vmem(second))
 
 
 def gather_kernel(kind_ref, *refs):
@@ -358,45 +382,49 @@
         out_shape=jax.ShapeDtypeStruct(sources[0].shape, sources[0].dtype),
         compiler_params=pltpu.CompilerParams(vmem_limit_bytes=SMALL_VMEM),
         name="gather_held",
-    )(kind, *sources)
-
-
-def decode_kernel(kind_ref, place_ref, mine_ref, other_ref, out_ref, values, sems):
-    count = values.shape[0]
-    top = mine_ref.shape[0] - CODE_ROWS
-    half = top // count
-    both = ((place_ref[0], mine_ref), (1 - place_ref[0], other_ref))
-    scales = []
-    for _, coded in both:
-        code = coded[pl.ds(top, CODE_ROWS)].astype(jnp.int32).astype(jnp.float32)
-        scales.append(jnp.exp2(code * (1.0 / CODE_STEPS)))
+    )(*in_smem(kind), *sources)
+
+
+def decode_kernel(kind_ref, core_ref, coded_ref, *refs, twin):
+    out_ref, values, sems = refs[-3:]
+    count, half = values.shape[:2]
+    top = count * half
+    place = 1 - core_ref[0] if twin else core_ref[0]
+    to = pl.ds(pl.multiple_of(place * half, half), half)
+    code = coded_ref[pl.ds(top, CODE_ROWS)].astype(jnp.int32).astype(jnp.float32)
+    scales = jnp.exp2(code * (1.0 / CODE_STEPS))
     copies = []
     for s in range(count):
-        for (place, coded), scale in zip(both, scales):
-            value = coded[pl.ds(s * half, half)].astype(jnp.int32).astype(jnp.float32)
-            to = pl.ds(pl.multiple_of(place * half, half), half)
-            values[s, to] = jnp.where(kind_ref[s] >= 0, value * scale[s : s + 1], 0.0)
-        copies.append(pltpu.make_async_copy(values.at[s], out_ref.at[s], sems.at[s]))
+        value = coded_ref[pl.ds(s * half, half)].astype(jnp.int32).astype(jnp.float32)
+        values[s] = jnp.where(kind_ref[s] >= 0, value * scales[s : s + 1], 0.0)
+        copies.append(pltpu.make_async_copy(values.at[s], out_ref.at[s, to], sems.at[s]))
         copies[-1].start()
     for copy in copies:
         copy.wait()
 
 
-def decode(kind, place, mine, other, width):
+def decode(kind, core, coded, base, width):
     count = kind.shape[0]
-    return pl.pallas_call(
-        decode_kernel,
+    half = (coded.shape[0] - CODE_ROWS) // count
+    twin = base is not None
+    return pl.pallas_call(
+        functools.partial(decode_kernel, twin=twin),
         in_specs=[pl.BlockSpec(memory_space=pltpu.SMEM)] * 2
-        + [pl.BlockSpec(memory_space=pltpu.VMEM)] * 2,
+        + [pl.BlockSpec(memory_space=pltpu.VMEM)]
+        + [pl.BlockSpec(memory_space=pltpu.HBM)] * twin,
         out_specs=pl.BlockSpec(memory_space=pltpu.HBM),
         out_shape=pltpu.HBM((count, width, width), jnp.float32),
+        input_output_aliases={3: 0} if twin else {},
         scratch_shapes=[
-            pltpu.VMEM((count, width, width), jnp.float32),
+            pltpu.VMEM((count, half, width), jnp.float32),
             pltpu.SemaphoreType.DMA((count,)),
         ],
         compiler_params=pltpu.CompilerParams(vmem_limit_bytes=SMALL_VMEM),
-        name="decode",
-    )(kind, place, mine, other)
+        cost_estimate=pl.CostEstimate(
+            flops=count * half * width, bytes_accessed=6 * count * half * width, transcendentals=0
+        ),
+        name="decode_twin" if twin else "decode_own",
+    )(*in_smem(kind, core), coded, *((base,) if twin else ()))
 
 
 def body(
@@ -411,8 +439,8 @@
     side, cross, flip, far = partner_pairs(devices)
     place = core.reshape(1)
 
-    own_kind, own_slot, held_kind = tables(
-        shard_starts, block_owners, me, slot_count, owned_slots
+    own_kind, own_slot, held_kind, core_index = tables(
+        shard_starts, block_owners, jnp.stack((me, core)), slot_count, owned_slots
     )
     replica = gradients[0]
     twin = swap_cores(replica)
@@ -426,9 +454,9 @@
     mine = collect(own_kind, own_slot, (summed, by_side, by_cross, by_flip, by_far))
     other = swap_cores(mine)
     second, keep, to_side, to_cross, to_flip, to_far = soap_step(
-        own_kind, own_slot, place, mine, other, prepared, slot_count
+        own_kind, own_slot, core_index, mine, other, prepared, slot_count
     )
-    first_new, second_new = finish(own_kind, place, mine, other, first_moment, second)
+    first_new, second_new = finish(own_kind, core_index, mine, other, first_moment, second)
     sent = (
         keep,
         exchange(to_side, side),
@@ -437,7 +465,9 @@
         exchange(to_far, far),
     )
     coded = gather_held(held_kind, sent)
-    direction = decode(held_kind, place, coded, swap_cores(coded), width)
+    twin_coded = swap_cores(coded)
+    direction = decode(held_kind, core_index, coded, None, width)
+    direction = decode(held_kind, core_index, twin_coded, direction, width)
     return (direction, first_new, second_new)
 
 

time: 67.5 us -> 65.1 us (0.964)
  Pallas kernels: 18.9 us -> 16 us
    pallas_call x2 -> x3, Pallas kernels: 5.69 us -> 4.86 us  [the longest x1 3.18 us: soap_step(): pl.pallas_call(step_kernel, grid=(count // group,), in_specs=[pl.BlockSpe...]
    pallas_call x1, Pallas kernels: 0.8 us -> 0.01 us  [collect(): pl.pallas_call(collect_kernel, in_specs=[pl.BlockSpec(memory_space=pltpu....]
  transfers between devices with their start and end apart: 11 -> 11, of which waited for: 6 -> 6; matrix products, arithmetic and copies ran while one was open for 0% -> 0% of each run, Pallas kernels for 17% -> 18%
where the time goes in v4:
time: 65.1 us; the launch traced here: 64.8 us
  waiting for transfers between devices  29.8 us (46%)
  starting transfers between devices  18.3 us (28%)
  Pallas kernels  16 us (25%)
  between operations  0.73 us (1%)
    ppermute x8, waiting for transfers between devices, exchange(): return lax.ppermute(value, 'fsdp', pairs + [(b, a) for a, b in pairs])  29 us
    ppermute x8, starting transfers between devices, exchange(): return lax.ppermute(value, 'fsdp', pairs + [(b, a) for a, b in pairs])  15.5 us
    pallas_call x1, Pallas kernels, finish(): pl.pallas_call(finish_kernel, grid=(count,), in_specs=[pl.BlockSpec(memor...  4.89 us
    pallas_call x1, Pallas kernels, prepare(): pl.pallas_call(prepare_kernel, grid=(count // group,), in_specs=[pl.Block...  3.86 us
    pallas_call x1, Pallas kernels, soap_step(): pl.pallas_call(step_kernel, grid=(count // group,), in_specs=[pl.BlockSpe...  3.18 us
    ppermute x3, starting transfers between devices, swap_cores(): return lax.ppermute(value, 'dp', [(0, 1), (1, 0)])  2.81 us
    pallas_call x2, Pallas kernels, decode(): pl.pallas_call(functools.partial(decode_kernel, twin=twin), in_specs=[pl....  1.68 us
  transfers between devices with their start and end apart: 11, of which 6 were waited for; matrix products, arithmetic and copies ran while one was open for 0% of the time, Pallas kernels for 18%

profile of v4, /device:TPU:11, one launch (start us, length us, event | category | flops | bytes accessed | tf_op | source)
XLA Modules:
  0.0 64.8 jit_solution(11240787652790418009)
XLA Ops:
  0.6 0.7 %collective-permute-start = (bf16[4,256,256]{2,1,0:T(8,128)(2,1)}, bf16[4,256,256]{2,1,0:T(8,128)(2,1)S(1)}, u32[]{:S(2)}, u32[]{:S(2)}) collective-permute-start(bf16[4,256,256]{2,1,0:T(8,128)(2,1)} %bitcast.3), channel_id=1, source_target_pairs={{0,1},{1,0},{2,3},{3,2},{4,5},{5,4},{6,7},{7,6},{8,9},{9,8},{10,11... | collective-permute-start | bytes 1572872 | tf_op jit(solution)/shard_map/ppermute | solution.py:42
  1.4 1.0 %load_rows.1.mine_ref = bf16[4,128,256]{2,1,0:T(8,128)(2,1)S(1)} custom-call(s32[1]{0:T(128)} %bitcast.1.place_ref, bf16[4,256,256]{2,1,0:T(8,128)(2,1)} %bitcast.4), custom_call_target="tpu_custom_call" | custom-call | tf_op jit(solution)/shard_map/load_rows/pallas_call | solution.py:169
  2.3 0.8 %collective-permute-done.other_ref = bf16[4,256,256]{2,1,0:T(8,128)(2,1)S(1)} collective-permute-done((bf16[4,256,256]{2,1,0:T(8,128)(2,1)}, bf16[4,256,256]{2,1,0:T(8,128)(2,1)S(1)}, u32[]{:S(2)}, u32[]{:S(2)}) %collective-permute-start) | collective-permute-done | bytes 524320 | tf_op jit(solution)/shard_map/ppermute | solution.py:42
  3.1 0.1 add_replicas.1.refs_0_
  3.2 3.0 %collective-permute-start.4 = (bf16[4,128,256]{2,1,0:T(8,128)(2,1)S(1)}, bf16[4,128,256]{2,1,0:T(8,128)(2,1)S(1)}, u32[]{:S(2)}, u32[]{:S(2)}) collective-permute-start(bf16[4,128,256]{2,1,0:T(8,128)(2,1)S(1)} %add_replicas.1.refs_0_), channel_id=1, source_target_pairs={{4,8},{6,10},{12,16},{14,18},{20,24},{22,26},{8,4},{10,6},{16,12},... | collective-permute-start | bytes 786440 | tf_op jit(solution)/shard_map/ppermute | solution.py:30
  6.2 1.4 %collective-permute-start.3 = (bf16[4,128,256]{2,1,0:T(8,128)(2,1)S(1)}, bf16[4,128,256]{2,1,0:T(8,128)(2,1)S(1)}, u32[]{:S(2)}, u32[]{:S(2)}) collective-permute-start(bf16[4,128,256]{2,1,0:T(8,128)(2,1)S(1)} %add_replicas.1.refs_0_), channel_id=1, source_target_pairs={{0,4},{2,6},{8,12},{10,14},{16,20},{18,22},{24,28},{26,30},{4,0},{... | collective-permute-start | bytes 786440 | tf_op jit(solution)/shard_map/ppermute | solution.py:30
  7.6 2.0 %collective-permute-start.2 = (bf16[4,128,256]{2,1,0:T(8,128)(2,1)S(1)}, bf16[4,128,256]{2,1,0:T(8,128)(2,1)S(1)}, u32[]{:S(2)}, u32[]{:S(2)}) collective-permute-start(bf16[4,128,256]{2,1,0:T(8,128)(2,1)S(1)} %add_replicas.1.refs_0_), channel_id=1, source_target_pairs={{2,4},{6,8},{10,12},{14,16},{18,20},{22,24},{26,28},{4,2},{8,6},{1... | collective-permute-start | bytes 786440 | tf_op jit(solution)/shard_map/ppermute | solution.py:30
  9.6 1.1 %collective-permute-start.1 = (bf16[4,128,256]{2,1,0:T(8,128)(2,1)S(1)}, bf16[4,128,256]{2,1,0:T(8,128)(2,1)S(1)}, u32[]{:S(2)}, u32[]{:S(2)}) collective-permute-start(bf16[4,128,256]{2,1,0:T(8,128)(2,1)S(1)} %add_replicas.1.refs_0_), channel_id=1, source_target_pairs={{0,2},{4,6},{8,10},{12,14},{16,18},{20,22},{24,26},{28,30},{2,0},{... | collective-permute-start | bytes 786440 | tf_op jit(solution)/shard_map/ppermute | solution.py:30
  10.7 0.1 pad_add_fusion.at_ref
  10.8 1.2 %tables.1 = (s32[6]{0:T(128)S(4)}, s32[6]{0:T(128)S(4)}, s32[4]{0:T(128)S(4)}, s32[1]{0:T(128)S(4)}) custom-call(s32[2]{0:T(128)S(1)} %pad_add_fusion.at_ref, s32[16]{0:T(128)} %starts_ref.1, s32[48]{0:T(128)} %owners_ref.1), custom_call_target="tpu_custom_call" | custom-call | tf_op jit(solution)/shard_map/tables/pallas_call | solution.py:94
  12.0 1.7 %collective-permute-done.4.refs_4_ = bf16[4,128,256]{2,1,0:T(8,128)(2,1)S(1)} collective-permute-done((bf16[4,128,256]{2,1,0:T(8,128)(2,1)S(1)}, bf16[4,128,256]{2,1,0:T(8,128)(2,1)S(1)}, u32[]{:S(2)}, u32[]{:S(2)}) %collective-permute-start.4) | collective-permute-done | bytes 262176 | tf_op jit(solution)/shard_map/ppermute | solution.py:30
  13.6 11.8 %collective-permute-done.3.refs_3_ = bf16[4,128,256]{2,1,0:T(8,128)(2,1)S(1)} collective-permute-done((bf16[4,128,256]{2,1,0:T(8,128)(2,1)S(1)}, bf16[4,128,256]{2,1,0:T(8,128)(2,1)S(1)}, u32[]{:S(2)}, u32[]{:S(2)}) %collective-permute-start.3) | collective-permute-done | bytes 262176 | tf_op jit(solution)/shard_map/ppermute | solution.py:30
  25.4 0.0 collective-permute-done.2.refs_2_
  25.4 0.0 collective-permute-done.1.refs_1_
  25.4 0.6 collective-permute-start.5
  26.0 3.9 %prepare.1 = (f32[6,256,256]{2,1,0:T(8,128)S(1)}, f32[6,256,256]{2,1,0:T(8,128)S(1)}, bf16[6,256,256]{2,1,0:T(8,128)(2,1)S(1)}, bf16[6,256,256]{2,1,0:T(8,128)(2...) custom-call(s32[1]{0:T(128)} %bitcast.1.place_ref, ...), custom_call_target="tpu_custom_call" | custom-call | flops 1207959552 | bytes 6291456 | tf_op jit(solution)/shard_map/prepare/pallas_call | solution.py:149
  29.9 0.0 collective-permute-done.5.other_ref
  29.9 3.2 %soap_step.1 = (f32[6,256,256]{2,1,0:T(8,128)S(1)}, s16[520,256]{1,0:T(8,128)(2,1)S(1)}, s16[520,256]{1,0:T(8,128)(2,1)S(1)}, s16[520,256]{1,0:T(8,128)(2,1)S(1)...) custom-call(s32[6]{0:T(128)S(4)} %get-tuple-element.25.kind_ref, s32[6]{0:T(128)S(4)} %get-tuple-element.26.slot_ref, ...), custom_call_target="tpu_custom_call" | custom-call | tf_op jit(solution)/shard_map/soap_step/pallas_call | solution.py:303
  33.1 0.3 collective-permute-start.6
  33.4 4.3 %collective-permute-start.7 = (s16[520,256]{1,0:T(8,128)(2,1)S(1)}, s16[520,256]{1,0:T(8,128)(2,1)S(1)}, u32[]{:S(2)}, u32[]{:S(2)}) collective-permute-start(s16[520,256]{1,0:T(8,128)(2,1)S(1)} %get-tuple-element.37), channel_id=1, source_target_pairs={{2,4},{6,8},{10,12},{14,16},{18,20},{22,24},{26,28},{4,2},{8,6},{1... | collective-permute-start | bytes 798728 | tf_op jit(solution)/shard_map/ppermute | solution.py:30
  37.7 1.3 %collective-permute-start.8 = (s16[520,256]{1,0:T(8,128)(2,1)S(1)}, s16[520,256]{1,0:T(8,128)(2,1)S(1)}, u32[]{:S(2)}, u32[]{:S(2)}) collective-permute-start(s16[520,256]{1,0:T(8,128)(2,1)S(1)} %get-tuple-element.38), channel_id=1, source_target_pairs={{0,4},{2,6},{8,12},{10,14},{16,20},{18,22},{24,28},{26,30},{4,0},{... | collective-permute-start | bytes 798728 | tf_op jit(solution)/shard_map/ppermute | solution.py:30
  39.0 2.0 %collective-permute-start.9 = (s16[520,256]{1,0:T(8,128)(2,1)S(1)}, s16[520,256]{1,0:T(8,128)(2,1)S(1)}, u32[]{:S(2)}, u32[]{:S(2)}) collective-permute-start(s16[520,256]{1,0:T(8,128)(2,1)S(1)} %get-tuple-element.39), channel_id=1, source_target_pairs={{4,8},{6,10},{12,16},{14,18},{20,24},{22,26},{8,4},{10,6},{16,12},... | collective-permute-start | bytes 798728 | tf_op jit(solution)/shard_map/ppermute | solution.py:30
  41.1 5.6 %collective-permute-done.6.refs_1_ = s16[520,256]{1,0:T(8,128)(2,1)S(1)} collective-permute-done((s16[520,256]{1,0:T(8,128)(2,1)S(1)}, s16[520,256]{1,0:T(8,128)(2,1)S(1)}, u32[]{:S(2)}, u32[]{:S(2)}) %collective-permute-start.6) | collective-permute-done | bytes 266272 | tf_op jit(solution)/shard_map/ppermute | solution.py:30
  46.7 3.5 %collective-permute-done.7.refs_2_ = s16[520,256]{1,0:T(8,128)(2,1)S(1)} collective-permute-done((s16[520,256]{1,0:T(8,128)(2,1)S(1)}, s16[520,256]{1,0:T(8,128)(2,1)S(1)}, u32[]{:S(2)}, u32[]{:S(2)}) %collective-permute-start.7) | collective-permute-done | bytes 266272 | tf_op jit(solution)/shard_map/ppermute | solution.py:30
  50.1 6.4 %collective-permute-done.8.refs_3_ = s16[520,256]{1,0:T(8,128)(2,1)S(1)} collective-permute-done((s16[520,256]{1,0:T(8,128)(2,1)S(1)}, s16[520,256]{1,0:T(8,128)(2,1)S(1)}, u32[]{:S(2)}, u32[]{:S(2)}) %collective-permute-start.8) | collective-permute-done | bytes 266272 | tf_op jit(solution)/shard_map/ppermute | solution.py:30
  56.6 0.0 collective-permute-done.9.refs_4_
  56.6 0.1 gather_held.1.coded_ref
  56.7 1.5 %collective-permute-start.10 = (s16[520,256]{1,0:T(8,128)(2,1)S(1)}, s16[520,256]{1,0:T(8,128)(2,1)S(1)}, u32[]{:S(2)}, u32[]{:S(2)}) collective-permute-start(s16[520,256]{1,0:T(8,128)(2,1)S(1)} %gather_held.1.coded_ref), channel_id=1, source_target_pairs={{0,1},{1,0},{2,3},{3,2},{4,5},{5,4},{6,7},{7,6},{8,9},{9,8},{10,11... | collective-permute-start | bytes 798728 | tf_op jit(solution)/shard_map/ppermute | solution.py:42
  58.2 4.9 %finish.1 = (f32[6,256,256]{2,1,0:T(8,128)}, f32[6,256,256]{2,1,0:T(8,128)}) custom-call(s32[6]{0:T(128)S(4)} %get-tuple-element.25.kind_ref, s32[1]{0:T(128)S(4)} %get-tuple-element.24.place_ref.core_ref, bf16[6,128,256]{2,1,0:T(8,128)(2,1)S(1)} %collect.1.mine_ref, bf16[6,128,256]{2,1,0:T(8,128)(2,1)S(1)} %collective-permute-done.5.other_ref, ...), custom_call_target="tpu_custom_call" | custom-call | flops 4718592 | bytes 4718592 | tf_op jit(solution)/shard_map/finish/pallas_call | solution.py:340
  63.1 0.8 %decode_own.1.refs_0_ = f32[4,256,256]{2,1,0:T(8,128)} custom-call(s32[4]{0:T(128)S(4)} %get-tuple-element.23.kind_ref, s32[1]{0:T(128)S(4)} %get-tuple-element.24.place_ref.core_ref, s16[520,256]{1,0:T(8,128)(2,1)S(1)} %gather_held.1.coded_ref), custom_call_target="tpu_custom_call" | custom-call | flops 131072 | bytes 786432 | tf_op jit(solution)/shard_map/decode_own/pallas_call | solution.py:410
  64.0 0.0 collective-permute-done.10.coded_ref
  64.0 0.8 %decode_twin.1 = f32[4,256,256]{2,1,0:T(8,128)} custom-call(s32[4]{0:T(128)S(4)} %get-tuple-element.23.kind_ref, s32[1]{0:T(128)S(4)} %get-tuple-element.24.place_ref.core_ref, s16[520,256]{1,0:T(8,128)(2,1)S(1)} %collective-permute-done.10.coded_ref, f32[4,256,256]{2,1,0:T(8,128)} %decode_own.1.refs_0_), custom_call_target="tpu_custom_call", output_to_operand_aliasing={{}: (3, {})} | custom-call | flops 131072 | bytes 786432 | tf_op jit(solution)/shard_map/decode_twin/pallas_call | solution.py:410
  (1 shorter events, 0.0 us)
Async XLA Ops:
  0.6 2.5 %collective-permute-start = (bf16[4,256,256]{2,1,0:T(8,128)(2,1)}, bf16[4,256,256]{2,1,0:T(8,128)(2,1)S(1)}, u32[]{:S(2)}, u32[]{:S(2)}) collective-permute-start(bf16[4,256,256]{2,1,0:T(8,128)(2,1)} %bitcast.3), channel_id=1, source_target_pairs={{0,1},{1,0},{2,3},{3,2},{4,5},{5,4},{6,7},{7,6},{8,9},{9,8},{10,11... | collective-permute-start | bytes 1572872 | tf_op jit(solution)/shard_map/ppermute | solution.py:42
  3.2 10.5 %collective-permute-start.4 = (bf16[4,128,256]{2,1,0:T(8,128)(2,1)S(1)}, bf16[4,128,256]{2,1,0:T(8,128)(2,1)S(1)}, u32[]{:S(2)}, u32[]{:S(2)}) collective-permute-start(bf16[4,128,256]{2,1,0:T(8,128)(2,1)S(1)} %add_replicas.1.refs_0_), channel_id=1, source_target_pairs={{4,8},{6,10},{12,16},{14,18},{20,24},{22,26},{8,4},{10,6},{16,12},... | collective-permute-start | bytes 786440 | tf_op jit(solution)/shard_map/ppermute | solution.py:30
  6.2 19.2 %collective-permute-start.3 = (bf16[4,128,256]{2,1,0:T(8,128)(2,1)S(1)}, bf16[4,128,256]{2,1,0:T(8,128)(2,1)S(1)}, u32[]{:S(2)}, u32[]{:S(2)}) collective-permute-start(bf16[4,128,256]{2,1,0:T(8,128)(2,1)S(1)} %add_replicas.1.refs_0_), channel_id=1, source_target_pairs={{0,4},{2,6},{8,12},{10,14},{16,20},{18,22},{24,28},{26,30},{4,0},{... | collective-permute-start | bytes 786440 | tf_op jit(solution)/shard_map/ppermute | solution.py:30
  7.6 17.8 %collective-permute-start.2 = (bf16[4,128,256]{2,1,0:T(8,128)(2,1)S(1)}, bf16[4,128,256]{2,1,0:T(8,128)(2,1)S(1)}, u32[]{:S(2)}, u32[]{:S(2)}) collective-permute-start(bf16[4,128,256]{2,1,0:T(8,128)(2,1)S(1)} %add_replicas.1.refs_0_), channel_id=1, source_target_pairs={{2,4},{6,8},{10,12},{14,16},{18,20},{22,24},{26,28},{4,2},{8,6},{1... | collective-permute-start | bytes 786440 | tf_op jit(solution)/shard_map/ppermute | solution.py:30
  9.6 15.8 %collective-permute-start.1 = (bf16[4,128,256]{2,1,0:T(8,128)(2,1)S(1)}, bf16[4,128,256]{2,1,0:T(8,128)(2,1)S(1)}, u32[]{:S(2)}, u32[]{:S(2)}) collective-permute-start(bf16[4,128,256]{2,1,0:T(8,128)(2,1)S(1)} %add_replicas.1.refs_0_), channel_id=1, source_target_pairs={{0,2},{4,6},{8,10},{12,14},{16,18},{20,22},{24,26},{28,30},{2,0},{... | collective-permute-start | bytes 786440 | tf_op jit(solution)/shard_map/ppermute | solution.py:30
  25.4 4.4 %collective-permute-start.5 = (bf16[6,128,256]{2,1,0:T(8,128)(2,1)S(1)}, bf16[6,128,256]{2,1,0:T(8,128)(2,1)S(1)}, u32[]{:S(2)}, u32[]{:S(2)}) collective-permute-start(bf16[6,128,256]{2,1,0:T(8,128)(2,1)S(1)} %collect.1.mine_ref), channel_id=1, source_target_pairs={{0,1},{1,0},{2,3},{3,2},{4,5},{5,4},{6,7},{7,6},{8,9},{9,8},{10,11... | collective-permute-start | bytes 1179656 | tf_op jit(solution)/shard_map/ppermute | solution.py:42
  33.1 13.6 %collective-permute-start.6 = (s16[520,256]{1,0:T(8,128)(2,1)S(1)}, s16[520,256]{1,0:T(8,128)(2,1)S(1)}, u32[]{:S(2)}, u32[]{:S(2)}) collective-permute-start(s16[520,256]{1,0:T(8,128)(2,1)S(1)} %get-tuple-element.36), channel_id=1, source_target_pairs={{0,2},{4,6},{8,10},{12,14},{16,18},{20,22},{24,26},{28,30},{2,0},{... | collective-permute-start | bytes 798728 | tf_op jit(solution)/shard_map/ppermute | solution.py:30
  33.4 16.7 %collective-permute-start.7 = (s16[520,256]{1,0:T(8,128)(2,1)S(1)}, s16[520,256]{1,0:T(8,128)(2,1)S(1)}, u32[]{:S(2)}, u32[]{:S(2)}) collective-permute-start(s16[520,256]{1,0:T(8,128)(2,1)S(1)} %get-tuple-element.37), channel_id=1, source_target_pairs={{2,4},{6,8},{10,12},{14,16},{18,20},{22,24},{26,28},{4,2},{8,6},{1... | collective-permute-start | bytes 798728 | tf_op jit(solution)/shard_map/ppermute | solution.py:30
  37.7 18.8 %collective-permute-start.8 = (s16[520,256]{1,0:T(8,128)(2,1)S(1)}, s16[520,256]{1,0:T(8,128)(2,1)S(1)}, u32[]{:S(2)}, u32[]{:S(2)}) collective-permute-start(s16[520,256]{1,0:T(8,128)(2,1)S(1)} %get-tuple-element.38), channel_id=1, source_target_pairs={{0,4},{2,6},{8,12},{10,14},{16,20},{18,22},{24,28},{26,30},{4,0},{... | collective-permute-start | bytes 798728 | tf_op jit(solution)/shard_map/ppermute | solution.py:30
  39.0 17.5 %collective-permute-start.9 = (s16[520,256]{1,0:T(8,128)(2,1)S(1)}, s16[520,256]{1,0:T(8,128)(2,1)S(1)}, u32[]{:S(2)}, u32[]{:S(2)}) collective-permute-start(s16[520,256]{1,0:T(8,128)(2,1)S(1)} %get-tuple-element.39), channel_id=1, source_target_pairs={{4,8},{6,10},{12,16},{14,18},{20,24},{22,26},{8,4},{10,6},{16,12},... | collective-permute-start | bytes 798728 | tf_op jit(solution)/shard_map/ppermute | solution.py:30
  56.7 7.2 %collective-permute-start.10 = (s16[520,256]{1,0:T(8,128)(2,1)S(1)}, s16[520,256]{1,0:T(8,128)(2,1)S(1)}, u32[]{:S(2)}, u32[]{:S(2)}) collective-permute-start(s16[520,256]{1,0:T(8,128)(2,1)S(1)} %gather_held.1.coded_ref), channel_id=1, source_target_pairs={{0,1},{1,0},{2,3},{3,2},{4,5},{5,4},{6,7},{7,6},{8,9},{9,8},{10,11... | collective-permute-start | bytes 798728 | tf_op jit(solution)/shard_map/ppermute | solution.py:42

commit v5 on v4

--- a/solution.py
+++ b/solution.py
@@ -223,11 +223,33 @@
     )(*in_smem(kind, slot), *sources)
 
 
-def step_kernel(kind_ref, slot_ref, place_ref, mine_ref, other_ref, *refs):
+def rotate_kernel(mine_ref, right_high, right_low, high_ref, low_ref):
+    for g in range(mine_ref.shape[0]):
+        gradient = mine_ref[g]
+        turned = product(gradient, right_high[g], NN) + product(gradient, right_low[g], NN)
+        high_ref[g], low_ref[g] = split(turned)
+
+
+def rotate_rows(mine, prepared):
+    right = prepared[4:6]
+    return pl.pallas_call(
+        rotate_kernel,
+        in_specs=[pl.BlockSpec(memory_space=pltpu.VMEM)] * 3,
+        out_specs=[pl.BlockSpec(memory_space=pltpu.VMEM)] * 2,
+        out_shape=[pltpu.VMEM(mine.shape, jnp.bfloat16)] * 2,
+        compiler_params=pltpu.CompilerParams(vmem_limit_bytes=SMALL_VMEM),
+        cost_estimate=pl.CostEstimate(
+            flops=4 * mine.size * mine.shape[2], bytes_accessed=6 * mine.size, transcendentals=0
+        ),
+        name="rotate_rows",
+    )(*in_vmem(mine, *right))
+
+
+def step_kernel(kind_ref, slot_ref, place_ref, mine_high, mine_low, other_ref, *refs):
     turned_ref, second_ref, flip_high, flip_low, right_high, right_low, row_high, row_low = refs[:8]
-    second_out, sends, codes, grads = refs[8], refs[9:14], refs[14], refs[15]
+    second_out, sends, codes, first_high, first_low = refs[8], refs[9:14], *refs[14:]
     step = pl.program_id(0)
-    group, half = mine_ref.shape[:2]
+    group, half = other_ref.shape[:2]
     here = pl.multiple_of(place_ref[0] * half, half)
     there = pl.multiple_of((1 - place_ref[0]) * half, half)
     every = range(group)
@@ -240,13 +262,15 @@
     at = [dict() for _ in every]
 
     def rotate_right(g):
-        grads[g, pl.ds(here, half)] = mine_ref[g]
-        grads[g, pl.ds(there, half)] = other_ref[g]
-        wide = jnp.concatenate((grads[g],) * 2, axis=1)
-        at[g]["first"] = product(wide, jnp.concatenate((right_high[g], right_low[g]), axis=0), NN)
+        gradient = other_ref[g]
+        turned = product(gradient, right_high[g], NN) + product(gradient, right_low[g], NN)
+        high, low = split(turned)
+        first_high[g, pl.ds(here, half)], first_low[g, pl.ds(here, half)] = mine_high[g], mine_low[g]
+        first_high[g, pl.ds(there, half)], first_low[g, pl.ds(there, half)] = high, low
 
     def rotate_left(g):
-        at[g]["turned"] = product3((flip_high[g], flip_low[g]), split(at[g].pop("first")), NN)
+        first = (first_high[g], first_low[g])
+        at[g]["turned"] = product3((flip_high[g], flip_low[g]), first, NN)
 
     def scale(g):
         turned = at[g].pop("turned")
@@ -263,12 +287,16 @@
     def return_right(g):
         at[g]["update"] = product3(split(at[g].pop("back")), (right_high[g], right_low[g]), NT)
 
-    def code_update(g):
+    def quantize(g):
         update = at[g].pop("update")
         peak = jnp.max(jnp.abs(update), axis=0, keepdims=True)
         code = jnp.ceil(jnp.log2(jnp.maximum(peak, 1e-30) * (1.0 / 32000.0)) * CODE_STEPS)
         coded = jnp.round(update * jnp.exp2(code * (-1.0 / CODE_STEPS)))
-        coded = jnp.clip(coded, -32767.0, 32767.0).astype(jnp.int32).astype(jnp.int16)
+        at[g]["coded"] = jnp.clip(coded, -32767.0, 32767.0).astype(jnp.int32).astype(jnp.int16)
+        at[g]["code"] = code.astype(jnp.int32)
+
+    def deliver(g):
+        coded, code = at[g].pop("coded"), at[g].pop("code")
         slot = slot_ref[step * group + g]
         rows = pl.ds(pl.multiple_of(slot * half, half), half)
         for kind in range(5):
@@ -276,15 +304,15 @@
             @pl.when(kind_ref[step * group + g] == kind)
             def _():
                 sends[kind][rows] = coded
-                codes[kind] = jnp.where(spots == slot, code.astype(jnp.int32), codes[kind])
-
-    stages = (rotate_right, rotate_left, scale, return_left, return_right)
+                codes[kind] = jnp.where(spots == slot, code, codes[kind])
+
+    stages = (rotate_right, rotate_left, scale, return_left, return_right, quantize)
     for wave in range(group + len(stages) - 1):
         for depth in reversed(range(len(stages))):
             if 0 <= wave - depth < group:
                 stages[depth](wave - depth)
     for g in every:
-        code_update(g)
+        deliver(g)
 
     @pl.when(step == pl.num_programs(0) - 1)
     def _():
@@ -293,8 +321,8 @@
             sends[kind][pl.ds(top, CODE_ROWS)] = codes[kind].astype(jnp.int16)
 
 
-def soap_step(kind, slot, place, mine, other, prepared, slot_count):
-    count, half, width = mine.shape
+def soap_step(kind, slot, place, rotated, other, prepared, slot_count):
+    count, half, width = other.shape
     group = GROUP if count % GROUP == 0 else 1
     full = pl.BlockSpec((group, width, width), lambda j: (j, 0, 0))
     part = pl.BlockSpec((group, half, width), lambda j: (j, 0, 0))
@@ -304,19 +332,20 @@
         step_kernel,
         grid=(count // group,),
         in_specs=[pl.BlockSpec(memory_space=pltpu.SMEM)] * 3
-        + [part, part]
+        + [part] * 3
         + [full] * 6
         + [part] * 2,
         out_specs=[full] + [send] * 5,
         scratch_shapes=[
             pltpu.VMEM((5, CODE_ROWS, width), jnp.int32),
             pltpu.VMEM((group, width, width), jnp.bfloat16),
+            pltpu.VMEM((group, width, width), jnp.bfloat16),
         ],
         out_shape=[pltpu.VMEM((count, width, width), jnp.float32)]
         + [pltpu.VMEM((send_rows, width), jnp.int16)] * 5,
         compiler_params=pltpu.CompilerParams(vmem_limit_bytes=STEP_VMEM),
         name="soap_step",
-    )(*in_smem(kind, slot, place), *in_vmem(mine, other, *prepared))
+    )(*in_smem(kind, slot, place), *in_vmem(*rotated, other, *prepared))
 
 
 def finish_kernel(kind_ref, place_ref, mine_ref, other_ref, moment_ref, second_ref, *outs):
@@ -454,7 +483,7 @@
     mine = collect(own_kind, own_slot, (summed, by_side, by_cross, by_flip, by_far))
     other = swap_cores(mine)
     second, keep, to_side, to_cross, to_flip, to_far = soap_step(
-        own_kind, own_slot, core_index, mine, other, prepared, slot_count
+        own_kind, own_slot, core_index, rotate_rows(mine, prepared), other, prepared, slot_count
     )
     first_new, second_new = finish(own_kind, core_index, mine, other, first_moment, second)
     sent = (

time: 65.1 us -> 65.2 us (level)
  transfers between devices with their start and end apart: 11 -> 11, of which waited for: 6 -> 6; matrix products, arithmetic and copies ran while one was open for 0% -> 0% of each run, Pallas kernels for 18% -> 19%
where the time goes in v5:
time: 65.2 us; the launch traced here: 64.9 us
  waiting for transfers between devices  29.7 us (46%)
  starting transfers between devices  18.3 us (28%)
  Pallas kernels  16 us (25%)
  between operations  0.74 us (1%)
    ppermute x8, waiting for transfers between devices, exchange(): return lax.ppermute(value, 'fsdp', pairs + [(b, a) for a, b in pairs])  29 us
    ppermute x8, starting transfers between devices, exchange(): return lax.ppermute(value, 'fsdp', pairs + [(b, a) for a, b in pairs])  15.5 us
    pallas_call x1, Pallas kernels, finish(): pl.pallas_call(finish_kernel, grid=(count,), in_specs=[pl.BlockSpec(memor...  4.89 us
    pallas_call x1, Pallas kernels, prepare(): pl.pallas_call(prepare_kernel, grid=(count // group,), in_specs=[pl.Block...  3.86 us
    pallas_call x1, Pallas kernels, soap_step(): pl.pallas_call(step_kernel, grid=(count // group,), in_specs=[pl.BlockSpe...  2.87 us
    ppermute x3, starting transfers between devices, swap_cores(): return lax.ppermute(value, 'dp', [(0, 1), (1, 0)])  2.81 us
    pallas_call x2, Pallas kernels, decode(): pl.pallas_call(functools.partial(decode_kernel, twin=twin), in_specs=[pl....  1.68 us
  transfers between devices with their start and end apart: 11, of which 6 were waited for; matrix products, arithmetic and copies ran while one was open for 0% of the time, Pallas kernels for 19%

profile of v5, /device:TPU:11, one launch (start us, length us, event | category | flops | bytes accessed | tf_op | source)
XLA Modules:
  0.0 64.9 jit_solution(2069597029839840766)
XLA Ops:
  0.6 0.7 %collective-permute-start = (bf16[4,256,256]{2,1,0:T(8,128)(2,1)}, bf16[4,256,256]{2,1,0:T(8,128)(2,1)S(1)}, u32[]{:S(2)}, u32[]{:S(2)}) collective-permute-start(bf16[4,256,256]{2,1,0:T(8,128)(2,1)} %bitcast.3), channel_id=1, source_target_pairs={{0,1},{1,0},{2,3},{3,2},{4,5},{5,4},{6,7},{7,6},{8,9},{9,8},{10,11... | collective-permute-start | bytes 1572872 | tf_op jit(solution)/shard_map/ppermute | solution.py:42
  1.4 1.0 %load_rows.1.mine_ref = bf16[4,128,256]{2,1,0:T(8,128)(2,1)S(1)} custom-call(s32[1]{0:T(128)} %bitcast.1.place_ref, bf16[4,256,256]{2,1,0:T(8,128)(2,1)} %bitcast.4), custom_call_target="tpu_custom_call" | custom-call | tf_op jit(solution)/shard_map/load_rows/pallas_call | solution.py:169
  2.3 0.8 %collective-permute-done.other_ref = bf16[4,256,256]{2,1,0:T(8,128)(2,1)S(1)} collective-permute-done((bf16[4,256,256]{2,1,0:T(8,128)(2,1)}, bf16[4,256,256]{2,1,0:T(8,128)(2,1)S(1)}, u32[]{:S(2)}, u32[]{:S(2)}) %collective-permute-start) | collective-permute-done | bytes 524320 | tf_op jit(solution)/shard_map/ppermute | solution.py:42
  3.1 0.1 add_replicas.1.refs_0_
  3.2 3.0 %collective-permute-start.4 = (bf16[4,128,256]{2,1,0:T(8,128)(2,1)S(1)}, bf16[4,128,256]{2,1,0:T(8,128)(2,1)S(1)}, u32[]{:S(2)}, u32[]{:S(2)}) collective-permute-start(bf16[4,128,256]{2,1,0:T(8,128)(2,1)S(1)} %add_replicas.1.refs_0_), channel_id=1, source_target_pairs={{4,8},{6,10},{12,16},{14,18},{20,24},{22,26},{8,4},{10,6},{16,12},... | collective-permute-start | bytes 786440 | tf_op jit(solution)/shard_map/ppermute | solution.py:30
  6.2 1.4 %collective-permute-start.3 = (bf16[4,128,256]{2,1,0:T(8,128)(2,1)S(1)}, bf16[4,128,256]{2,1,0:T(8,128)(2,1)S(1)}, u32[]{:S(2)}, u32[]{:S(2)}) collective-permute-start(bf16[4,128,256]{2,1,0:T(8,128)(2,1)S(1)} %add_replicas.1.refs_0_), channel_id=1, source_target_pairs={{0,4},{2,6},{8,12},{10,14},{16,20},{18,22},{24,28},{26,30},{4,0},{... | collective-permute-start | bytes 786440 | tf_op jit(solution)/shard_map/ppermute | solution.py:30
  7.6 2.0 %collective-permute-start.2 = (bf16[4,128,256]{2,1,0:T(8,128)(2,1)S(1)}, bf16[4,128,256]{2,1,0:T(8,128)(2,1)S(1)}, u32[]{:S(2)}, u32[]{:S(2)}) collective-permute-start(bf16[4,128,256]{2,1,0:T(8,128)(2,1)S(1)} %add_replicas.1.refs_0_), channel_id=1, source_target_pairs={{2,4},{6,8},{10,12},{14,16},{18,20},{22,24},{26,28},{4,2},{8,6},{1... | collective-permute-start | bytes 786440 | tf_op jit(solution)/shard_map/ppermute | solution.py:30
  9.6 1.1 %collective-permute-start.1 = (bf16[4,128,256]{2,1,0:T(8,128)(2,1)S(1)}, bf16[4,128,256]{2,1,0:T(8,128)(2,1)S(1)}, u32[]{:S(2)}, u32[]{:S(2)}) collective-permute-start(bf16[4,128,256]{2,1,0:T(8,128)(2,1)S(1)} %add_replicas.1.refs_0_), channel_id=1, source_target_pairs={{0,2},{4,6},{8,10},{12,14},{16,18},{20,22},{24,26},{28,30},{2,0},{... | collective-permute-start | bytes 786440 | tf_op jit(solution)/shard_map/ppermute | solution.py:30
  10.7 0.1 pad_add_fusion.at_ref
  10.8 1.2 %tables.1 = (s32[6]{0:T(128)S(4)}, s32[6]{0:T(128)S(4)}, s32[4]{0:T(128)S(4)}, s32[1]{0:T(128)S(4)}) custom-call(s32[2]{0:T(128)S(1)} %pad_add_fusion.at_ref, s32[16]{0:T(128)} %starts_ref.1, s32[48]{0:T(128)} %owners_ref.1), custom_call_target="tpu_custom_call" | custom-call | tf_op jit(solution)/shard_map/tables/pallas_call | solution.py:94
  12.0 1.7 %collective-permute-done.4.refs_4_ = bf16[4,128,256]{2,1,0:T(8,128)(2,1)S(1)} collective-permute-done((bf16[4,128,256]{2,1,0:T(8,128)(2,1)S(1)}, bf16[4,128,256]{2,1,0:T(8,128)(2,1)S(1)}, u32[]{:S(2)}, u32[]{:S(2)}) %collective-permute-start.4) | collective-permute-done | bytes 262176 | tf_op jit(solution)/shard_map/ppermute | solution.py:30
  13.6 11.8 %collective-permute-done.3.refs_3_ = bf16[4,128,256]{2,1,0:T(8,128)(2,1)S(1)} collective-permute-done((bf16[4,128,256]{2,1,0:T(8,128)(2,1)S(1)}, bf16[4,128,256]{2,1,0:T(8,128)(2,1)S(1)}, u32[]{:S(2)}, u32[]{:S(2)}) %collective-permute-start.3) | collective-permute-done | bytes 262176 | tf_op jit(solution)/shard_map/ppermute | solution.py:30
  25.4 0.0 collective-permute-done.2.refs_2_
  25.4 0.0 collective-permute-done.1.refs_1_
  25.4 0.6 collective-permute-start.5
  26.0 3.9 %prepare.1 = (f32[6,256,256]{2,1,0:T(8,128)S(1)}, f32[6,256,256]{2,1,0:T(8,128)S(1)}, bf16[6,256,256]{2,1,0:T(8,128)(2,1)S(1)}, bf16[6,256,256]{2,1,0:T(8,128)(2...) custom-call(s32[1]{0:T(128)} %bitcast.1.place_ref, ...), custom_call_target="tpu_custom_call" | custom-call | flops 1207959552 | bytes 6291456 | tf_op jit(solution)/shard_map/prepare/pallas_call | solution.py:149
  29.9 0.4 rotate_rows.1
  30.3 2.9 %soap_step.1 = (f32[6,256,256]{2,1,0:T(8,128)S(1)}, s16[520,256]{1,0:T(8,128)(2,1)S(1)}, s16[520,256]{1,0:T(8,128)(2,1)S(1)}, s16[520,256]{1,0:T(8,128)(2,1)S(1)...) custom-call(s32[6]{0:T(128)S(4)} %get-tuple-element.27.kind_ref, s32[6]{0:T(128)S(4)} %get-tuple-element.28.slot_ref, ...), custom_call_target="tpu_custom_call" | custom-call | tf_op jit(solution)/shard_map/soap_step/pallas_call | solution.py:331
  33.1 0.4 collective-permute-start.6
  33.5 4.3 %collective-permute-start.7 = (s16[520,256]{1,0:T(8,128)(2,1)S(1)}, s16[520,256]{1,0:T(8,128)(2,1)S(1)}, u32[]{:S(2)}, u32[]{:S(2)}) collective-permute-start(s16[520,256]{1,0:T(8,128)(2,1)S(1)} %get-tuple-element.41), channel_id=1, source_target_pairs={{2,4},{6,8},{10,12},{14,16},{18,20},{22,24},{26,28},{4,2},{8,6},{1... | collective-permute-start | bytes 798728 | tf_op jit(solution)/shard_map/ppermute | solution.py:30
  37.8 1.3 %collective-permute-start.8 = (s16[520,256]{1,0:T(8,128)(2,1)S(1)}, s16[520,256]{1,0:T(8,128)(2,1)S(1)}, u32[]{:S(2)}, u32[]{:S(2)}) collective-permute-start(s16[520,256]{1,0:T(8,128)(2,1)S(1)} %get-tuple-element.42), channel_id=1, source_target_pairs={{0,4},{2,6},{8,12},{10,14},{16,20},{18,22},{24,28},{26,30},{4,0},{... | collective-permute-start | bytes 798728 | tf_op jit(solution)/shard_map/ppermute | solution.py:30
  39.1 2.0 %collective-permute-start.9 = (s16[520,256]{1,0:T(8,128)(2,1)S(1)}, s16[520,256]{1,0:T(8,128)(2,1)S(1)}, u32[]{:S(2)}, u32[]{:S(2)}) collective-permute-start(s16[520,256]{1,0:T(8,128)(2,1)S(1)} %get-tuple-element.43), channel_id=1, source_target_pairs={{4,8},{6,10},{12,16},{14,18},{20,24},{22,26},{8,4},{10,6},{16,12},... | collective-permute-start | bytes 798728 | tf_op jit(solution)/shard_map/ppermute | solution.py:30
  41.2 5.6 %collective-permute-done.6.refs_1_ = s16[520,256]{1,0:T(8,128)(2,1)S(1)} collective-permute-done((s16[520,256]{1,0:T(8,128)(2,1)S(1)}, s16[520,256]{1,0:T(8,128)(2,1)S(1)}, u32[]{:S(2)}, u32[]{:S(2)}) %collective-permute-start.6) | collective-permute-done | bytes 266272 | tf_op jit(solution)/shard_map/ppermute | solution.py:30
  46.7 3.5 %collective-permute-done.7.refs_2_ = s16[520,256]{1,0:T(8,128)(2,1)S(1)} collective-permute-done((s16[520,256]{1,0:T(8,128)(2,1)S(1)}, s16[520,256]{1,0:T(8,128)(2,1)S(1)}, u32[]{:S(2)}, u32[]{:S(2)}) %collective-permute-start.7) | collective-permute-done | bytes 266272 | tf_op jit(solution)/shard_map/ppermute | solution.py:30
  50.2 6.4 %collective-permute-done.8.refs_3_ = s16[520,256]{1,0:T(8,128)(2,1)S(1)} collective-permute-done((s16[520,256]{1,0:T(8,128)(2,1)S(1)}, s16[520,256]{1,0:T(8,128)(2,1)S(1)}, u32[]{:S(2)}, u32[]{:S(2)}) %collective-permute-start.8) | collective-permute-done | bytes 266272 | tf_op jit(solution)/shard_map/ppermute | solution.py:30
  56.6 0.0 collective-permute-done.9.refs_4_
  56.6 0.1 gather_held.1.coded_ref
  56.8 1.5 %collective-permute-start.10 = (s16[520,256]{1,0:T(8,128)(2,1)S(1)}, s16[520,256]{1,0:T(8,128)(2,1)S(1)}, u32[]{:S(2)}, u32[]{:S(2)}) collective-permute-start(s16[520,256]{1,0:T(8,128)(2,1)S(1)} %gather_held.1.coded_ref), channel_id=1, source_target_pairs={{0,1},{1,0},{2,3},{3,2},{4,5},{5,4},{6,7},{7,6},{8,9},{9,8},{10,11... | collective-permute-start | bytes 798728 | tf_op jit(solution)/shard_map/ppermute | solution.py:42
  58.3 4.9 %finish.1 = (f32[6,256,256]{2,1,0:T(8,128)}, f32[6,256,256]{2,1,0:T(8,128)}) custom-call(s32[6]{0:T(128)S(4)} %get-tuple-element.27.kind_ref, s32[1]{0:T(128)S(4)} %get-tuple-element.26.place_ref.core_ref, bf16[6,128,256]{2,1,0:T(8,128)(2,1)S(1)} %collect.1.mine_ref, bf16[6,128,256]{2,1,0:T(8,128)(2,1)S(1)} %collective-permute-done.5.other_ref, ...), custom_call_target="tpu_custom_call" | custom-call | flops 4718592 | bytes 4718592 | tf_op jit(solution)/shard_map/finish/pallas_call | solution.py:369
  63.2 0.8 %decode_own.1.refs_0_ = f32[4,256,256]{2,1,0:T(8,128)} custom-call(s32[4]{0:T(128)S(4)} %get-tuple-element.25.kind_ref, s32[1]{0:T(128)S(4)} %get-tuple-element.26.place_ref.core_ref, s16[520,256]{1,0:T(8,128)(2,1)S(1)} %gather_held.1.coded_ref), custom_call_target="tpu_custom_call" | custom-call | flops 131072 | bytes 786432 | tf_op jit(solution)/shard_map/decode_own/pallas_call | solution.py:439
  64.0 0.0 collective-permute-done.10.coded_ref
  64.1 0.8 %decode_twin.1 = f32[4,256,256]{2,1,0:T(8,128)} custom-call(s32[4]{0:T(128)S(4)} %get-tuple-element.25.kind_ref, s32[1]{0:T(128)S(4)} %get-tuple-element.26.place_ref.core_ref, s16[520,256]{1,0:T(8,128)(2,1)S(1)} %collective-permute-done.10.coded_ref, f32[4,256,256]{2,1,0:T(8,128)} %decode_own.1.refs_0_), custom_call_target="tpu_custom_call", output_to_operand_aliasing={{}: (3, {})} | custom-call | flops 131072 | bytes 786432 | tf_op jit(solution)/shard_map/decode_twin/pallas_call | solution.py:439
  (2 shorter events, 0.0 us)
Async XLA Ops:
  0.6 2.5 %collective-permute-start = (bf16[4,256,256]{2,1,0:T(8,128)(2,1)}, bf16[4,256,256]{2,1,0:T(8,128)(2,1)S(1)}, u32[]{:S(2)}, u32[]{:S(2)}) collective-permute-start(bf16[4,256,256]{2,1,0:T(8,128)(2,1)} %bitcast.3), channel_id=1, source_target_pairs={{0,1},{1,0},{2,3},{3,2},{4,5},{5,4},{6,7},{7,6},{8,9},{9,8},{10,11... | collective-permute-start | bytes 1572872 | tf_op jit(solution)/shard_map/ppermute | solution.py:42
  3.2 10.5 %collective-permute-start.4 = (bf16[4,128,256]{2,1,0:T(8,128)(2,1)S(1)}, bf16[4,128,256]{2,1,0:T(8,128)(2,1)S(1)}, u32[]{:S(2)}, u32[]{:S(2)}) collective-permute-start(bf16[4,128,256]{2,1,0:T(8,128)(2,1)S(1)} %add_replicas.1.refs_0_), channel_id=1, source_target_pairs={{4,8},{6,10},{12,16},{14,18},{20,24},{22,26},{8,4},{10,6},{16,12},... | collective-permute-start | bytes 786440 | tf_op jit(solution)/shard_map/ppermute | solution.py:30
  6.2 19.2 %collective-permute-start.3 = (bf16[4,128,256]{2,1,0:T(8,128)(2,1)S(1)}, bf16[4,128,256]{2,1,0:T(8,128)(2,1)S(1)}, u32[]{:S(2)}, u32[]{:S(2)}) collective-permute-start(bf16[4,128,256]{2,1,0:T(8,128)(2,1)S(1)} %add_replicas.1.refs_0_), channel_id=1, source_target_pairs={{0,4},{2,6},{8,12},{10,14},{16,20},{18,22},{24,28},{26,30},{4,0},{... | collective-permute-start | bytes 786440 | tf_op jit(solution)/shard_map/ppermute | solution.py:30
  7.6 17.8 %collective-permute-start.2 = (bf16[4,128,256]{2,1,0:T(8,128)(2,1)S(1)}, bf16[4,128,256]{2,1,0:T(8,128)(2,1)S(1)}, u32[]{:S(2)}, u32[]{:S(2)}) collective-permute-start(bf16[4,128,256]{2,1,0:T(8,128)(2,1)S(1)} %add_replicas.1.refs_0_), channel_id=1, source_target_pairs={{2,4},{6,8},{10,12},{14,16},{18,20},{22,24},{26,28},{4,2},{8,6},{1... | collective-permute-start | bytes 786440 | tf_op jit(solution)/shard_map/ppermute | solution.py:30
  9.6 15.8 %collective-permute-start.1 = (bf16[4,128,256]{2,1,0:T(8,128)(2,1)S(1)}, bf16[4,128,256]{2,1,0:T(8,128)(2,1)S(1)}, u32[]{:S(2)}, u32[]{:S(2)}) collective-permute-start(bf16[4,128,256]{2,1,0:T(8,128)(2,1)S(1)} %add_replicas.1.refs_0_), channel_id=1, source_target_pairs={{0,2},{4,6},{8,10},{12,14},{16,18},{20,22},{24,26},{28,30},{2,0},{... | collective-permute-start | bytes 786440 | tf_op jit(solution)/shard_map/ppermute | solution.py:30
  25.4 4.8 %collective-permute-start.5 = (bf16[6,128,256]{2,1,0:T(8,128)(2,1)S(1)}, bf16[6,128,256]{2,1,0:T(8,128)(2,1)S(1)}, u32[]{:S(2)}, u32[]{:S(2)}) collective-permute-start(bf16[6,128,256]{2,1,0:T(8,128)(2,1)S(1)} %collect.1.mine_ref), channel_id=1, source_target_pairs={{0,1},{1,0},{2,3},{3,2},{4,5},{5,4},{6,7},{7,6},{8,9},{9,8},{10,11... | collective-permute-start | bytes 1179656 | tf_op jit(solution)/shard_map/ppermute | solution.py:42
  33.1 13.6 %collective-permute-start.6 = (s16[520,256]{1,0:T(8,128)(2,1)S(1)}, s16[520,256]{1,0:T(8,128)(2,1)S(1)}, u32[]{:S(2)}, u32[]{:S(2)}) collective-permute-start(s16[520,256]{1,0:T(8,128)(2,1)S(1)} %get-tuple-element.40), channel_id=1, source_target_pairs={{0,2},{4,6},{8,10},{12,14},{16,18},{20,22},{24,26},{28,30},{2,0},{... | collective-permute-start | bytes 798728 | tf_op jit(solution)/shard_map/ppermute | solution.py:30
  33.5 16.7 %collective-permute-start.7 = (s16[520,256]{1,0:T(8,128)(2,1)S(1)}, s16[520,256]{1,0:T(8,128)(2,1)S(1)}, u32[]{:S(2)}, u32[]{:S(2)}) collective-permute-start(s16[520,256]{1,0:T(8,128)(2,1)S(1)} %get-tuple-element.41), channel_id=1, source_target_pairs={{2,4},{6,8},{10,12},{14,16},{18,20},{22,24},{26,28},{4,2},{8,6},{1... | collective-permute-start | bytes 798728 | tf_op jit(solution)/shard_map/ppermute | solution.py:30
  37.8 18.8 %collective-permute-start.8 = (s16[520,256]{1,0:T(8,128)(2,1)S(1)}, s16[520,256]{1,0:T(8,128)(2,1)S(1)}, u32[]{:S(2)}, u32[]{:S(2)}) collective-permute-start(s16[520,256]{1,0:T(8,128)(2,1)S(1)} %get-tuple-element.42), channel_id=1, source_target_pairs={{0,4},{2,6},{8,12},{10,14},{16,20},{18,22},{24,28},{26,30},{4,0},{... | collective-permute-start | bytes 798728 | tf_op jit(solution)/shard_map/ppermute | solution.py:30
  39.1 17.5 %collective-permute-start.9 = (s16[520,256]{1,0:T(8,128)(2,1)S(1)}, s16[520,256]{1,0:T(8,128)(2,1)S(1)}, u32[]{:S(2)}, u32[]{:S(2)}) collective-permute-start(s16[520,256]{1,0:T(8,128)(2,1)S(1)} %get-tuple-element.43), channel_id=1, source_target_pairs={{4,8},{6,10},{12,16},{14,18},{20,24},{22,26},{8,4},{10,6},{16,12},... | collective-permute-start | bytes 798728 | tf_op jit(solution)/shard_map/ppermute | solution.py:30
  56.8 7.3 %collective-permute-start.10 = (s16[520,256]{1,0:T(8,128)(2,1)S(1)}, s16[520,256]{1,0:T(8,128)(2,1)S(1)}, u32[]{:S(2)}, u32[]{:S(2)}) collective-permute-start(s16[520,256]{1,0:T(8,128)(2,1)S(1)} %gather_held.1.coded_ref), channel_id=1, source_target_pairs={{0,1},{1,0},{2,3},{3,2},{4,5},{5,4},{6,7},{7,6},{8,9},{9,8},{10,11... | collective-permute-start | bytes 798728 | tf_op jit(solution)/shard_map/ppermute | solution.py:42

commit v6 on v5

--- a/solution.py
+++ b/solution.py
@@ -200,27 +200,29 @@
     )(place, *in_vmem(mine, other))
 
 
-def collect_kernel(kind_ref, slot_ref, *refs):
-    sources, out_ref = refs[:5], refs[5]
+def collect_kernel(kind_ref, slot_ref, *refs, kinds):
+    sources, out_ref = refs[: len(kinds)], refs[-1]
     for j in range(out_ref.shape[0]):
-        for kind in range(5):
+        for kind, source in zip(kinds, sources):
 
             @pl.when(kind_ref[j] == kind)
             def _():
-                out_ref[j] = sources[kind][slot_ref[j]]
-
-
-def collect(kind, slot, sources):
+                out_ref[j] = source[slot_ref[j]]
+
+
+def collect(kind, slot, sources, base):
     count = kind.shape[0]
-    return pl.pallas_call(
-        collect_kernel,
+    first = next(iter(sources.values()))
+    extra = () if base is None else (base,)
+    return pl.pallas_call(
+        functools.partial(collect_kernel, kinds=tuple(sources)),
         in_specs=[pl.BlockSpec(memory_space=pltpu.SMEM)] * 2
-        + [pl.BlockSpec(memory_space=pltpu.VMEM)] * 5,
+        + [pl.BlockSpec(memory_space=pltpu.VMEM)] * (len(sources) + len(extra)),
         out_specs=pl.BlockSpec(memory_space=pltpu.VMEM),
-        out_shape=jax.ShapeDtypeStruct((count,) + sources[0].shape[1:], sources[0].dtype),
-        compiler_params=pltpu.CompilerParams(vmem_limit_bytes=SMALL_VMEM),
-        name="collect",
-    )(*in_smem(kind, slot), *sources)
+        out_shape=pltpu.VMEM((count,) + first.shape[1:], first.dtype),
+        input_output_aliases={2 + len(sources): 0} if extra else {},
+        compiler_params=pltpu.CompilerParams(vmem_limit_bytes=SMALL_VMEM),
+    )(*in_smem(kind, slot), *in_vmem(*sources.values(), *extra))
 
 
 def rotate_kernel(mine_ref, right_high, right_low, high_ref, low_ref):
@@ -480,7 +482,9 @@
     by_far = exchange(summed, far)
     by_side = exchange(summed, side)
     prepared = prepare(place, first_moment, second_moment, left_basis, right_basis, half)
-    mine = collect(own_kind, own_slot, (summed, by_side, by_cross, by_flip, by_far))
+    sooner = {HERE: summed, SIDE: by_side, CROSS: by_cross, FAR: by_far}
+    mine = collect(own_kind, own_slot, sooner, None)
+    mine = collect(own_kind, own_slot, {FLIP: by_flip}, mine)
     other = swap_cores(mine)
     second, keep, to_side, to_cross, to_flip, to_far = soap_step(
         own_kind, own_slot, core_index, rotate_rows(mine, prepared), other, prepared, slot_count

time: 65.2 us -> 64.9 us (level)
  the two profiles are of different devices: /device:TPU:11 before, /device:TPU:0 now
where the time goes in v6:
time: 64.9 us; the launch traced here: 63.9 us
  waiting for transfers between devices  28.7 us (44%)
  starting transfers between devices  18 us (28%)
  Pallas kernels  16.3 us (25%)
  between operations  0.79 us (1%)
    ppermute x8, waiting for transfers between devices, exchange(): return lax.ppermute(value, 'fsdp', pairs + [(b, a) for a, b in pairs])  27.9 us
    ppermute x8, starting transfers between devices, exchange(): return lax.ppermute(value, 'fsdp', pairs + [(b, a) for a, b in pairs])  17.3 us
    pallas_call x1, Pallas kernels, finish(): pl.pallas_call(finish_kernel, grid=(count,), in_specs=[pl.BlockSpec(memor...  4.9 us
    pallas_call x1, Pallas kernels, prepare(): pl.pallas_call(prepare_kernel, grid=(count // group,), in_specs=[pl.Block...  3.88 us
    pallas_call x1, Pallas kernels, soap_step(): pl.pallas_call(step_kernel, grid=(count // group,), in_specs=[pl.BlockSpe...  2.89 us
    pallas_call x2, Pallas kernels, decode(): pl.pallas_call(functools.partial(decode_kernel, twin=twin), in_specs=[pl....  1.68 us
  transfers between devices with their start and end apart: 11, of which 4 were waited for; matrix products, arithmetic and copies ran while one was open for 0% of the time, Pallas kernels for 19%

profile of v6, /device:TPU:0, one launch (start us, length us, event | category | flops | bytes accessed | tf_op | source)
XLA Modules:
  0.0 63.9 jit_solution(6228816269032309018)
XLA Ops:
  0.6 0.6 collective-permute-start
  1.2 1.0 %load_rows.1.mine_ref = bf16[4,128,256]{2,1,0:T(8,128)(2,1)S(1)} custom-call(s32[1]{0:T(128)} %bitcast.1.place_ref, bf16[4,256,256]{2,1,0:T(8,128)(2,1)} %bitcast.4), custom_call_target="tpu_custom_call" | custom-call | tf_op jit(solution)/shard_map/load_rows/pallas_call | solution.py:169
  2.2 0.8 %collective-permute-done.other_ref = bf16[4,256,256]{2,1,0:T(8,128)(2,1)S(1)} collective-permute-done((bf16[4,256,256]{2,1,0:T(8,128)(2,1)}, bf16[4,256,256]{2,1,0:T(8,128)(2,1)S(1)}, u32[]{:S(2)}, u32[]{:S(2)}) %collective-permute-start) | collective-permute-done | bytes 524320 | tf_op jit(solution)/shard_map/ppermute | solution.py:42
  2.9 0.1 add_replicas.1.refs_0_
  3.0 0.7 %collective-permute-start.4 = (bf16[4,128,256]{2,1,0:T(8,128)(2,1)S(1)}, bf16[4,128,256]{2,1,0:T(8,128)(2,1)S(1)}, u32[]{:S(2)}, u32[]{:S(2)}) collective-permute-start(bf16[4,128,256]{2,1,0:T(8,128)(2,1)S(1)} %add_replicas.1.refs_0_), channel_id=1, source_target_pairs={{4,8},{6,10},{12,16},{14,18},{20,24},{22,26},{8,4},{10,6},{16,12},... | collective-permute-start | bytes 786440 | tf_op jit(solution)/shard_map/ppermute | solution.py:30
  3.7 0.7 %collective-permute-start.3 = (bf16[4,128,256]{2,1,0:T(8,128)(2,1)S(1)}, bf16[4,128,256]{2,1,0:T(8,128)(2,1)S(1)}, u32[]{:S(2)}, u32[]{:S(2)}) collective-permute-start(bf16[4,128,256]{2,1,0:T(8,128)(2,1)S(1)} %add_replicas.1.refs_0_), channel_id=1, source_target_pairs={{2,4},{6,8},{10,12},{14,16},{18,20},{22,24},{26,28},{4,2},{8,6},{1... | collective-permute-start | bytes 786440 | tf_op jit(solution)/shard_map/ppermute | solution.py:30
  4.4 8.4 %collective-permute-start.2 = (bf16[4,128,256]{2,1,0:T(8,128)(2,1)S(1)}, bf16[4,128,256]{2,1,0:T(8,128)(2,1)S(1)}, u32[]{:S(2)}, u32[]{:S(2)}) collective-permute-start(bf16[4,128,256]{2,1,0:T(8,128)(2,1)S(1)} %add_replicas.1.refs_0_), channel_id=1, source_target_pairs={{0,2},{4,6},{8,10},{12,14},{16,18},{20,22},{24,26},{28,30},{2,0},{... | collective-permute-start | bytes 786440 | tf_op jit(solution)/shard_map/ppermute | solution.py:30
  12.8 1.4 %collective-permute-start.1 = (bf16[4,128,256]{2,1,0:T(8,128)(2,1)S(1)}, bf16[4,128,256]{2,1,0:T(8,128)(2,1)S(1)}, u32[]{:S(2)}, u32[]{:S(2)}) collective-permute-start(bf16[4,128,256]{2,1,0:T(8,128)(2,1)S(1)} %add_replicas.1.refs_0_), channel_id=1, source_target_pairs={{0,4},{2,6},{8,12},{10,14},{16,20},{18,22},{24,28},{26,30},{4,0},{... | collective-permute-start | bytes 786440 | tf_op jit(solution)/shard_map/ppermute | solution.py:30
  14.2 0.1 pad_add_fusion.at_ref
  14.2 1.2 %tables.1 = (s32[6]{0:T(128)S(4)}, s32[6]{0:T(128)S(4)}, s32[4]{0:T(128)S(4)}, s32[1]{0:T(128)S(4)}) custom-call(s32[2]{0:T(128)S(1)} %pad_add_fusion.at_ref, s32[16]{0:T(128)} %starts_ref.1, s32[48]{0:T(128)} %owners_ref.1), custom_call_target="tpu_custom_call" | custom-call | tf_op jit(solution)/shard_map/tables/pallas_call | solution.py:94
  15.4 0.0 collective-permute-done.3.refs_2_
  15.4 11.4 %collective-permute-done.2.refs_1_ = bf16[4,128,256]{2,1,0:T(8,128)(2,1)S(1)} collective-permute-done((bf16[4,128,256]{2,1,0:T(8,128)(2,1)S(1)}, bf16[4,128,256]{2,1,0:T(8,128)(2,1)S(1)}, u32[]{:S(2)}, u32[]{:S(2)}) %collective-permute-start.2) | collective-permute-done | bytes 262176 | tf_op jit(solution)/shard_map/ppermute | solution.py:30
  26.8 0.2 shard_map.94.refs_1_
  27.0 0.1 shard_map.95.mine_ref
  27.1 0.1 collective-permute-start.5
  27.2 3.9 %prepare.1 = (f32[6,256,256]{2,1,0:T(8,128)S(1)}, f32[6,256,256]{2,1,0:T(8,128)S(1)}, bf16[6,256,256]{2,1,0:T(8,128)(2,1)S(1)}, bf16[6,256,256]{2,1,0:T(8,128)(2...) custom-call(s32[1]{0:T(128)} %bitcast.1.place_ref, ...), custom_call_target="tpu_custom_call" | custom-call | flops 1207959552 | bytes 6291456 | tf_op jit(solution)/shard_map/prepare/pallas_call | solution.py:149
  31.1 0.4 rotate_rows.1
  31.4 0.0 collective-permute-done.5.other_ref
  31.5 2.9 %soap_step.1 = (f32[6,256,256]{2,1,0:T(8,128)S(1)}, s16[520,256]{1,0:T(8,128)(2,1)S(1)}, s16[520,256]{1,0:T(8,128)(2,1)S(1)}, s16[520,256]{1,0:T(8,128)(2,1)S(1)...) custom-call(s32[6]{0:T(128)S(4)} %get-tuple-element.27.kind_ref, s32[6]{0:T(128)S(4)} %get-tuple-element.28.slot_ref, ...), custom_call_target="tpu_custom_call" | custom-call | tf_op jit(solution)/shard_map/soap_step/pallas_call | solution.py:333
  34.3 0.2 collective-permute-start.6
  34.5 0.7 %collective-permute-start.7 = (s16[520,256]{1,0:T(8,128)(2,1)S(1)}, s16[520,256]{1,0:T(8,128)(2,1)S(1)}, u32[]{:S(2)}, u32[]{:S(2)}) collective-permute-start(s16[520,256]{1,0:T(8,128)(2,1)S(1)} %get-tuple-element.41), channel_id=1, source_target_pairs={{2,4},{6,8},{10,12},{14,16},{18,20},{22,24},{26,28},{4,2},{8,6},{1... | collective-permute-start | bytes 798728 | tf_op jit(solution)/shard_map/ppermute | solution.py:30
  35.2 4.7 %collective-permute-start.8 = (s16[520,256]{1,0:T(8,128)(2,1)S(1)}, s16[520,256]{1,0:T(8,128)(2,1)S(1)}, u32[]{:S(2)}, u32[]{:S(2)}) collective-permute-start(s16[520,256]{1,0:T(8,128)(2,1)S(1)} %get-tuple-element.42), channel_id=1, source_target_pairs={{0,4},{2,6},{8,12},{10,14},{16,20},{18,22},{24,28},{26,30},{4,0},{... | collective-permute-start | bytes 798728 | tf_op jit(solution)/shard_map/ppermute | solution.py:30
  39.9 0.7 %collective-permute-start.9 = (s16[520,256]{1,0:T(8,128)(2,1)S(1)}, s16[520,256]{1,0:T(8,128)(2,1)S(1)}, u32[]{:S(2)}, u32[]{:S(2)}) collective-permute-start(s16[520,256]{1,0:T(8,128)(2,1)S(1)} %get-tuple-element.43), channel_id=1, source_target_pairs={{4,8},{6,10},{12,16},{14,18},{20,24},{22,26},{8,4},{10,6},{16,12},... | collective-permute-start | bytes 798728 | tf_op jit(solution)/shard_map/ppermute | solution.py:30
  40.5 5.4 %collective-permute-done.6.refs_1_ = s16[520,256]{1,0:T(8,128)(2,1)S(1)} collective-permute-done((s16[520,256]{1,0:T(8,128)(2,1)S(1)}, s16[520,256]{1,0:T(8,128)(2,1)S(1)}, u32[]{:S(2)}, u32[]{:S(2)}) %collective-permute-start.6) | collective-permute-done | bytes 266272 | tf_op jit(solution)/shard_map/ppermute | solution.py:30
  45.9 0.0 collective-permute-done.7.refs_2_
  45.9 11.1 %collective-permute-done.8.refs_3_ = s16[520,256]{1,0:T(8,128)(2,1)S(1)} collective-permute-done((s16[520,256]{1,0:T(8,128)(2,1)S(1)}, s16[520,256]{1,0:T(8,128)(2,1)S(1)}, u32[]{:S(2)}, u32[]{:S(2)}) %collective-permute-start.8) | collective-permute-done | bytes 266272 | tf_op jit(solution)/shard_map/ppermute | solution.py:30
  57.0 0.0 collective-permute-done.9.refs_4_
  57.0 0.2 gather_held.1.coded_ref
  57.2 0.1 collective-permute-start.10
  57.3 4.9 %finish.1 = (f32[6,256,256]{2,1,0:T(8,128)}, f32[6,256,256]{2,1,0:T(8,128)}) custom-call(s32[6]{0:T(128)S(4)} %get-tuple-element.27.kind_ref, s32[1]{0:T(128)S(4)} %get-tuple-element.26.place_ref.core_ref, bf16[6,128,256]{2,1,0:T(8,128)(2,1)S(1)} %shard_map.95.mine_ref, bf16[6,128,256]{2,1,0:T(8,128)(2,1)S(1)} %collective-permute-done.5.other_ref, ...), custom_call_target="tpu_custom_call" | custom-call | flops 4718592 | bytes 4718592 | tf_op jit(solution)/shard_map/finish/pallas_call | solution.py:371
  62.2 0.8 %decode_own.1.refs_0_ = f32[4,256,256]{2,1,0:T(8,128)} custom-call(s32[4]{0:T(128)S(4)} %get-tuple-element.25.kind_ref, s32[1]{0:T(128)S(4)} %get-tuple-element.26.place_ref.core_ref, s16[520,256]{1,0:T(8,128)(2,1)S(1)} %gather_held.1.coded_ref), custom_call_target="tpu_custom_call" | custom-call | flops 131072 | bytes 786432 | tf_op jit(solution)/shard_map/decode_own/pallas_call | solution.py:441
  63.0 0.8 %decode_twin.1 = f32[4,256,256]{2,1,0:T(8,128)} custom-call(s32[4]{0:T(128)S(4)} %get-tuple-element.25.kind_ref, s32[1]{0:T(128)S(4)} %get-tuple-element.26.place_ref.core_ref, s16[520,256]{1,0:T(8,128)(2,1)S(1)} %collective-permute-done.10.coded_ref, f32[4,256,256]{2,1,0:T(8,128)} %decode_own.1.refs_0_), custom_call_target="tpu_custom_call", output_to_operand_aliasing={{}: (3, {})} | custom-call | flops 131072 | bytes 786432 | tf_op jit(solution)/shard_map/decode_twin/pallas_call | solution.py:441
  (3 shorter events, 0.0 us)
Async XLA Ops:
  0.6 2.3 %collective-permute-start = (bf16[4,256,256]{2,1,0:T(8,128)(2,1)}, bf16[4,256,256]{2,1,0:T(8,128)(2,1)S(1)}, u32[]{:S(2)}, u32[]{:S(2)}) collective-permute-start(bf16[4,256,256]{2,1,0:T(8,128)(2,1)} %bitcast.3), channel_id=1, source_target_pairs={{0,1},{1,0},{2,3},{3,2},{4,5},{5,4},{6,7},{7,6},{8,9},{9,8},{10,11... | collective-permute-start | bytes 1572872 | tf_op jit(solution)/shard_map/ppermute | solution.py:42
  3.0 12.4 %collective-permute-start.4 = (bf16[4,128,256]{2,1,0:T(8,128)(2,1)S(1)}, bf16[4,128,256]{2,1,0:T(8,128)(2,1)S(1)}, u32[]{:S(2)}, u32[]{:S(2)}) collective-permute-start(bf16[4,128,256]{2,1,0:T(8,128)(2,1)S(1)} %add_replicas.1.refs_0_), channel_id=1, source_target_pairs={{4,8},{6,10},{12,16},{14,18},{20,24},{22,26},{8,4},{10,6},{16,12},... | collective-permute-start | bytes 786440 | tf_op jit(solution)/shard_map/ppermute | solution.py:30
  3.7 11.7 %collective-permute-start.3 = (bf16[4,128,256]{2,1,0:T(8,128)(2,1)S(1)}, bf16[4,128,256]{2,1,0:T(8,128)(2,1)S(1)}, u32[]{:S(2)}, u32[]{:S(2)}) collective-permute-start(bf16[4,128,256]{2,1,0:T(8,128)(2,1)S(1)} %add_replicas.1.refs_0_), channel_id=1, source_target_pairs={{2,4},{6,8},{10,12},{14,16},{18,20},{22,24},{26,28},{4,2},{8,6},{1... | collective-permute-start | bytes 786440 | tf_op jit(solution)/shard_map/ppermute | solution.py:30
  4.4 22.5 %collective-permute-start.2 = (bf16[4,128,256]{2,1,0:T(8,128)(2,1)S(1)}, bf16[4,128,256]{2,1,0:T(8,128)(2,1)S(1)}, u32[]{:S(2)}, u32[]{:S(2)}) collective-permute-start(bf16[4,128,256]{2,1,0:T(8,128)(2,1)S(1)} %add_replicas.1.refs_0_), channel_id=1, source_target_pairs={{0,2},{4,6},{8,10},{12,14},{16,18},{20,22},{24,26},{28,30},{2,0},{... | collective-permute-start | bytes 786440 | tf_op jit(solution)/shard_map/ppermute | solution.py:30
  12.8 14.3 %collective-permute-start.1 = (bf16[4,128,256]{2,1,0:T(8,128)(2,1)S(1)}, bf16[4,128,256]{2,1,0:T(8,128)(2,1)S(1)}, u32[]{:S(2)}, u32[]{:S(2)}) collective-permute-start(bf16[4,128,256]{2,1,0:T(8,128)(2,1)S(1)} %add_replicas.1.refs_0_), channel_id=1, source_target_pairs={{0,4},{2,6},{8,12},{10,14},{16,20},{18,22},{24,28},{26,30},{4,0},{... | collective-permute-start | bytes 786440 | tf_op jit(solution)/shard_map/ppermute | solution.py:30
  27.1 4.4 %collective-permute-start.5 = (bf16[6,128,256]{2,1,0:T(8,128)(2,1)S(1)}, bf16[6,128,256]{2,1,0:T(8,128)(2,1)S(1)}, u32[]{:S(2)}, u32[]{:S(2)}) collective-permute-start(bf16[6,128,256]{2,1,0:T(8,128)(2,1)S(1)} %shard_map.95.mine_ref), channel_id=1, source_target_pairs={{0,1},{1,0},{2,3},{3,2},{4,5},{5,4},{6,7},{7,6},{8,9},{9,8},{10,11... | collective-permute-start | bytes 1179656 | tf_op jit(solution)/shard_map/ppermute | solution.py:42
  34.3 11.6 %collective-permute-start.6 = (s16[520,256]{1,0:T(8,128)(2,1)S(1)}, s16[520,256]{1,0:T(8,128)(2,1)S(1)}, u32[]{:S(2)}, u32[]{:S(2)}) collective-permute-start(s16[520,256]{1,0:T(8,128)(2,1)S(1)} %get-tuple-element.40), channel_id=1, source_target_pairs={{0,2},{4,6},{8,10},{12,14},{16,18},{20,22},{24,26},{28,30},{2,0},{... | collective-permute-start | bytes 798728 | tf_op jit(solution)/shard_map/ppermute | solution.py:30
  34.5 11.4 %collective-permute-start.7 = (s16[520,256]{1,0:T(8,128)(2,1)S(1)}, s16[520,256]{1,0:T(8,128)(2,1)S(1)}, u32[]{:S(2)}, u32[]{:S(2)}) collective-permute-start(s16[520,256]{1,0:T(8,128)(2,1)S(1)} %get-tuple-element.41), channel_id=1, source_target_pairs={{2,4},{6,8},{10,12},{14,16},{18,20},{22,24},{26,28},{4,2},{8,6},{1... | collective-permute-start | bytes 798728 | tf_op jit(solution)/shard_map/ppermute | solution.py:30
  35.2 21.8 %collective-permute-start.8 = (s16[520,256]{1,0:T(8,128)(2,1)S(1)}, s16[520,256]{1,0:T(8,128)(2,1)S(1)}, u32[]{:S(2)}, u32[]{:S(2)}) collective-permute-start(s16[520,256]{1,0:T(8,128)(2,1)S(1)} %get-tuple-element.42), channel_id=1, source_target_pairs={{0,4},{2,6},{8,12},{10,14},{16,20},{18,22},{24,28},{26,30},{4,0},{... | collective-permute-start | bytes 798728 | tf_op jit(solution)/shard_map/ppermute | solution.py:30
  39.9 17.1 %collective-permute-start.9 = (s16[520,256]{1,0:T(8,128)(2,1)S(1)}, s16[520,256]{1,0:T(8,128)(2,1)S(1)}, u32[]{:S(2)}, u32[]{:S(2)}) collective-permute-start(s16[520,256]{1,0:T(8,128)(2,1)S(1)} %get-tuple-element.43), channel_id=1, source_target_pairs={{4,8},{6,10},{12,16},{14,18},{20,24},{22,26},{8,4},{10,6},{16,12},... | collective-permute-start | bytes 798728 | tf_op jit(solution)/shard_map/ppermute | solution.py:30
  57.2 5.8 %collective-permute-start.10 = (s16[520,256]{1,0:T(8,128)(2,1)S(1)}, s16[520,256]{1,0:T(8,128)(2,1)S(1)}, u32[]{:S(2)}, u32[]{:S(2)}) collective-permute-start(s16[520,256]{1,0:T(8,128)(2,1)S(1)} %gather_held.1.coded_ref), channel_id=1, source_target_pairs={{0,1},{1,0},{2,3},{3,2},{4,5},{5,4},{6,7},{7,6},{8,9},{9,8},{10,11... | collective-permute-start | bytes 798728 | tf_op jit(solution)/shard_map/ppermute | solution.py:42
